TPU v7x, 256 devices: a whole 4x4x8 slice. The times are simulated.
256 devices in a mesh: dp: 64 (over z, y, core), mp: 4 (over x).
Axes of the slice: x: 4, y: 4, z: 8, core: 2. Of those that a mesh axis runs over, the one named last changes fastest.
Arguments:
- patches: bfloat16 [131072, 1024], P('dp'), may hold values from -110 to 110
- dest_owner: int32 [8192], P('dp'), may hold values from 0 to 63, as said below
- dest_slot: int32 [8192], P('dp'), may hold values from 0 to 127
- packed_image: int32 [8192], P('dp'), may hold values from -1 to 15, as said below
- w_query: bfloat16 [1024, 1024], P(None, 'mp'), may hold values from -0.328125 to 0.328125
- w_key: bfloat16 [1024, 1024], P(None, 'mp'), may hold values from -1.9375 to 1.9375
- w_value: bfloat16 [1024, 1024], P(None, 'mp'), may hold values from -0.1875 to 0.1875
- w_out: bfloat16 [1024, 1024], P('mp'), may hold values from -0.1875 to 0.1875
Outputs:
- packed_out: bfloat16 [131072, 1024], P('dp', 'mp')
- pooled_out: bfloat16 [1024, 1024], P('dp', 'mp')
Inputs may be any that keep to these rules, and one draw needn't show every extreme that they name: dest_owner and dest_slot take the tiles of all indices of dp one to one onto the 128 tile slots of every packed sequence; each index of dp holds exactly 2 tiles for each packed sequence. `packed_image`: in every packed sequence the images 0, 1, 2 and so on lie on consecutive tile slots from slot 0 in the order of their numbers, each on 8 to 16 slots; fewer than 16 slots stay empty after the last image and hold -1.
All inputs are finite; a program needn't handle non-finite values.
Results may differ from a plain program's by a relative error of at most 0.0075.
Values may be sent and summed in bfloat16 or wider, within the bound.
No kernel may reach another device: no remote copies, remote signals or barrier semaphores. Data moves between devices by JAX's collectives and lax.ppermute only.
A program may use at most 128 MiB of HBM per device.

v0:
```python
import jax
import jax.numpy as jnp
from jax import lax
from jax.sharding import PartitionSpec as P

HEAD_DIM = 64
IMG_OWN = 16


EPSILON = 1e-06


def cut_along(shard, dim, length):
    lengths = shard.shape
    tiles = shard.reshape(*lengths[:dim], length, lengths[dim] // length, *lengths[dim + 1 :])
    return jnp.moveaxis(tiles, dim, 0)


def sent_and_summed(shard, axis, dim):
    length = lax.axis_size(axis)
    tiles = lax.all_to_all(cut_along(shard, dim, length), axis, 0, 0, tiled=True)
    return jnp.sum(tiles.astype(jnp.float32), axis=0)


def sent_to_all(shard, axis):
    copies = jnp.broadcast_to(shard, (lax.axis_size(axis), *shard.shape))
    return lax.all_to_all(copies, axis, split_axis=0, concat_axis=0, tiled=True)


def of_everyone(shard, axis):
    return sent_to_all(shard, axis).sum(axis=0)


def in_one(arrays, axis):
    line, at, outs = (jnp.concatenate([a.reshape(-1) for a in arrays]), 0, [])
    running = of_everyone(line, axis)
    for a in arrays:
        outs.append(running[at : at + a.size].reshape(a.shape))
        at += a.size
    return tuple(outs)


def normalize(rows):
    values = rows.astype(jnp.float32)
    centred = values - jnp.mean(values, axis=-1, keepdims=True)
    spread = jnp.mean(centred * centred, axis=-1, keepdims=True)
    return (centred * lax.rsqrt(spread + EPSILON)).astype(jnp.bfloat16)


def attend(queries, key_rows, values, allowed, present):
    scores = jnp.einsum(
        "qhd,khd->hqk", queries, key_rows, preferred_element_type=jnp.float32
    ) * HEAD_DIM ** (-0.5)
    masked = jnp.where(allowed[None], scores, -1e30)
    peak = jnp.max(masked, axis=-1, keepdims=True)
    raised = jnp.where(allowed[None], jnp.exp(scores - peak), 0.0)
    denominator = jnp.sum(raised, axis=-1, keepdims=True)
    denominator = jnp.where(present[None, :, None], denominator, 1.0)
    weights = (raised / denominator).astype(jnp.bfloat16)
    return jnp.einsum("hqk,khd->qhd", weights, values, preferred_element_type=jnp.float32).astype(
        jnp.bfloat16
    )


def whole_rows(queries, key_rows, values, segment, present):
    count_rows = queries.shape[0]
    block_rows = min(512, count_rows)

    def one_block(step_index):
        first_row = step_index * block_rows
        query_part = lax.dynamic_slice_in_dim(queries, first_row, block_rows, 0)
        segment_part = lax.dynamic_slice_in_dim(segment, first_row, block_rows, 0)
        live_rows = lax.dynamic_slice_in_dim(present, first_row, block_rows, 0)
        allowed = (segment_part[:, None] == segment[None, :]) & live_rows[:, None]
        return attend(query_part, key_rows, values, allowed, live_rows)

    outcome = lax.map(one_block, jnp.arange(count_rows // block_rows, dtype=jnp.int32))
    return outcome.reshape(count_rows, -1)


def on_device(patches, dest_owner, dest_slot, packed_image, w_query, w_key, w_value, w_out):
    senders = lax.axis_size("dp")
    splits = lax.axis_size("mp")
    slot_count = dest_owner.shape[0]
    per_owner = slot_count // senders
    tile_size = patches.shape[0] // slot_count
    full_width = patches.shape[1]
    part_width = full_width // splits
    numbers = jnp.arange(slot_count, dtype=jnp.int32)
    same_owner = dest_owner[:, None] == dest_owner[None, :]
    ranking = jnp.sum(
        (same_owner & (numbers[None, :] < numbers[:, None])).astype(jnp.int32), axis=1
    )
    position = dest_owner * per_owner + ranking
    picked = position[None, :] == numbers[:, None]
    ordering = jnp.sum(jnp.where(picked, numbers[None, :], 0), axis=1)
    slot_sent = jnp.sum(jnp.where(picked, dest_slot[None, :], 0), axis=1)
    got_slot = lax.all_to_all(slot_sent, "dp", split_axis=0, concat_axis=0, tiled=True)
    arrive = jnp.sum(jnp.where(got_slot[None, :] == numbers[:, None], numbers[None, :], 0), axis=1)
    tile_data = patches.reshape(slot_count, tile_size, full_width)
    column_start = lax.axis_index("mp") * part_width
    own_part = lax.dynamic_slice_in_dim(tile_data, column_start, part_width, 2)
    outgoing = jnp.take(own_part, ordering, axis=0).reshape(slot_count * tile_size, part_width)
    incoming = lax.all_to_all(outgoing, "dp", split_axis=0, concat_axis=0, tiled=True)
    own_cols = jnp.take(
        incoming.reshape(slot_count, tile_size, part_width), arrive, axis=0
    ).reshape(slot_count * tile_size, part_width)
    full_rows = lax.all_gather(own_cols, "mp", axis=1, tiled=True)
    count_rows = slot_count * tile_size
    segment = jnp.repeat(packed_image, tile_size)
    present = segment >= 0
    normed = normalize(full_rows)
    head_count = w_query.shape[1] // HEAD_DIM
    queries = (
        jnp.dot(normed, w_query, preferred_element_type=jnp.float32)
        .astype(jnp.bfloat16)
        .reshape(count_rows, head_count, HEAD_DIM)
    )
    key_rows = (
        jnp.dot(normed, w_key, preferred_element_type=jnp.float32)
        .astype(jnp.bfloat16)
        .reshape(count_rows, head_count, HEAD_DIM)
    )
    values = (
        jnp.dot(normed, w_value, preferred_element_type=jnp.float32)
        .astype(jnp.bfloat16)
        .reshape(count_rows, head_count, HEAD_DIM)
    )
    attended = whole_rows(queries, key_rows, values, segment, present)
    head_term = jnp.dot(attended, w_out, preferred_element_type=jnp.float32)
    summed = sent_and_summed(head_term.astype(jnp.bfloat16), "mp", 1)
    result_rows = jnp.where(present[:, None], own_cols.astype(jnp.float32) + summed, 0.0)
    packed_out = result_rows.astype(jnp.bfloat16)
    labels = jnp.arange(IMG_OWN, dtype=jnp.int32)
    member = (segment[None, :] == labels[:, None]).astype(jnp.float32)
    sums = jnp.dot(member, result_rows)
    image_rows = jnp.sum(member, axis=1)
    filled = image_rows > 0
    pooled = sums / jnp.maximum(image_rows, 1.0)[:, None]
    local_sum = jnp.sum(jnp.where(filled[:, None], pooled, 0.0), axis=0)
    local_count = jnp.sum(filled.astype(jnp.float32))
    grand_total, number = in_one((local_sum, local_count), "dp")
    centre = grand_total / number
    pooled_out = jnp.where(filled[:, None], pooled - centre[None, :], 0.0).astype(jnp.bfloat16)
    return (packed_out, pooled_out)


def solution(mesh):
    in_specs = (
        P("dp", None),
        P("dp"),
        P("dp"),
        P("dp"),
        P(None, "mp"),
        P(None, "mp"),
        P(None, "mp"),
        P("mp", None),
    )
    out_specs = (P("dp", "mp"), P("dp", "mp"))
    return jax.shard_map(
        on_device, mesh=mesh, in_specs=in_specs, out_specs=out_specs, check_vma=False
    )
```

profile of v0, /device:TPU:1, one launch (start us, length us, event | category | flops | bytes accessed | tf_op | source)
XLA Modules:
  0.0 322.7 jit_solution(6817620751752851636)
XLA Ops:
  7.2 0.9 convert_reduce_fusion.3
  8.1 0.7 multiply_add_fusion
  8.8 0.8 select_reduce_fusion.2
  9.5 0.8 all_to_all.21
  10.3 13.1 %all-to-all-start.1 = ((s32[64,2,1]{1,2,0:T(1,128)}), s32[64,2,1]{1,2,0:T(1,128)S(1)}, u32[]{:S(2)}, u32[]{:S(2)}) async-start(s32[64,2,1]{1,2,0:T(1,128)} %bitcast), calls=%async_computation.1 | async-start | bytes 65536 | tf_op jit(solution)/shard_map/all_to_all | solution.py:98
  23.5 1.3 constant_dynamic-slice_fusion
  24.8 0.6 gather_fusion
  25.4 1.2 broadcast_select_fusion.2
  26.6 6.2 %all-to-all-done.1 = s32[64,2,1]{1,2,0:T(1,128)S(1)} async-done(((s32[64,2,1]{1,2,0:T(1,128)}), s32[64,2,1]{1,2,0:T(1,128)S(1)}, u32[]{:S(2)}, u32[]{:S(2)}) %all-to-all-start.1) | async-done | bytes 544 | tf_op jit(solution)/shard_map/all_to_all | solution.py:98
  32.8 4.7 %all-to-all-start = ((bf16[64,32,256]{2,1,0:T(8,128)(2,1)}), bf16[64,32,256]{2,1,0:T(8,128)(2,1)S(1)}, u32[]{:S(2)}, u32[]{:S(2)}) async-start(bf16[64,32,256]{2,1,0:T(8,128)(2,1)} %bitcast.2), calls=%async_computation | async-start | bytes 2097152 | tf_op jit(solution)/shard_map/all_to_all | solution.py:104
  37.6 0.5 broadcast.118
  38.1 0.7 reduce.4
  38.9 0.1 eq.74
  39.0 0.1 select_reduce_fusion.1
  39.2 26.7 %all-to-all-done = bf16[64,32,256]{2,1,0:T(8,128)(2,1)S(1)} async-done(((bf16[64,32,256]{2,1,0:T(8,128)(2,1)}), bf16[64,32,256]{2,1,0:T(8,128)(2,1)S(1)}, u32[]{:S(2)}, u32[]{:S(2)}) %all-to-all-start) | async-done | bytes 1048608 | tf_op jit(solution)/shard_map/all_to_all | solution.py:104
  65.9 0.6 gather_fusion.1
  66.5 1.2 broadcast_select_fusion.1
  67.8 0.1 reshape.146
  67.9 49.4 %all-gather.2.cloned.1.call-done = bf16[2048,1024]{1,0:T(8,128)(2,1)} async-done(((bf16[2048,256]{1,0:T(8,128)(2,1)}), bf16[2048,1024]{1,0:T(8,128)(2,1)}) %all-gather.2.cloned.1.call-update) | async-done | bytes 4194320 | tf_op jit(solution)/shard_map/all_gather | solution.py:108
  117.4 3.0 convert_reduce_fusion
  120.3 0.5 copy-done.1
  120.8 1.4 fusion.31
  122.2 1.1 fusion.32
  123.4 2.3 convolution_convert_fusion.3
  125.7 2.3 convolution_convert_fusion.2
  128.0 2.3 convolution_convert_fusion.1
  130.3 98.7 %while.11 = (s32[]{:T(128)}, bf16[4,512,4,64]{1,3,2,0:T(8,128)(2,1)S(1)}, s32[4]{0:T(128)S(1)}, s32[2048]{0:T(1024)S(1)}, pred[2048]{0:T(1024)(128)(4,1)S(1)}, /...) while((s32[]{:T(128)}, ...), condition=%wide.region_9.11_spmd.clone, body=%wide.region_6.0_spmd.clone.sunk | while | flops 1646399488 | bytes 40707776 | solution.py:77
  130.3 0.7 dynamic_slice.41
  131.9 0.1 eq.127
  132.0 0.8 compare_and_fusion.4
  132.8 13.4 %fusion.69 = (f32[4,512]{1,0:T(4,128)S(1)}, f32[4,512,2048]{2,1,0:T(8,128)}) fusion(pred[512,2048]{1,0:T(8,128)(4,1)S(1)} %compare_and_fusion.4, bf16[2048,4,64]{0,2,1:T(8,128)(2,1)} %get-tuple-element.197, bf16[2048,4,64]{0,2,1:T(8,128)(2,1)} %get-tuple-element.196, s32[]{:T(128)S(6)} %select_n.104), kind=kOutput, calls=%fused_computation.75.clone.1 | convolution fusion | flops 1098909696 | bytes 21505024 | tf_op jit(solution)/shard_map/while/body/eval_jaxpr/sub | solution.py:56
  146.2 8.7 %fusion.70 = bf16[4,512,4,64]{1,3,2,0:T(8,128)(2,1)S(1)} fusion(bf16[4,512,4,64]{1,3,2,0:T(8,128)(2,1)S(1)} %get-tuple-element.179, s32[]{:T(128)} %get-tuple-element.178, bf16[2048,4,64]{0,2,1:T(8,128)(2,1)} %get-tuple-element.198, f32[4,512,2048]{2,1,0:T(8,128)} %get-tuple-element.163, f32[4,512]{1,0:T(4,128)S(1)} %broadcast_select_fusion.4), kind=kOutput, calls=%fused_computation.17.clone.1 | convolution fusion | flops 545390592 | bytes 18096132 | tf_op jit(solution)/shard_map/while/body/eval_jaxpr/hqk,khd->qhd/dot_general | solution.py:60
  154.9 0.7 dynamic_slice.41
  156.6 0.8 compare_and_fusion.4
  157.4 13.4 %fusion.69 = (f32[4,512]{1,0:T(4,128)S(1)}, f32[4,512,2048]{2,1,0:T(8,128)}) fusion(pred[512,2048]{1,0:T(8,128)(4,1)S(1)} %compare_and_fusion.4, bf16[2048,4,64]{0,2,1:T(8,128)(2,1)} %get-tuple-element.197, bf16[2048,4,64]{0,2,1:T(8,128)(2,1)} %get-tuple-element.196, s32[]{:T(128)S(6)} %select_n.104), kind=kOutput, calls=%fused_computation.75.clone.1 | convolution fusion | flops 1098909696 | bytes 21505024 | tf_op jit(solution)/shard_map/while/body/eval_jaxpr/sub | solution.py:56
  170.9 8.7 %fusion.70 = bf16[4,512,4,64]{1,3,2,0:T(8,128)(2,1)S(1)} fusion(bf16[4,512,4,64]{1,3,2,0:T(8,128)(2,1)S(1)} %get-tuple-element.179, s32[]{:T(128)} %get-tuple-element.178, bf16[2048,4,64]{0,2,1:T(8,128)(2,1)} %get-tuple-element.198, f32[4,512,2048]{2,1,0:T(8,128)} %get-tuple-element.163, f32[4,512]{1,0:T(4,128)S(1)} %broadcast_select_fusion.4), kind=kOutput, calls=%fused_computation.17.clone.1 | convolution fusion | flops 545390592 | bytes 18096132 | tf_op jit(solution)/shard_map/while/body/eval_jaxpr/hqk,khd->qhd/dot_general | solution.py:60
  179.6 0.7 dynamic_slice.41
  181.3 0.8 compare_and_fusion.4
  182.1 13.5 %fusion.69 = (f32[4,512]{1,0:T(4,128)S(1)}, f32[4,512,2048]{2,1,0:T(8,128)}) fusion(pred[512,2048]{1,0:T(8,128)(4,1)S(1)} %compare_and_fusion.4, bf16[2048,4,64]{0,2,1:T(8,128)(2,1)} %get-tuple-element.197, bf16[2048,4,64]{0,2,1:T(8,128)(2,1)} %get-tuple-element.196, s32[]{:T(128)S(6)} %select_n.104), kind=kOutput, calls=%fused_computation.75.clone.1 | convolution fusion | flops 1098909696 | bytes 21505024 | tf_op jit(solution)/shard_map/while/body/eval_jaxpr/sub | solution.py:56
  195.6 8.7 %fusion.70 = bf16[4,512,4,64]{1,3,2,0:T(8,128)(2,1)S(1)} fusion(bf16[4,512,4,64]{1,3,2,0:T(8,128)(2,1)S(1)} %get-tuple-element.179, s32[]{:T(128)} %get-tuple-element.178, bf16[2048,4,64]{0,2,1:T(8,128)(2,1)} %get-tuple-element.198, f32[4,512,2048]{2,1,0:T(8,128)} %get-tuple-element.163, f32[4,512]{1,0:T(4,128)S(1)} %broadcast_select_fusion.4), kind=kOutput, calls=%fused_computation.17.clone.1 | convolution fusion | flops 545390592 | bytes 18096132 | tf_op jit(solution)/shard_map/while/body/eval_jaxpr/hqk,khd->qhd/dot_general | solution.py:60
  204.3 0.7 dynamic_slice.41
  206.0 0.8 compare_and_fusion.4
  206.8 13.4 %fusion.69 = (f32[4,512]{1,0:T(4,128)S(1)}, f32[4,512,2048]{2,1,0:T(8,128)}) fusion(pred[512,2048]{1,0:T(8,128)(4,1)S(1)} %compare_and_fusion.4, bf16[2048,4,64]{0,2,1:T(8,128)(2,1)} %get-tuple-element.197, bf16[2048,4,64]{0,2,1:T(8,128)(2,1)} %get-tuple-element.196, s32[]{:T(128)S(6)} %select_n.104), kind=kOutput, calls=%fused_computation.75.clone.1 | convolution fusion | flops 1098909696 | bytes 21505024 | tf_op jit(solution)/shard_map/while/body/eval_jaxpr/sub | solution.py:56
  220.2 8.7 %fusion.70 = bf16[4,512,4,64]{1,3,2,0:T(8,128)(2,1)S(1)} fusion(bf16[4,512,4,64]{1,3,2,0:T(8,128)(2,1)S(1)} %get-tuple-element.179, s32[]{:T(128)} %get-tuple-element.178, bf16[2048,4,64]{0,2,1:T(8,128)(2,1)} %get-tuple-element.198, f32[4,512,2048]{2,1,0:T(8,128)} %get-tuple-element.163, f32[4,512]{1,0:T(4,128)S(1)} %broadcast_select_fusion.4), kind=kOutput, calls=%fused_computation.17.clone.1 | convolution fusion | flops 545390592 | bytes 18096132 | tf_op jit(solution)/shard_map/while/body/eval_jaxpr/hqk,khd->qhd/dot_general | solution.py:60
  229.0 0.8 copy.24
  229.8 0.3 copy.30
  230.1 3.3 %convolution_convert_fusion = bf16[2048,1024]{0,1:T(8,128)(2,1)} fusion(bf16[2048,256]{0,1:T(8,128)(2,1)S(1)} %bitcast.50, bf16[256,1024]{1,0:T(8,128)(2,1)S(1)} %copy-done), kind=kOutput, calls=%fused_computation.33 | convolution fusion | flops 1075838976 | bytes 5767168 | tf_op jit(solution)/shard_map/dot_general | solution.py:130
  233.4 5.0 %all-to-all-start.2 = ((bf16[4,2048,256]{1,2,0:T(8,128)(2,1)}), bf16[4,2048,256]{1,2,0:T(8,128)(2,1)}, u32[]{:S(2)}, u32[]{:S(2)}) async-start(bf16[4,2048,256]{1,2,0:T(8,128)(2,1)} %bitcast.47), calls=%async_computation.2 | async-start | bytes 8388608 | tf_op jit(solution)/shard_map/all_to_all | solution.py:21
  238.4 0.1 convert_reduce_fusion.2
  238.5 0.6 convert_reduce_fusion.4
  239.1 1.4 copy.23
  240.5 44.8 %all-to-all-done.2 = bf16[4,2048,256]{1,2,0:T(8,128)(2,1)} async-done(((bf16[4,2048,256]{1,2,0:T(8,128)(2,1)}), bf16[4,2048,256]{1,2,0:T(8,128)(2,1)}, u32[]{:S(2)}, u32[]{:S(2)}) %all-to-all-start.2) | async-done | bytes 4194336 | tf_op jit(solution)/shard_map/all_to_all | solution.py:21
  285.3 3.2 %convert_reduce_fusion.1 = f32[2048,256]{0,1:T(8,128)S(1)} fusion(bf16[4,2048,256]{1,2,0:T(8,128)(2,1)} %all-to-all-done.2), kind=kLoop, calls=%fused_computation.32 | loop fusion | flops 3670016 | bytes 6291456 | tf_op jit(solution)/shard_map/reduce_sum | solution.py:22
  288.6 0.4 select_reduce_fusion.4
  289.0 0.7 pad_maximum_fusion
  289.7 0.7 broadcast_in_dim.134
  290.4 12.9 %all-to-all-start.3 = ((f32[64,1,257]{2,1,0:T(1,128)}), f32[64,1,257]{2,1,0:T(1,128)S(1)}, u32[]{:S(2)}, u32[]{:S(2)}) async-start(f32[64,1,257]{2,1,0:T(1,128)} %broadcast_in_dim.134), calls=%async_computation.3 | async-start | bytes 196608 | tf_op jit(solution)/shard_map/all_to_all | solution.py:27
  303.3 2.5 fusion.34
  305.8 2.3 copy.26
  308.1 5.8 %all-to-all-done.3 = f32[64,1,257]{2,1,0:T(1,128)S(1)} async-done(((f32[64,1,257]{2,1,0:T(1,128)}), f32[64,1,257]{2,1,0:T(1,128)S(1)}, u32[]{:S(2)}, u32[]{:S(2)}) %all-to-all-start.3) | async-done | bytes 65824 | tf_op jit(solution)/shard_map/all_to_all | solution.py:27
  313.9 0.1 reduce_sum.118
  314.0 0.5 slice.7
  314.5 0.6 slice_divide_fusion
  315.2 0.7 select_convert_fusion
  (49 shorter events, 1.5 us)
Async XLA Ops:
  7.2 222.9 %copy-start = (bf16[256,1024]{1,0:T(8,128)(2,1)S(1)}, bf16[256,1024]{1,0:T(8,128)(2,1)}, u32[]{:S(2)}) copy-start(bf16[256,1024]{1,0:T(8,128)(2,1)} %param.19) | copy-start | bytes 1572868
  10.3 22.6 %all-to-all-start.1 = ((s32[64,2,1]{1,2,0:T(1,128)}), s32[64,2,1]{1,2,0:T(1,128)S(1)}, u32[]{:S(2)}, u32[]{:S(2)}) async-start(s32[64,2,1]{1,2,0:T(1,128)} %bitcast), calls=%async_computation.1 | async-start | bytes 65536 | tf_op jit(solution)/shard_map/all_to_all | solution.py:98
  26.6 41.1 %copy-start.4 = (s32[128]{0:T(128)S(1)}, s32[128]{0:T(128)}, u32[]{:S(2)}) copy-start(s32[128]{0:T(128)} %param.15) | copy-start | bytes 1540
  32.8 33.1 %all-to-all-start = ((bf16[64,32,256]{2,1,0:T(8,128)(2,1)}), bf16[64,32,256]{2,1,0:T(8,128)(2,1)S(1)}, u32[]{:S(2)}, u32[]{:S(2)}) async-start(bf16[64,32,256]{2,1,0:T(8,128)(2,1)} %bitcast.2), calls=%async_computation | async-start | bytes 2097152 | tf_op jit(solution)/shard_map/all_to_all | solution.py:104
  37.6 79.8 %all-gather.2.cloned.1.call-start = ((), (), s32[]{:S(2)}) async-start(), calls=%async_computation.4 | async-start | bytes 5242880 | tf_op jit(solution)/shard_map/all_gather | solution.py:108
  117.4 3.4 %copy-start.1 = (bf16[2048,1024]{1,0:T(8,128)(2,1)S(1)}, bf16[2048,1024]{1,0:T(8,128)(2,1)}, u32[]{:S(2)}) copy-start(bf16[2048,1024]{1,0:T(8,128)(2,1)} %all-gather.2.cloned.1.call-done) | copy-start | bytes 12582916
  122.2 1.1 copy-start.5
  123.4 2.3 copy-start.6
  125.7 2.3 copy-start.7
  233.4 5.7 %copy-start.2 = (bf16[128,16,256]{2,1,0:T(8,128)(2,1)S(1)}, bf16[128,16,256]{2,1,0:T(8,128)(2,1)}, u32[]{:S(2)}) copy-start(bf16[128,16,256]{2,1,0:T(8,128)(2,1)} %broadcast_select_fusion.1) | copy-start | bytes 3145732
  233.4 51.9 %all-to-all-start.2 = ((bf16[4,2048,256]{1,2,0:T(8,128)(2,1)}), bf16[4,2048,256]{1,2,0:T(8,128)(2,1)}, u32[]{:S(2)}, u32[]{:S(2)}) async-start(bf16[4,2048,256]{1,2,0:T(8,128)(2,1)} %bitcast.47), calls=%async_computation.2 | async-start | bytes 8388608 | tf_op jit(solution)/shard_map/all_to_all | solution.py:21
  285.3 3.3 %copy-start.3 = (bf16[2048,256]{0,1:T(8,128)(2,1)S(1)}, bf16[2048,256]{0,1:T(8,128)(2,1)}, u32[]{:S(2)}) copy-start(bf16[2048,256]{0,1:T(8,128)(2,1)} %copy.23) | copy-start | bytes 3145732
  290.4 23.5 %all-to-all-start.3 = ((f32[64,1,257]{2,1,0:T(1,128)}), f32[64,1,257]{2,1,0:T(1,128)S(1)}, u32[]{:S(2)}, u32[]{:S(2)}) async-start(f32[64,1,257]{2,1,0:T(1,128)} %broadcast_in_dim.134), calls=%async_computation.3 | async-start | bytes 196608 | tf_op jit(solution)/shard_map/all_to_all | solution.py:27
Sparse Core Ops, SparseCore 0:
  67.9 49.4 all-gather.1
where the time goes:
time: 323 us
  waiting for transfers between devices  133 us (41%)
  matrix products  99.3 us (31%)
  starting transfers between devices  35.8 us (11%)
  other arithmetic  22.8 us (7%)
  local copies, waits for them, and re-layouts  14.6 us (5%)
  between operations  14.3 us (4%)
    sub x4, matrix products, attend(): raised = jnp.where(allowed[None], jnp.exp(scores - peak), 0.0)  53.8 us
    all_gather x1, waiting for transfers between devices, on_device(): full_rows = lax.all_gather(own_cols, 'mp', axis=1, tiled=True)  49.4 us
    all_to_all x1, waiting for transfers between devices, sent_and_summed(): lax.all_to_all(cut_along(shard, dim, length), axis, 0, 0, tiled=True)  44.8 us
    dot_general x4, matrix products, attend(): jnp.einsum('hqk,khd->qhd', weights, values, preferred_element_type=jnp.fl...  34.9 us
    all_to_all x1, waiting for transfers between devices, on_device(): lax.all_to_all(outgoing, 'dp', split_axis=0, concat_axis=0, tiled=True)  26.7 us
    all_to_all x1, starting transfers between devices, on_device(): lax.all_to_all(slot_sent, 'dp', split_axis=0, concat_axis=0, tiled=True)  13.1 us
    all_to_all x1, starting transfers between devices, sent_to_all(): return lax.all_to_all(copies, axis, split_axis=0, concat_axis=0, tiled=True)  12.9 us
  transfers between devices with their start and end apart: 5, of which 5 were waited for; matrix products, arithmetic and copies ran while one was open for 4% of the time, Pallas kernels for 0%

commit v1 on v0

v1 whole, which is shorter than its diff:
```python
import functools
import jax
import jax.numpy as jnp
from jax import lax
from jax.experimental import pallas as pl
from jax.experimental.pallas import tpu as pltpu
from jax.sharding import PartitionSpec as P

EPSILON = 1e-06
SLOTS = 128
TILE = 16
D = 1024
PARTS = 4
PW = D // PARTS
PART_SLOTS = SLOTS // PARTS
WIN = PART_SLOTS + 16
ROWS_W = WIN * TILE
IMG = 16
EXTRA = 3 * IMG
HD = 64
MAX_LOCAL = 4
PAY = 72
IMG_ROWS = 256
VMEM = pltpu.CompilerParams(vmem_limit_bytes=56 * 1024 * 1024)


def send_kernel(owner_ref, slot_ref, mp_ref, patch_ref, out_ref, count_ref, place_ref):
    owners = out_ref.shape[0]

    def clear(o, carry):
        count_ref[o] = 0
        return carry

    lax.fori_loop(0, owners, clear, 0)

    def move(t, carry):
        o = owner_ref[t]
        r = count_ref[o]
        count_ref[o] = r + 1
        place_ref[2 * o + r] = slot_ref[t]
        rows = patch_ref[pl.ds(pl.multiple_of(t * TILE, TILE), TILE), :]
        base = pl.multiple_of(r * 2 * TILE, TILE)
        out_ref[o, pl.ds(base, TILE), :] = rows[:, :128]
        out_ref[o, pl.ds(base + TILE, TILE), :] = rows[:, 128:]
        return carry

    lax.fori_loop(0, SLOTS, move, 0)
    row = lax.broadcasted_iota(jnp.int32, (PAY - 64, 128), 0)

    def label(o, carry):
        value = jnp.where(row == 0, place_ref[2 * o], place_ref[2 * o + 1])
        out_ref[o, 64:, :] = value.astype(jnp.float32).astype(jnp.bfloat16)
        return carry

    lax.fori_loop(0, owners, label, 0)


def send_pack(owner, slot, mp, patches, senders):
    return pl.pallas_call(
        send_kernel,
        grid_spec=pltpu.PrefetchScalarGridSpec(
            num_scalar_prefetch=3,
            grid=(1,),
            in_specs=[pl.BlockSpec((SLOTS * TILE, PW), lambda i, a, b, m: (0, m[0]))],
            out_specs=pl.BlockSpec((senders, PAY, 128), lambda i, a, b, m: (0, 0, 0)),
            scratch_shapes=[pltpu.SMEM((senders,), jnp.int32), pltpu.SMEM((2 * senders,), jnp.int32)],
        ),
        out_shape=jax.ShapeDtypeStruct((senders, PAY, 128), jnp.bfloat16),
        compiler_params=VMEM,
        name="send_pack",
    )(owner, slot, mp, patches)


def arrive_kernel(slot_ref, in_ref, out_ref):
    out_ref[PARTS - 1, PART_SLOTS * TILE :, :] = jnp.zeros((ROWS_W - PART_SLOTS * TILE, PW), jnp.bfloat16)

    def move(n, carry):
        t = slot_ref[n]
        s = n // 2
        base = pl.multiple_of((n % 2) * 2 * TILE, TILE)
        left = in_ref[s, pl.ds(base, TILE), :]
        right = in_ref[s, pl.ds(base + TILE, TILE), :]
        part = t // PART_SLOTS
        local = t % PART_SLOTS
        at = pl.multiple_of(local * TILE, TILE)
        out_ref[part, pl.ds(at, TILE), :128] = left
        out_ref[part, pl.ds(at, TILE), 128:] = right

        @pl.when((local < WIN - PART_SLOTS) & (part > 0))
        def _():
            again = pl.multiple_of((PART_SLOTS + local) * TILE, TILE)
            out_ref[part - 1, pl.ds(again, TILE), :128] = left
            out_ref[part - 1, pl.ds(again, TILE), 128:] = right

        return carry

    lax.fori_loop(0, SLOTS, move, 0)


def arrive_sort(slots, incoming):
    return pl.pallas_call(
        arrive_kernel,
        grid_spec=pltpu.PrefetchScalarGridSpec(
            num_scalar_prefetch=1,
            grid=(1,),
            in_specs=[pl.BlockSpec(incoming.shape, lambda i, a: (0, 0, 0))],
            out_specs=pl.BlockSpec((PARTS, ROWS_W, PW), lambda i, a: (0, 0, 0)),
        ),
        out_shape=jax.ShapeDtypeStruct((PARTS, ROWS_W, PW), jnp.bfloat16),
        compiler_params=VMEM,
        name="arrive_sort",
    )(slots, incoming)


def block_kernel(meta_ref, x_ref, own_m, own_o, a_m, a_o, b_m, b_o, c_m1, c_m2, c_o1, c_o2, out_ref, sum_ref,
                 norm_ref, q_ref, k_ref, v_ref, att_ref, acc_ref, w_refs, sems):
    core = meta_ref[10]
    first = meta_ref[0]
    count = meta_ref[1]
    copies = []
    sources = ((own_m, None), (own_o, None), (a_m, None), (a_o, None), (b_m, None), (b_o, None), (c_m1, c_m2), (c_o1, c_o2))
    at = 0
    for n, (one, two) in enumerate(sources):
        if two is None:
            copies.append([pltpu.make_async_copy(one, w_refs.at[n], sems.at[at])])
            at += 1
        else:
            copies.append([
                pltpu.make_async_copy(one, w_refs.at[n, 0:2], sems.at[at]),
                pltpu.make_async_copy(two, w_refs.at[n, 2:4], sems.at[at + 1]),
            ])
            at += 2
    for group in copies:
        for copy in group:
            copy.start()

    chunk = 64

    def norm(i, carry):
        at = pl.multiple_of(i * chunk, chunk)
        rows = [x_ref[p, pl.ds(at, chunk), :].astype(jnp.float32) for p in range(PARTS)]
        mean = sum(jnp.sum(r, axis=-1, keepdims=True) for r in rows) * (1.0 / D)
        centred = [r - mean for r in rows]
        spread = sum(jnp.sum(r * r, axis=-1, keepdims=True) for r in centred) * (1.0 / D)
        scale = lax.rsqrt(spread + EPSILON)
        for p in range(PARTS):
            norm_ref[p // 2, pl.ds(at, chunk), (p % 2) * PW : (p % 2 + 1) * PW] = (centred[p] * scale).astype(jnp.bfloat16)
        return carry

    lax.fori_loop(0, ROWS_W // chunk, norm, 0)
    lane = lax.broadcasted_iota(jnp.int32, (IMG_ROWS, PW), 1)
    low = lax.broadcasted_iota(jnp.int32, (IMG_ROWS, 128), 1) < HD

    for g in range(PARTS):
        for copy in copies[2 * g] + copies[2 * g + 1]:
            copy.wait()
        mine = norm_ref[core]
        other = norm_ref[1 - core]
        for n, ref in enumerate((q_ref, k_ref, v_ref)):
            total = jnp.dot(mine, w_refs[2 * g, n], preferred_element_type=jnp.float32)
            total = total + jnp.dot(other, w_refs[2 * g + 1, n], preferred_element_type=jnp.float32)
            ref[...] = total.astype(jnp.bfloat16)

        def image(i, carry):
            row = pl.multiple_of(meta_ref[2 + i] * TILE, TILE)
            limit = (meta_ref[6 + i] - meta_ref[2 + i]) * TILE
            queries = q_ref[pl.ds(row, IMG_ROWS), :]
            keys = k_ref[pl.ds(row, IMG_ROWS), :]
            values = v_ref[pl.ds(row, IMG_ROWS), :]
            allowed = lane < limit
            parts = []
            for h in range(PW // HD):
                inside = (lane >= h * HD) & (lane < (h + 1) * HD)
                head_keys = jnp.where(inside, keys, jnp.zeros_like(keys))
                head_values = jnp.where(inside, values, jnp.ones_like(values))
                scores = lax.dot_general(queries, head_keys, (((1,), (1,)), ((), ())), preferred_element_type=jnp.float32)
                scores = jnp.where(allowed, scores, -1e30)
                peak = jnp.max(scores, axis=-1, keepdims=True)
                raised = jnp.exp((scores - peak) * HD ** (-0.5)).astype(jnp.bfloat16)
                mixed = jnp.dot(raised, head_values, preferred_element_type=jnp.float32)
                near, far = (mixed[:, :128], mixed[:, 128:]) if h < 2 else (mixed[:, 128:], mixed[:, :128])
                parts.append(near / far)
            for half in range(2):
                att_ref[half, pl.ds(row, IMG_ROWS), :] = jnp.where(low, parts[2 * half], parts[2 * half + 1]).astype(jnp.bfloat16)
            return carry

        lax.fori_loop(0, count, image, 0)
        att_mine = att_ref[core]
        att_other = att_ref[1 - core]
        for n in range(PARTS):
            rows = slice(n * 128, (n + 1) * 128)
            term = jnp.dot(att_mine, w_refs[2 * g, 3, rows, :], preferred_element_type=jnp.float32)
            term = term + jnp.dot(att_other, w_refs[2 * g + 1, 3, rows, :], preferred_element_type=jnp.float32)
            term = term.astype(jnp.bfloat16).astype(jnp.float32)
            if g == 0:
                acc_ref[n] = term
            else:
                acc_ref[n] += term

    begin = meta_ref[2] * TILE
    end = meta_ref[11] * TILE
    row_ids = lax.broadcasted_iota(jnp.int32, (ROWS_W, PW), 0)
    live = (row_ids >= begin) & (row_ids < end)
    image_ids = lax.broadcasted_iota(jnp.int32, (IMG, WIN), 0)
    tile_ids = lax.broadcasted_iota(jnp.int32, (IMG, WIN), 1)
    lengths = jnp.ones((IMG, PW), jnp.float32)
    pooled_ids = lax.broadcasted_iota(jnp.int32, (IMG, PW), 0)
    member = jnp.zeros((IMG, WIN), jnp.float32)
    for i in range(MAX_LOCAL):
        here = (image_ids == first + i) & (tile_ids >= meta_ref[2 + i]) & (tile_ids < meta_ref[6 + i])
        member = jnp.where(here, 1.0, member)
        rows_i = ((meta_ref[6 + i] - meta_ref[2 + i]) * TILE).astype(jnp.float32)
        lengths = jnp.where((pooled_ids == first + i) & (rows_i > 0), rows_i, lengths)
    for n in range(PARTS):
        result = jnp.where(live, x_ref[n].astype(jnp.float32) + acc_ref[n], 0.0)
        out_ref[n, :ROWS_W, :] = result.astype(jnp.bfloat16)
        tile_sums = jnp.sum(result.reshape(WIN, TILE, PW), axis=1)
        sums = jnp.dot(member, tile_sums, precision=lax.Precision.HIGHEST, preferred_element_type=jnp.float32)
        pooled = sums / lengths
        one = pooled.astype(jnp.bfloat16)
        rest = pooled - one.astype(jnp.float32)
        two = rest.astype(jnp.bfloat16)
        three = (rest - two.astype(jnp.float32)).astype(jnp.bfloat16)
        out_ref[n, ROWS_W : ROWS_W + IMG, :] = one
        out_ref[n, ROWS_W + IMG : ROWS_W + 2 * IMG, :] = two
        out_ref[n, ROWS_W + 2 * IMG : ROWS_W + 3 * IMG, :] = three
        sum_ref[0:1, n * PW : (n + 1) * PW] = jnp.sum(pooled, axis=0, keepdims=True)
    sum_ref[1:2, :] = jnp.full((1, D), count, jnp.int32).astype(jnp.float32)


def block(meta, x, weights):
    whole = lambda i, a: (0, 0, 0)
    return pl.pallas_call(
        block_kernel,
        grid_spec=pltpu.PrefetchScalarGridSpec(
            num_scalar_prefetch=1,
            grid=(1,),
            in_specs=[pl.BlockSpec(x.shape, whole)] + [pl.BlockSpec(memory_space=pl.ANY)] * len(weights),
            out_specs=[
                pl.BlockSpec((PARTS, ROWS_W + EXTRA, PW), whole),
                pl.BlockSpec((2, D), lambda i, a: (0, 0)),
            ],
            scratch_shapes=[
                pltpu.VMEM((2, ROWS_W, D // 2), jnp.bfloat16),
                pltpu.VMEM((ROWS_W, PW), jnp.bfloat16),
                pltpu.VMEM((ROWS_W, PW), jnp.bfloat16),
                pltpu.VMEM((ROWS_W, PW), jnp.bfloat16),
                pltpu.VMEM((2, ROWS_W, PW // 2), jnp.bfloat16),
                pltpu.VMEM((PARTS, ROWS_W, PW), jnp.float32),
                pltpu.VMEM((2 * PARTS, 4, D // 2, PW), jnp.bfloat16),
                pltpu.SemaphoreType.DMA((10,)),
            ],
        ),
        out_shape=[
            jax.ShapeDtypeStruct((PARTS, ROWS_W + EXTRA, PW), jnp.bfloat16),
            jax.ShapeDtypeStruct((2, D), jnp.float32),
        ],
        compiler_params=VMEM,
        name="block",
    )(meta, x, *weights)


def finish_kernel(in_ref, out_ref):
    size = PART_SLOTS * TILE
    halo = ROWS_W - size
    for p in range(PARTS):
        start = in_ref[p, :halo, :]
        if p:
            start = start + in_ref[p - 1, size:ROWS_W, :]
        out_ref[p * size : p * size + halo, :] = start
        out_ref[p * size + halo : (p + 1) * size, :] = in_ref[p, halo:size, :]


def finish(incoming):
    return pl.pallas_call(
        finish_kernel,
        out_shape=jax.ShapeDtypeStruct((SLOTS * TILE, PW), jnp.bfloat16),
        compiler_params=VMEM,
        name="finish",
    )(incoming)


def packed_weights(w_query, w_key, w_value, w_out):
    half = D // 2
    inner = jnp.stack([w_query, w_key, w_value]).reshape(3, 2, half, PW).transpose(1, 0, 2, 3)
    outer = w_out.reshape(2, PW // 2, PARTS, PW).transpose(0, 2, 1, 3).reshape(2, 1, half, PW)
    return jnp.concatenate([inner, outer], axis=1)


def on_device(patches, dest_owner, dest_slot, packed_image, w_query, w_key, w_value, w_out):
    senders = lax.axis_size("dp")
    splits = lax.axis_size("mp")
    mp = lax.axis_index("mp")
    core = lax.axis_index("dp") % 2
    up = [(i, (i + 1) % splits) for i in range(splits)]
    down = [(i, (i - 1) % splits) for i in range(splits)]
    swap = [(i, i ^ 1) for i in range(senders)]

    both = packed_weights(w_query, w_key, w_value, w_out)
    own_m = lax.dynamic_index_in_dim(both, core, 0, keepdims=False)
    own_o = lax.dynamic_index_in_dim(both, 1 - core, 0, keepdims=False)
    a_m = lax.ppermute(own_m, "mp", up)
    b_m = lax.ppermute(own_m, "mp", down)
    c_m1 = lax.ppermute(a_m[:2], "mp", up)
    c_m2 = lax.ppermute(b_m[2:], "mp", down)
    a_o = lax.ppermute(a_m, "dp", swap)
    b_o = lax.ppermute(b_m, "dp", swap)
    c_o1 = lax.ppermute(c_m1, "dp", swap)
    c_o2 = lax.ppermute(c_m2, "dp", swap)

    labels = jnp.arange(IMG, dtype=jnp.int32)
    lengths = jnp.sum((packed_image[None, :] == labels[:, None]).astype(jnp.int32), axis=1)
    starts = jnp.sum(((packed_image[None, :] >= 0) & (packed_image[None, :] < labels[:, None])).astype(jnp.int32), axis=1)
    present = lengths > 0
    window = mp * PART_SLOTS
    inside = present & (starts >= window) & (starts < window + PART_SLOTS)
    count = jnp.sum(inside.astype(jnp.int32))
    first = jnp.sum((present & (starts < window)).astype(jnp.int32))
    local = jnp.arange(MAX_LOCAL, dtype=jnp.int32)
    chosen = inside[None, :] & (labels[None, :] == first + local[:, None])
    begin = jnp.sum(jnp.where(chosen, starts[None, :] - window, 0), axis=1)
    end = jnp.sum(jnp.where(chosen, starts[None, :] + lengths[None, :] - window, 0), axis=1)
    meta = jnp.concatenate([jnp.stack([first, count]), begin, end, jnp.stack([core, jnp.max(end)])]).astype(jnp.int32)

    outgoing = send_pack(dest_owner, dest_slot, mp.reshape(1).astype(jnp.int32), patches, senders)
    incoming = lax.all_to_all(outgoing, "dp", split_axis=0, concat_axis=0, tiled=True)
    got_slot = incoming[:, 64:66, 0].astype(jnp.int32).reshape(SLOTS)
    windows = arrive_sort(got_slot, incoming)
    rows = lax.all_to_all(windows, "mp", split_axis=0, concat_axis=0, tiled=True)
    result, local_sum = block(meta, rows, (own_m, own_o, a_m, a_o, b_m, b_o, c_m1, c_m2, c_o1, c_o2))
    total = lax.psum(local_sum, ("dp", "mp"))
    back = lax.all_to_all(result, "mp", split_axis=0, concat_axis=0, tiled=True)
    packed_out = finish(back)
    pooled = jnp.sum(back[:, ROWS_W:, :].astype(jnp.float32).reshape(PARTS, 3, IMG, PW), axis=(0, 1))
    centre = lax.dynamic_slice_in_dim(total[0], mp * PW, PW) / total[1, 0]
    pooled_out = jnp.where(present[:, None], pooled - centre[None, :], 0.0).astype(jnp.bfloat16)
    return (packed_out, pooled_out)


def solution(mesh):
    in_specs = (
        P("dp", None),
        P("dp"),
        P("dp"),
        P("dp"),
        P(None, "mp"),
        P(None, "mp"),
        P(None, "mp"),
        P("mp", None),
    )
    out_specs = (P("dp", "mp"), P("dp", "mp"))
    return jax.shard_map(on_device, mesh=mesh, in_specs=in_specs, out_specs=out_specs, check_vma=False)
```

time: 323 us -> 227 us (0.70)
  matrix products: 99.3 us -> 0 us
  blocking collectives: 0 us -> 88.7 us
  waiting for transfers between devices: 133 us -> 44.7 us
  Pallas kernels: 0 us -> 43.7 us
  other arithmetic: 22.8 us -> 7.42 us
  between operations: 14.3 us -> 0.86 us
  local copies, waits for them, and re-layouts: 14.6 us -> 9.91 us
  starting transfers between devices: 35.8 us -> 32.2 us
    psum x0 -> x1, blocking collectives: none -> 88.7 us  [on_device(): total = lax.psum(local_sum, ('dp', 'mp'))]
    all_to_all x3 -> x2, waiting for transfers between devices: 56.8 us -> 0.01 us  [the longest x1 0.01 us: on_device(): back = lax.all_to_all(result, 'mp', split_axis=0, concat_axis=0, tiled=True)]
    sub x4 -> x0, matrix products: 53.8 us -> none  [attend(): raised = jnp.where(allowed[None], jnp.exp(scores - peak), 0.0)]
    all_gather x1 -> x0, waiting for transfers between devices: 49.4 us -> none  [on_device(): full_rows = lax.all_gather(own_cols, 'mp', axis=1, tiled=True)]
    dot_general x9 -> x0, matrix products: 45.5 us -> none  [the longest x4 34.9 us: attend(): jnp.einsum('hqk,khd->qhd', weights, values, preferred_element_type=jnp.fl...]
    pallas_call x0 -> x4, Pallas kernels: none -> 43.7 us  [the longest x1 29.7 us: block(): pl.pallas_call(block_kernel, grid_spec=pltpu.PrefetchScalarGridSpec(num_s...]
    all_to_all x3 -> x2, starting transfers between devices: 31 us -> 7.59 us  [the longest x1 4.01 us: on_device(): lax.all_to_all(windows, 'mp', split_axis=0, concat_axis=0, tiled=True)]
    ppermute x0 -> x8, waiting for transfers between devices: none -> 20.1 us  [the longest x1 20.1 us: on_device(): c_m2 = lax.ppermute(b_m[2:], 'mp', down)]
  transfers between devices with their start and end apart: 5 -> 11, of which waited for: 5 -> 2; matrix products, arithmetic and copies ran while one was open for 4% -> 6% of each run, Pallas kernels for 0% -> 3%
where the time goes in v1:
time: 227 us
  blocking collectives  88.7 us (39%)
  waiting for transfers between devices  44.7 us (20%)
  Pallas kernels  43.7 us (19%)
  starting transfers between devices  32.2 us (14%)
  local copies, waits for them, and re-layouts  9.91 us (4%)
  other arithmetic  7.42 us (3%)
    psum x1, blocking collectives, on_device(): total = lax.psum(local_sum, ('dp', 'mp'))  88.7 us
    pallas_call x1, Pallas kernels, block(): pl.pallas_call(block_kernel, grid_spec=pltpu.PrefetchScalarGridSpec(num_s...  29.7 us
    all_to_all x1, waiting for transfers between devices, on_device(): lax.all_to_all(outgoing, 'dp', split_axis=0, concat_axis=0, tiled=True)  24.6 us
    ppermute x1, waiting for transfers between devices, on_device(): c_m2 = lax.ppermute(b_m[2:], 'mp', down)  20.1 us
    all_to_all x1, starting transfers between devices, on_device(): lax.all_to_all(outgoing, 'dp', split_axis=0, concat_axis=0, tiled=True)  13.3 us
    pallas_call x1, Pallas kernels, arrive_sort(): pl.pallas_call(arrive_kernel, grid_spec=pltpu.PrefetchScalarGridSpec(num_...  6.36 us
    pallas_call x1, Pallas kernels, send_pack(): pl.pallas_call(send_kernel, grid_spec=pltpu.PrefetchScalarGridSpec(num_sc...  5.14 us
  transfers between devices with their start and end apart: 11, of which 2 were waited for; matrix products, arithmetic and copies ran while one was open for 6% of the time, Pallas kernels for 3%

profile of v1, /device:TPU:1, one launch (start us, length us, event | category | flops | bytes accessed | tf_op | source)
XLA Modules:
  0.0 227.4 jit_solution(17321461863418835286)
XLA Ops:
  0.6 5.1 %send_pack.1 = bf16[64,72,128]{2,1,0:T(8,128)(2,1)} custom-call(s32[128]{0:T(128)} %owner_ref.1, s32[128]{0:T(128)} %slot_ref.1, s32[1]{0:T(128)} %bitcast.4.mp_ref, bf16[2048,1024]{1,0:T(8,128)(2,1)} %patch_ref.1), custom_call_target="tpu_custom_call" | custom-call | tf_op jit(solution)/shard_map/send_pack/pallas_call | solution.py:59
  5.8 0.0 copy-start.5
  5.8 13.3 %all-to-all-start = ((bf16[64,72,128]{2,1,0:T(8,128)(2,1)}), bf16[64,72,128]{2,1,0:T(8,128)(2,1)S(1)}, u32[]{:S(2)}, u32[]{:S(2)}) async-start(bf16[64,72,128]{2,1,0:T(8,128)(2,1)} %send_pack.1), calls=%async_computation | async-start | bytes 2359296 | tf_op jit(solution)/shard_map/all_to_all | solution.py:326
  19.1 0.0 copy-start.6
  19.1 0.0 copy-done.5
  19.1 0.4 reshape.60
  19.5 0.1 copy.21
  19.6 0.5 copy-done.6
  20.1 1.4 maximum_bitcast_fusion
  21.5 1.2 fusion.1
  22.6 0.0 copy-start.3
  22.6 2.5 %collective-permute-start.2 = (bf16[4,512,256]{2,1,0:T(8,128)(2,1)S(1)}, bf16[4,512,256]{2,1,0:T(8,128)(2,1)}, u32[]{:S(2)}, u32[]{:S(2)}) collective-permute-start(bf16[4,512,256]{2,1,0:T(8,128)(2,1)S(1)} %get-tuple-element.13.own_m), channel_id=1, source_target_pairs={{0,3},{1,0},{2,1},{3,2},{4,7},{5,4},{6,5},{7,6},{8,11},{9,8},{10,9... | collective-permute-start | bytes 3145736 | tf_op jit(solution)/shard_map/ppermute | solution.py:303
  25.1 0.0 collective-permute-start
  25.1 24.6 %all-to-all-done.in_ref = bf16[64,72,128]{2,1,0:T(8,128)(2,1)S(1)} async-done(((bf16[64,72,128]{2,1,0:T(8,128)(2,1)}), bf16[64,72,128]{2,1,0:T(8,128)(2,1)S(1)}, u32[]{:S(2)}, u32[]{:S(2)}) %all-to-all-start) | async-done | bytes 1179680 | tf_op jit(solution)/shard_map/all_to_all | solution.py:326
  49.7 0.0 copy-start.2
  49.7 1.2 convert_reduce_fusion.1
  50.8 0.7 reshape.62.slot_ref
  51.5 0.0 copy-done.2
  51.5 6.4 %arrive_sort.1 = bf16[4,768,256]{2,1,0:T(8,128)(2,1)} custom-call(s32[128]{0:T(128)} %reshape.62.slot_ref, bf16[64,72,128]{2,1,0:T(8,128)(2,1)} %copy-done.2), custom_call_target="tpu_custom_call" | custom-call | tf_op jit(solution)/shard_map/arrive_sort/pallas_call | solution.py:101
  57.9 4.0 %all-to-all-start.1 = ((bf16[4,768,256]{2,1,0:T(8,128)(2,1)}), bf16[4,768,256]{2,1,0:T(8,128)(2,1)S(1)}, u32[]{:S(2)}, u32[]{:S(2)}) async-start(bf16[4,768,256]{2,1,0:T(8,128)(2,1)} %arrive_sort.1), calls=%async_computation.1 | async-start | bytes 3145728 | tf_op jit(solution)/shard_map/all_to_all | solution.py:329
  61.9 0.0 copy-start.8
  61.9 0.0 collective-permute-done.2.b_m
  61.9 1.9 slice.26
  63.8 2.7 %collective-permute-start.5 = (bf16[2,512,256]{2,1,0:T(8,128)(2,1)}, bf16[2,512,256]{2,1,0:T(8,128)(2,1)S(1)}, u32[]{:S(2)}, u32[]{:S(2)}) collective-permute-start(bf16[2,512,256]{2,1,0:T(8,128)(2,1)} %slice.26), channel_id=1, source_target_pairs={{0,3},{1,0},{2,1},{3,2},{4,7},{5,4},{6,5},{7,6},{8,11},{9,8},{10,9... | collective-permute-start | bytes 1572872 | tf_op jit(solution)/shard_map/ppermute | solution.py:305
  66.4 0.0 collective-permute-done.a_m
  66.4 1.9 slice.25
  68.3 0.0 collective-permute-start.4
  68.3 2.4 %collective-permute-start.3 = (bf16[4,512,256]{2,1,0:T(8,128)(2,1)}, bf16[4,512,256]{2,1,0:T(8,128)(2,1)}, u32[]{:S(2)}, u32[]{:S(2)}) collective-permute-start(bf16[4,512,256]{2,1,0:T(8,128)(2,1)} %collective-permute-done.2.b_m), channel_id=1, source_target_pairs={{0,4},{4,0},{8,12},{12,8},{16,20},{20,16},{24,28},{28,24},{32,36},... | collective-permute-start | bytes 3145736 | tf_op jit(solution)/shard_map/ppermute | solution.py:307
  70.7 0.0 collective-permute-start.1
  70.7 0.0 copy-done.8
  70.7 20.1 %collective-permute-done.5.c_m2 = bf16[2,512,256]{2,1,0:T(8,128)(2,1)S(1)} collective-permute-done((bf16[2,512,256]{2,1,0:T(8,128)(2,1)}, bf16[2,512,256]{2,1,0:T(8,128)(2,1)S(1)}, u32[]{:S(2)}, u32[]{:S(2)}) %collective-permute-start.5) | collective-permute-done | bytes 524320 | tf_op jit(solution)/shard_map/ppermute | solution.py:305
  90.8 0.0 copy-start.4
  90.8 2.5 %collective-permute-start.7 = (bf16[2,512,256]{2,1,0:T(8,128)(2,1)S(1)}, bf16[2,512,256]{2,1,0:T(8,128)(2,1)}, u32[]{:S(2)}, u32[]{:S(2)}) collective-permute-start(bf16[2,512,256]{2,1,0:T(8,128)(2,1)S(1)} %collective-permute-done.5.c_m2), channel_id=1, source_target_pairs={{0,4},{4,0},{8,12},{12,8},{16,20},{20,16},{24,28},{28,24},{32,36},... | collective-permute-start | bytes 1572872 | tf_op jit(solution)/shard_map/ppermute | solution.py:309
  93.3 0.0 collective-permute-done.4.c_m1
  93.3 1.3 collective-permute-start.6
  94.6 0.1 convert_reduce_fusion.3
  94.7 0.6 convert_reduce_fusion.4
  95.3 0.6 iota_add_fusion
  95.9 0.2 select_reduce_fusion
  96.1 0.7 reduce_max.9
  96.8 2.5 %concatenate.7.meta_ref = s32[12]{0:T(128)} concatenate(s32[1]{0:T(128)} %bitcast, s32[1]{0:T(128)} %bitcast.1, s32[4]{0:T(128)S(1)} %get-tuple-element.7, s32[4]{0:T(128)S(1)} %get-tuple-element.6, s32[1]{0:T(128)} %bitcast.2, s32[1]{0:T(128)} %bitcast.3), dimensions={0} | concatenate | bytes 96 | tf_op jit(solution)/shard_map/concatenate | solution.py:323
  99.3 0.0 collective-permute-done.7.c_o2
  99.3 0.0 collective-permute-done.3.b_o
  99.3 0.0 collective-permute-done.6.c_o1
  99.3 0.0 collective-permute-done.1.a_o
  99.4 0.0 all-to-all-done.1.x_ref
  99.4 0.0 copy-start.1
  99.4 0.0 copy-done.3
  99.4 0.0 copy-done.4
  99.4 1.1 copy-done.1
  100.5 29.7 %block.1 = (bf16[4,816,256]{2,1,0:T(8,128)(2,1)}, f32[2,1024]{1,0:T(2,128)}) custom-call(s32[12]{0:T(128)} %concatenate.7.meta_ref, bf16[4,768,256]{2,1,0:T(8,128)(2,1)} %copy-done.1, bf16[4,512,256]{2,1,0:T(8,128)(2,1)} %copy-done.3, bf16[4,512,256]{2,1,0:T(8,128)(2,1)} %get-tuple-element.12.own_o, bf16[4,512,256]{2,1,0:T(8,128)(2,1)} %collective-permute-done.a_m, ...), custom_call_target="tpu_custom_call" | custom-call | tf_op jit(solution)/shard_map/block/pallas_call | solution.py:233
  130.2 0.0 copy-start.7
  130.2 3.6 %all-to-all-start.2 = ((bf16[4,816,256]{2,1,0:T(8,128)(2,1)}), bf16[4,816,256]{2,1,0:T(8,128)(2,1)S(1)}, u32[]{:S(2)}, u32[]{:S(2)}) async-start(bf16[4,816,256]{2,1,0:T(8,128)(2,1)} %get-tuple-element.4), calls=%async_computation.2 | async-start | bytes 3342336 | tf_op jit(solution)/shard_map/all_to_all | solution.py:332
  133.8 0.0 copy-done.7
  133.8 88.7 %psum.7 = f32[2,1024]{1,0:T(2,128)S(1)} all-reduce(f32[2,1024]{1,0:T(2,128)S(1)} %copy-done.7), channel_id=1, replica_groups=mesh['dp'=64,'mp'=4] {'dp','mp'}, use_global_device_ids=true, to_apply=%region_9.10 | all-reduce | flops 2048 | bytes 16384 | tf_op jit(solution)/shard_map/psum | solution.py:331
  222.6 0.5 slice.29
  223.1 0.7 fusion.6
  223.7 0.0 all-to-all-done.2.in_ref
  223.7 0.0 copy-start
  223.8 0.8 select_convert_fusion
  224.6 0.3 copy-done
  224.9 2.5 %finish.1 = bf16[2048,256]{1,0:T(8,128)(2,1)} custom-call(bf16[4,816,256]{2,1,0:T(8,128)(2,1)} %copy-done), custom_call_target="tpu_custom_call" | custom-call | tf_op jit(solution)/shard_map/finish/pallas_call | solution.py:275
  (5 shorter events, 0.0 us)
Async XLA Ops:
  5.8 13.3 %copy-start.5 = (bf16[256,1024]{1,0:T(8,128)(2,1)S(1)}, bf16[256,1024]{1,0:T(8,128)(2,1)}, u32[]{:S(2)}) copy-start(bf16[256,1024]{1,0:T(8,128)(2,1)} %param.15) | copy-start | bytes 1572868
  5.8 43.9 %all-to-all-start = ((bf16[64,72,128]{2,1,0:T(8,128)(2,1)}), bf16[64,72,128]{2,1,0:T(8,128)(2,1)S(1)}, u32[]{:S(2)}, u32[]{:S(2)}) async-start(bf16[64,72,128]{2,1,0:T(8,128)(2,1)} %send_pack.1), calls=%async_computation | async-start | bytes 2359296 | tf_op jit(solution)/shard_map/all_to_all | solution.py:326
  19.1 1.0 copy-start.6
  22.6 76.7 %copy-start.3 = (bf16[4,512,256]{2,1,0:T(8,128)(2,1)}, bf16[4,512,256]{2,1,0:T(8,128)(2,1)S(1)}, u32[]{:S(2)}) copy-start(bf16[4,512,256]{2,1,0:T(8,128)(2,1)S(1)} %get-tuple-element.13.own_m) | copy-start | bytes 3145732
  22.6 39.2 %collective-permute-start.2 = (bf16[4,512,256]{2,1,0:T(8,128)(2,1)S(1)}, bf16[4,512,256]{2,1,0:T(8,128)(2,1)}, u32[]{:S(2)}, u32[]{:S(2)}) collective-permute-start(bf16[4,512,256]{2,1,0:T(8,128)(2,1)S(1)} %get-tuple-element.13.own_m), channel_id=1, source_target_pairs={{0,3},{1,0},{2,1},{3,2},{4,7},{5,4},{6,5},{7,6},{8,11},{9,8},{10,9... | collective-permute-start | bytes 3145736 | tf_op jit(solution)/shard_map/ppermute | solution.py:303
  25.1 41.3 %collective-permute-start = (bf16[4,512,256]{2,1,0:T(8,128)(2,1)S(1)}, bf16[4,512,256]{2,1,0:T(8,128)(2,1)}, u32[]{:S(2)}, u32[]{:S(2)}) collective-permute-start(bf16[4,512,256]{2,1,0:T(8,128)(2,1)S(1)} %get-tuple-element.13.own_m), channel_id=1, source_target_pairs={{0,1},{1,2},{2,3},{3,0},{4,5},{5,6},{6,7},{7,4},{8,9},{9,10},{10,1... | collective-permute-start | bytes 3145736 | tf_op jit(solution)/shard_map/ppermute | solution.py:302
  49.7 1.8 copy-start.2
  57.9 41.5 %all-to-all-start.1 = ((bf16[4,768,256]{2,1,0:T(8,128)(2,1)}), bf16[4,768,256]{2,1,0:T(8,128)(2,1)S(1)}, u32[]{:S(2)}, u32[]{:S(2)}) async-start(bf16[4,768,256]{2,1,0:T(8,128)(2,1)} %arrive_sort.1), calls=%async_computation.1 | async-start | bytes 3145728 | tf_op jit(solution)/shard_map/all_to_all | solution.py:329
  61.9 8.8 %copy-start.8 = (s32[128]{0:T(128)S(1)}, s32[128]{0:T(128)}, u32[]{:S(2)}) copy-start(s32[128]{0:T(128)} %param.11) | copy-start | bytes 1540
  63.8 27.0 %collective-permute-start.5 = (bf16[2,512,256]{2,1,0:T(8,128)(2,1)}, bf16[2,512,256]{2,1,0:T(8,128)(2,1)S(1)}, u32[]{:S(2)}, u32[]{:S(2)}) collective-permute-start(bf16[2,512,256]{2,1,0:T(8,128)(2,1)} %slice.26), channel_id=1, source_target_pairs={{0,3},{1,0},{2,1},{3,2},{4,7},{5,4},{6,5},{7,6},{8,11},{9,8},{10,9... | collective-permute-start | bytes 1572872 | tf_op jit(solution)/shard_map/ppermute | solution.py:305
  68.3 25.0 %collective-permute-start.4 = (bf16[2,512,256]{2,1,0:T(8,128)(2,1)}, bf16[2,512,256]{2,1,0:T(8,128)(2,1)}, u32[]{:S(2)}, u32[]{:S(2)}) collective-permute-start(bf16[2,512,256]{2,1,0:T(8,128)(2,1)} %slice.25), channel_id=1, source_target_pairs={{0,1},{1,2},{2,3},{3,0},{4,5},{5,6},{6,7},{7,4},{8,9},{9,10},{10,1... | collective-permute-start | bytes 1572872 | tf_op jit(solution)/shard_map/ppermute | solution.py:304
  68.3 31.0 %collective-permute-start.3 = (bf16[4,512,256]{2,1,0:T(8,128)(2,1)}, bf16[4,512,256]{2,1,0:T(8,128)(2,1)}, u32[]{:S(2)}, u32[]{:S(2)}) collective-permute-start(bf16[4,512,256]{2,1,0:T(8,128)(2,1)} %collective-permute-done.2.b_m), channel_id=1, source_target_pairs={{0,4},{4,0},{8,12},{12,8},{16,20},{20,16},{24,28},{28,24},{32,36},... | collective-permute-start | bytes 3145736 | tf_op jit(solution)/shard_map/ppermute | solution.py:307
  70.7 28.7 %collective-permute-start.1 = (bf16[4,512,256]{2,1,0:T(8,128)(2,1)}, bf16[4,512,256]{2,1,0:T(8,128)(2,1)}, u32[]{:S(2)}, u32[]{:S(2)}) collective-permute-start(bf16[4,512,256]{2,1,0:T(8,128)(2,1)} %collective-permute-done.a_m), channel_id=1, source_target_pairs={{0,4},{4,0},{8,12},{12,8},{16,20},{20,16},{24,28},{28,24},{32,36},... | collective-permute-start | bytes 3145736 | tf_op jit(solution)/shard_map/ppermute | solution.py:306
  90.8 8.6 %copy-start.4 = (bf16[2,512,256]{2,1,0:T(8,128)(2,1)}, bf16[2,512,256]{2,1,0:T(8,128)(2,1)S(1)}, u32[]{:S(2)}) copy-start(bf16[2,512,256]{2,1,0:T(8,128)(2,1)S(1)} %collective-permute-done.5.c_m2) | copy-start | bytes 1572868
  90.8 8.6 %collective-permute-start.7 = (bf16[2,512,256]{2,1,0:T(8,128)(2,1)S(1)}, bf16[2,512,256]{2,1,0:T(8,128)(2,1)}, u32[]{:S(2)}, u32[]{:S(2)}) collective-permute-start(bf16[2,512,256]{2,1,0:T(8,128)(2,1)S(1)} %collective-permute-done.5.c_m2), channel_id=1, source_target_pairs={{0,4},{4,0},{8,12},{12,8},{16,20},{20,16},{24,28},{28,24},{32,36},... | collective-permute-start | bytes 1572872 | tf_op jit(solution)/shard_map/ppermute | solution.py:309
  93.3 6.0 %collective-permute-start.6 = (bf16[2,512,256]{2,1,0:T(8,128)(2,1)}, bf16[2,512,256]{2,1,0:T(8,128)(2,1)}, u32[]{:S(2)}, u32[]{:S(2)}) collective-permute-start(bf16[2,512,256]{2,1,0:T(8,128)(2,1)} %collective-permute-done.4.c_m1), channel_id=1, source_target_pairs={{0,4},{4,0},{8,12},{12,8},{16,20},{20,16},{24,28},{28,24},{32,36},... | collective-permute-start | bytes 1572872 | tf_op jit(solution)/shard_map/ppermute | solution.py:308
  99.4 1.1 copy-start.1
  130.2 3.6 %copy-start.7 = (f32[2,1024]{1,0:T(2,128)S(1)}, f32[2,1024]{1,0:T(2,128)}, u32[]{:S(2)}) copy-start(f32[2,1024]{1,0:T(2,128)} %get-tuple-element.5) | copy-start | bytes 24580
  130.2 93.5 %all-to-all-start.2 = ((bf16[4,816,256]{2,1,0:T(8,128)(2,1)}), bf16[4,816,256]{2,1,0:T(8,128)(2,1)S(1)}, u32[]{:S(2)}, u32[]{:S(2)}) async-start(bf16[4,816,256]{2,1,0:T(8,128)(2,1)} %get-tuple-element.4), calls=%async_computation.2 | async-start | bytes 3342336 | tf_op jit(solution)/shard_map/all_to_all | solution.py:332
  223.7 1.2 copy-start

commit v2 on v1

v2 whole, which is shorter than its diff:
```python
import jax
import jax.numpy as jnp
from jax import lax
from jax.experimental import pallas as pl
from jax.experimental.pallas import tpu as pltpu
from jax.sharding import PartitionSpec as P

EPSILON = 1e-06
SLOTS = 128
TILE = 16
D = 1024
PARTS = 4
PW = D // PARTS
PART_SLOTS = SLOTS // PARTS
WIN = PART_SLOTS + 16
ROWS_W = WIN * TILE
IMG = 16
EXTRA = 3 * IMG
HD = 64
MAX_LOCAL = 4
PAY = 72
IMG_ROWS = 256
EXP_SCALE = HD ** (-0.5) * 1.4426950408889634
VMEM = pltpu.CompilerParams(vmem_limit_bytes=56 * 1024 * 1024)


def send_kernel(owner_ref, slot_ref, mp_ref, image_ref, patch_ref, out_ref, count_ref, place_ref):
    owners = out_ref.shape[0]

    def clear(o, carry):
        count_ref[o] = 0
        return carry

    lax.fori_loop(0, owners, clear, 0, unroll=8)

    def move(t, carry):
        o = owner_ref[t]
        r = count_ref[o]
        count_ref[o] = r + 1
        place_ref[2 * o + r] = slot_ref[t]
        rows = patch_ref[pl.ds(pl.multiple_of(t * TILE, TILE), TILE), :]
        base = pl.multiple_of(r * 2 * TILE, TILE)
        out_ref[o, pl.ds(base, TILE), :] = rows[:, :128]
        out_ref[o, pl.ds(base + TILE, TILE), :] = rows[:, 128:]
        return carry

    lax.fori_loop(0, SLOTS, move, 0, unroll=8)
    row = lax.broadcasted_iota(jnp.int32, (PAY - 64, 128), 0)
    images = jnp.max(image_ref[...], axis=1, keepdims=True) + 1
    images = jnp.broadcast_to(images, row.shape)

    def label(o, carry):
        value = jnp.where(row == 0, place_ref[2 * o], jnp.where(row == 1, place_ref[2 * o + 1], images))
        out_ref[o, 64:, :] = value.astype(jnp.float32).astype(jnp.bfloat16)
        return carry

    lax.fori_loop(0, owners, label, 0, unroll=8)


def send_pack(owner, slot, mp, image, patches, senders):
    return pl.pallas_call(
        send_kernel,
        grid_spec=pltpu.PrefetchScalarGridSpec(
            num_scalar_prefetch=3,
            grid=(1,),
            in_specs=[
                pl.BlockSpec((1, SLOTS), lambda i, a, b, m: (0, 0)),
                pl.BlockSpec((SLOTS * TILE, PW), lambda i, a, b, m: (0, m[0])),
            ],
            out_specs=pl.BlockSpec((senders, PAY, 128), lambda i, a, b, m: (0, 0, 0)),
            scratch_shapes=[pltpu.SMEM((senders,), jnp.int32), pltpu.SMEM((2 * senders,), jnp.int32)],
        ),
        out_shape=jax.ShapeDtypeStruct((senders, PAY, 128), jnp.bfloat16),
        compiler_params=VMEM,
        name="send_pack",
    )(owner, slot, mp, image, patches)


def arrive_kernel(mp_ref, in_ref, out0, out1, out2, out3, total_ref, sorted_ref, label_ref, slot_ref, sems):
    senders = in_ref.shape[0]
    row = lax.broadcasted_iota(jnp.int32, (8, 128), 0)
    lane = lax.broadcasted_iota(jnp.int32, (8, 128), 1)
    picked = jnp.zeros((8, 128), jnp.float32)
    total = jnp.zeros((8, 128), jnp.float32)
    for s in range(senders):
        marks = in_ref[s, 64:, :].astype(jnp.float32)
        picked = jnp.where((lane == 2 * s) | (lane == 2 * s + 1), marks, picked)
        total = total + marks
    odd = (lane & 1) == 1
    own = jnp.where(row == jnp.where(odd, 1, 0), picked, 0.0)
    label_ref[...] = jnp.broadcast_to(jnp.sum(own, axis=0, keepdims=True), (8, 128)).astype(jnp.int32)
    copy = pltpu.make_async_copy(label_ref, slot_ref, sems.at[4])
    copy.start()
    total_ref[...] = jnp.broadcast_to(jnp.sum(jnp.where(row == 2, total, 0.0), axis=0, keepdims=True), (8, 128))
    sorted_ref[SLOTS * TILE :, :] = jnp.zeros((ROWS_W - PART_SLOTS * TILE, PW), jnp.bfloat16)
    copy.wait()

    def move(s, carry):
        for r in range(2):
            at = pl.multiple_of(slot_ref[0, 2 * s + r] * TILE, TILE)
            sorted_ref[pl.ds(at, TILE), :128] = in_ref[s, 2 * r * TILE : (2 * r + 1) * TILE, :]
            sorted_ref[pl.ds(at, TILE), 128:] = in_ref[s, (2 * r + 1) * TILE : (2 * r + 2) * TILE, :]
        return carry

    lax.fori_loop(0, senders, move, 0, unroll=8)
    copies = []
    for d, out in enumerate((out0, out1, out2, out3)):
        part = (mp_ref[0] + d) % PARTS
        at = pl.multiple_of(part * PART_SLOTS * TILE, TILE)
        copies.append(pltpu.make_async_copy(sorted_ref.at[pl.ds(at, ROWS_W), :], out, sems.at[d]))
    for copy in copies:
        copy.start()
    for copy in copies:
        copy.wait()


def arrive_sort(mp, incoming):
    window = jax.ShapeDtypeStruct((ROWS_W, PW), jnp.bfloat16)
    return pl.pallas_call(
        arrive_kernel,
        grid_spec=pltpu.PrefetchScalarGridSpec(
            num_scalar_prefetch=1,
            grid=(1,),
            in_specs=[pl.BlockSpec(incoming.shape, lambda i, a: (0, 0, 0))],
            out_specs=[pl.BlockSpec(memory_space=pl.ANY)] * PARTS + [pl.BlockSpec((8, 128), lambda i, a: (0, 0))],
            scratch_shapes=[
                pltpu.VMEM((SLOTS * TILE + ROWS_W - PART_SLOTS * TILE, PW), jnp.bfloat16),
                pltpu.VMEM((8, 128), jnp.int32),
                pltpu.SMEM((8, 128), jnp.int32),
                pltpu.SemaphoreType.DMA((5,)),
            ],
        ),
        out_shape=[window] * PARTS + [jax.ShapeDtypeStruct((8, 128), jnp.float32)],
        compiler_params=VMEM,
        name="arrive_sort",
    )(mp, incoming)


def block_kernel(place_ref, image_ref, x0, x1, x2, x3, wq, wk, wv, wo, a0, a1, a0x, a1x, b0, b1, b0x, b1x, c0, c1, c0x, c1x,
                 out0, out1, out2, out3, sum_ref,
                 x_ref, norm_ref, q_ref, k_ref, v_ref, att_ref, w_refs, begin_ref, end_ref, xsem, wsem):
    part = place_ref[0]
    core = place_ref[1]
    x_copies = []
    for d, x in enumerate((x0, x1, x2, x3)):
        x_copies.append(pltpu.make_async_copy(x, x_ref.at[(part + PARTS - d) % PARTS], xsem.at[d]))
        x_copies[-1].start()
    copies = [[pltpu.make_async_copy(w, w_refs.at[0, n], wsem.at[n]) for n, w in enumerate((wq, wk, wv, wo))]]
    for g, (m0, m1, o0, o1) in enumerate(((a0, a1, a0x, a1x), (b0, b1, b0x, b1x), (c0, c1, c0x, c1x))):
        group = []
        for n, (w, place) in enumerate(((m0, 2 * core), (m1, 2 * core + 1), (o0, 2 - 2 * core), (o1, 3 - 2 * core))):
            group.append(pltpu.make_async_copy(w, w_refs.at[g + 1, place], wsem.at[4 * g + 4 + n]))
        copies.append(group)
    for group in copies:
        for copy in group:
            copy.start()

    window = part * PART_SLOTS
    for i in range(8):
        begin_ref[i] = 0
        end_ref[i] = 0

    def scan(l, carry):
        before, count, first, mine = carry
        t = window + l
        label = jnp.where(t < SLOTS, image_ref[jnp.minimum(t, SLOTS - 1)], -1)
        fresh = (label >= 0) & (label != before)
        starts = fresh & (l < PART_SLOTS)
        mine = jnp.where(fresh, jnp.where(starts, 1, 0), jnp.where(label >= 0, mine, 0))
        first = jnp.where(starts & (count == 0), label, first)
        count = count + jnp.where(starts, 1, 0)
        begin_ref[jnp.where(starts, count - 1, 7)] = l
        end_ref[jnp.where(mine == 1, count - 1, 7)] = l + 1
        return label, count, first, mine

    before = jnp.where(part > 0, image_ref[jnp.maximum(window - 1, 0)], -1)
    _, count, first, _ = lax.fori_loop(0, WIN, scan, (before, jnp.int32(0), jnp.int32(0), jnp.int32(0)), unroll=4)
    for copy in x_copies:
        copy.wait()

    chunk = 64

    def norm(i, carry):
        at = pl.multiple_of(i * chunk, chunk)
        rows = [x_ref[p, pl.ds(at, chunk), :].astype(jnp.float32) for p in range(PARTS)]
        mean = jnp.sum(rows[0] + rows[1] + rows[2] + rows[3], axis=-1, keepdims=True) * (1.0 / D)
        centred = [r - mean for r in rows]
        squares = [r * r for r in centred]
        spread = jnp.sum(squares[0] + squares[1] + squares[2] + squares[3], axis=-1, keepdims=True) * (1.0 / D)
        scale = lax.rsqrt(spread + EPSILON)
        for p in range(PARTS):
            norm_ref[pl.ds(at, chunk), p * PW : (p + 1) * PW] = (centred[p] * scale).astype(jnp.bfloat16)
        return carry

    lax.fori_loop(0, ROWS_W // chunk, norm, 0)
    lane = lax.broadcasted_iota(jnp.int32, (IMG_ROWS, PW), 1)
    upper = lax.broadcasted_iota(jnp.int32, (IMG_ROWS, 128), 1) + 128
    low = lax.broadcasted_iota(jnp.int32, (IMG_ROWS, 128), 1) < HD

    for g in range(PARTS):
        for copy in copies[g]:
            copy.wait()
        for n, ref in enumerate((q_ref, k_ref, v_ref)):
            ref[...] = jnp.dot(norm_ref[...], w_refs[g, n], preferred_element_type=jnp.float32).astype(jnp.bfloat16)

        def image(i, carry):
            row = pl.multiple_of(begin_ref[i] * TILE, TILE)
            limit = (end_ref[i] - begin_ref[i]) * TILE
            queries = q_ref[pl.ds(row, IMG_ROWS), :]
            keys = k_ref[pl.ds(row, IMG_ROWS), :]
            values = v_ref[pl.ds(row, IMG_ROWS), :]
            allowed = upper < limit
            nears, fars = [], []
            for h in range(PW // HD):
                inside = (lane >= h * HD) & (lane < (h + 1) * HD)
                head_keys = jnp.where(inside, keys, jnp.zeros_like(keys))
                head_values = jnp.where(inside, values, jnp.ones_like(values))
                scores = lax.dot_general(queries, head_keys, (((1,), (1,)), ((), ())), preferred_element_type=jnp.float32)
                always, maybe = scores[:, :128], jnp.where(allowed, scores[:, 128:], -1e30)
                peak = jnp.max(jnp.maximum(always, maybe), axis=-1, keepdims=True)
                raised = jnp.exp2((jnp.concatenate([always, maybe], axis=1) - peak) * EXP_SCALE).astype(jnp.bfloat16)
                mixed = jnp.dot(raised, head_values, preferred_element_type=jnp.float32)
                near, far = (mixed[:, :128], mixed[:, 128:]) if h < 2 else (mixed[:, 128:], mixed[:, :128])
                nears.append(near)
                fars.append(far)
            for half in range(2):
                top = jnp.where(low, nears[2 * half], nears[2 * half + 1])
                bottom = jnp.where(low, fars[2 * half], fars[2 * half + 1])
                att_ref[pl.ds(row, IMG_ROWS), g * PW + half * 128 : g * PW + (half + 1) * 128] = (top / bottom).astype(jnp.bfloat16)
            return carry

        lax.fori_loop(0, count, image, 0)

    start_row = begin_ref[0] * TILE
    end_row = end_ref[0]
    for i in range(1, MAX_LOCAL):
        end_row = jnp.maximum(end_row, end_ref[i])
    end_row = end_row * TILE
    row_ids = lax.broadcasted_iota(jnp.int32, (ROWS_W, PW), 0)
    live = (row_ids >= start_row) & (row_ids < end_row)
    image_ids = lax.broadcasted_iota(jnp.int32, (IMG, WIN), 0)
    tile_ids = lax.broadcasted_iota(jnp.int32, (IMG, WIN), 1)
    lengths = jnp.ones((IMG, PW), jnp.float32)
    pooled_ids = lax.broadcasted_iota(jnp.int32, (IMG, PW), 0)
    member = jnp.zeros((IMG, WIN), jnp.float32)
    for i in range(MAX_LOCAL):
        here = (image_ids == first + i) & (tile_ids >= begin_ref[i]) & (tile_ids < end_ref[i])
        member = jnp.where(here, 1.0, member)
        rows_i = ((end_ref[i] - begin_ref[i]) * TILE).astype(jnp.float32)
        lengths = jnp.where((pooled_ids == first + i) & (rows_i > 0), rows_i, lengths)
    for d, out in enumerate((out0, out1, out2, out3)):
        n = (part + d) % PARTS
        block_rows = pl.ds(pl.multiple_of(n * PW, PW), PW)
        mix = jnp.concatenate([w_refs[g, 3, block_rows, :] for g in range(PARTS)], axis=0)
        projected = jnp.dot(att_ref[...], mix, preferred_element_type=jnp.float32)
        result = jnp.where(live, x_ref[n].astype(jnp.float32) + projected, 0.0)
        out[:ROWS_W, :] = result.astype(jnp.bfloat16)
        tile_sums = jnp.sum(result.reshape(WIN, TILE, PW), axis=1)
        sums = jnp.dot(member, tile_sums, precision=lax.Precision.HIGHEST, preferred_element_type=jnp.float32)
        pooled = sums / lengths
        one = pooled.astype(jnp.bfloat16)
        rest = pooled - one.astype(jnp.float32)
        two = rest.astype(jnp.bfloat16)
        three = (rest - two.astype(jnp.float32)).astype(jnp.bfloat16)
        out[ROWS_W : ROWS_W + IMG, :] = one
        out[ROWS_W + IMG : ROWS_W + 2 * IMG, :] = two
        out[ROWS_W + 2 * IMG : ROWS_W + 3 * IMG, :] = three
        sum_ref[pl.ds(n, 1), :] = jnp.sum(pooled, axis=0, keepdims=True)


def block(place, image, xs, weights):
    outs = jax.ShapeDtypeStruct((ROWS_W + EXTRA, PW), jnp.bfloat16)
    whole = lambda i, a, b: (0, 0)
    wide = pltpu.VMEM((ROWS_W, PW), jnp.bfloat16)
    return pl.pallas_call(
        block_kernel,
        grid_spec=pltpu.PrefetchScalarGridSpec(
            num_scalar_prefetch=2,
            grid=(1,),
            in_specs=[pl.BlockSpec(memory_space=pl.ANY)] * (len(xs) + len(weights)),
            out_specs=[pl.BlockSpec((ROWS_W + EXTRA, PW), whole)] * PARTS + [pl.BlockSpec((PARTS, PW), whole)],
            scratch_shapes=[
                pltpu.VMEM((PARTS, ROWS_W, PW), jnp.bfloat16),
                pltpu.VMEM((ROWS_W, D), jnp.bfloat16),
                wide,
                wide,
                wide,
                pltpu.VMEM((ROWS_W, D), jnp.bfloat16),
                pltpu.VMEM((PARTS, 4, D, PW), jnp.bfloat16),
                pltpu.SMEM((8,), jnp.int32),
                pltpu.SMEM((8,), jnp.int32),
                pltpu.SemaphoreType.DMA((PARTS,)),
                pltpu.SemaphoreType.DMA((4 * PARTS,)),
            ],
        ),
        out_shape=[outs] * PARTS + [jax.ShapeDtypeStruct((PARTS, PW), jnp.float32)],
        compiler_params=VMEM,
        name="block",
    )(place, image, *xs, *weights)


def finish_kernel(place_ref, r0, r1, r2, r3, out_ref, pooled_ref, in_ref, out_vmem, sems, out_sems):
    size = PART_SLOTS * TILE
    halo = ROWS_W - size
    part = place_ref[0]
    copies = []
    for d, r in enumerate((r0, r1, r2, r3)):
        copies.append(pltpu.make_async_copy(r, in_ref.at[(part + PARTS - d) % PARTS], sems.at[d]))
    for copy in copies:
        copy.start()
    for copy in copies:
        copy.wait()
    writes = []
    for p in range(PARTS):
        start = in_ref[p, :halo, :]
        if p:
            start = start + in_ref[p - 1, size:ROWS_W, :]
        out_vmem[p * size : p * size + halo, :] = start
        out_vmem[p * size + halo : (p + 1) * size, :] = in_ref[p, halo:size, :]
        rows = pl.ds(p * size, size)
        writes.append(pltpu.make_async_copy(out_vmem.at[rows, :], out_ref.at[rows, :], out_sems.at[p]))
        writes[-1].start()
    pooled = jnp.zeros((IMG, PW), jnp.float32)
    for p in range(PARTS):
        for n in range(3):
            pooled = pooled + in_ref[p, ROWS_W + n * IMG : ROWS_W + (n + 1) * IMG, :].astype(jnp.float32)
    pooled_ref[...] = pooled
    for write in writes:
        write.wait()


def finish(place, received):
    return pl.pallas_call(
        finish_kernel,
        grid_spec=pltpu.PrefetchScalarGridSpec(
            num_scalar_prefetch=1,
            grid=(1,),
            in_specs=[pl.BlockSpec(memory_space=pl.ANY)] * PARTS,
            out_specs=[pl.BlockSpec(memory_space=pl.ANY), pl.BlockSpec((IMG, PW), lambda i, a: (0, 0))],
            scratch_shapes=[
                pltpu.VMEM((PARTS, ROWS_W + EXTRA, PW), jnp.bfloat16),
                pltpu.VMEM((SLOTS * TILE, PW), jnp.bfloat16),
                pltpu.SemaphoreType.DMA((PARTS,)),
                pltpu.SemaphoreType.DMA((PARTS,)),
            ],
        ),
        out_shape=[
            jax.ShapeDtypeStruct((SLOTS * TILE, PW), jnp.bfloat16),
            jax.ShapeDtypeStruct((IMG, PW), jnp.float32),
        ],
        compiler_params=VMEM,
        name="finish",
    )(place, *received)


def whole_block(patches, dest_owner, dest_slot, packed_image, w_query, w_key, w_value, w_out):
    senders = lax.axis_size("dp")
    splits = lax.axis_size("mp")
    mp = lax.axis_index("mp").astype(jnp.int32)
    core = (lax.axis_index("dp") % 2).astype(jnp.int32)
    place = jnp.stack([mp, core])
    shift = lambda d: [(i, (i + d) % splits) for i in range(splits)]
    swap = [(i, i ^ 1) for i in range(senders)]

    out_blocks = w_out.reshape(PW, PARTS, PW).transpose(1, 0, 2).reshape(D, PW)
    s0 = jnp.where(core == 0, w_query, w_value)
    s1 = jnp.where(core == 0, w_key, out_blocks)
    a0, a1 = (lax.ppermute(s, "mp", shift(1)) for s in (s0, s1))
    b0, b1 = (lax.ppermute(s, "mp", shift(-1)) for s in (s0, s1))
    c0 = lax.ppermute(a0, "mp", shift(1))
    c1 = lax.ppermute(b1, "mp", shift(-1))
    a0x, a1x, b0x, b1x, c0x, c1x = (lax.ppermute(w, "dp", swap) for w in (a0, a1, b0, b1, c0, c1))
    weights = (w_query, w_key, w_value, out_blocks, a0, a1, a0x, a1x, b0, b1, b0x, b1x, c0, c1, c0x, c1x)

    outgoing = send_pack(dest_owner, dest_slot, place[:1], packed_image.reshape(1, SLOTS), patches, senders)
    incoming = lax.all_to_all(outgoing, "dp", split_axis=0, concat_axis=0, tiled=True)
    *windows, number = arrive_sort(place[:1], incoming)
    rows = [windows[0]] + [lax.ppermute(windows[d], "mp", shift(d)) for d in (1, 2, 3)]
    *results, local_sum = block(place, packed_image, rows, weights)
    received = [results[0]] + [lax.ppermute(results[d], "mp", shift(d)) for d in (1, 2, 3)]
    spread = jnp.broadcast_to(local_sum.reshape(1, PARTS, 2, PW // 2), (senders, PARTS, 2, PW // 2))
    gathered = lax.all_to_all(
        spread.reshape(senders * PARTS, 2, PW // 2), ("dp", "mp"), split_axis=0, concat_axis=0, tiled=True
    )
    packed_out, pooled = finish(place[:1], received)
    centre = (jnp.sum(gathered, axis=0) / number[0, 0]).reshape(1, PW)
    present = jnp.any(packed_image[None, :] == jnp.arange(IMG, dtype=jnp.int32)[:, None], axis=1, keepdims=True)
    pooled_out = jnp.where(present, pooled - centre, 0.0).astype(jnp.bfloat16)
    return (packed_out, pooled_out)


def solution(mesh):
    in_specs = (
        P("dp", None),
        P("dp"),
        P("dp"),
        P("dp"),
        P(None, "mp"),
        P(None, "mp"),
        P(None, "mp"),
        P("mp", None),
    )
    out_specs = (P("dp", "mp"), P("dp", "mp"))
    return jax.shard_map(whole_block, mesh=mesh, in_specs=in_specs, out_specs=out_specs, check_vma=False)
```

time: 227 us -> 161 us (0.71)
  blocking collectives: 88.7 us -> 0 us
  starting transfers between devices: 32.2 us -> 48.7 us
  waiting for transfers between devices: 44.7 us -> 59.3 us
  local copies, waits for them, and re-layouts: 9.91 us -> 5.51 us
  other arithmetic: 7.42 us -> 3.07 us
    psum x1 -> x0, blocking collectives: 88.7 us -> none  [on_device(): total = lax.psum(local_sum, ('dp', 'mp'))]
    ppermute x8 -> x18, waiting for transfers between devices: 20.1 us -> 59.3 us  [the longest x3 18.4 us: whole_block(): lax.ppermute(results[d], 'mp', shift(d))]
    all_to_all x3 -> x2, waiting for transfers between devices: 24.6 us -> 0.01 us  [the longest x1 0.01 us: whole_block(): lax.all_to_all(outgoing, 'dp', split_axis=0, concat_axis=0, tiled=True)]
    ppermute x8 -> x18, starting transfers between devices: 11.3 us -> 25.2 us  [the longest x6 8.37 us: whole_block(): lax.ppermute(w, 'dp', swap)]
    slice x4 -> x1, local copies, waits for them, and re-layouts: 4.29 us -> 1.19 us  [whole_block(): centre = (jnp.sum(gathered, axis=0) / number[0, 0]).reshape(1, PW)]
    all_to_all x3 -> x2, starting transfers between devices: 20.9 us -> 23.5 us  [the longest x1 13.3 us: whole_block(): lax.all_to_all(outgoing, 'dp', split_axis=0, concat_axis=0, tiled=True)]
    concatenate x1 -> x0, local copies, waits for them, and re-layouts: 2.5 us -> none  [on_device(): jnp.concatenate([jnp.stack([first, count]), begin, end, jnp.stack([core,...]
    pallas_call x1, Pallas kernels: 6.36 us -> 3.97 us  [arrive_sort(): pl.pallas_call(arrive_kernel, grid_spec=pltpu.PrefetchScalarGridSpec(num_...]
  transfers between devices with their start and end apart: 11 -> 20, of which waited for: 2 -> 8; matrix products, arithmetic and copies ran while one was open for 6% -> 1% of each run, Pallas kernels for 3% -> 4%
where the time goes in v2:
time: 161 us; the launch traced here: 160 us
  waiting for transfers between devices  59.3 us (37%)
  starting transfers between devices  48.7 us (30%)
  Pallas kernels  42.9 us (27%)
  local copies, waits for them, and re-layouts  5.51 us (3%)
  other arithmetic  3.07 us (2%)
    pallas_call x1, Pallas kernels, block(): pl.pallas_call(block_kernel, grid_spec=pltpu.PrefetchScalarGridSpec(num_s...  31.7 us
    ppermute x3, waiting for transfers between devices, whole_block(): lax.ppermute(results[d], 'mp', shift(d))  18.4 us
    ppermute x3, waiting for transfers between devices, whole_block(): lax.ppermute(windows[d], 'mp', shift(d))  17.3 us
    all_to_all x1, starting transfers between devices, whole_block(): lax.all_to_all(outgoing, 'dp', split_axis=0, concat_axis=0, tiled=True)  13.3 us
    all_to_all x1, starting transfers between devices, whole_block(): lax.all_to_all(spread.reshape(senders * PARTS, 2, PW // 2), ('dp', 'mp'),...  10.3 us
    ppermute x2, waiting for transfers between devices, whole_block(): a0, a1 = (lax.ppermute(s, 'mp', shift(1)) for s in (s0, s1))  8.6 us
    ppermute x6, starting transfers between devices, whole_block(): lax.ppermute(w, 'dp', swap)  8.37 us
    ppermute x2, waiting for transfers between devices, whole_block(): b0, b1 = (lax.ppermute(s, 'mp', shift(-1)) for s in (s0, s1))  7.91 us
  transfers between devices with their start and end apart: 20, of which 8 were waited for; matrix products, arithmetic and copies ran while one was open for 1% of the time, Pallas kernels for 4%

profile of v2, /device:TPU:1, one launch (start us, length us, event | category | flops | bytes accessed | tf_op | source)
XLA Modules:
  0.0 160.4 jit_solution(13824264952093753002)
XLA Ops:
  0.6 4.2 %send_pack.1 = bf16[64,72,128]{2,1,0:T(8,128)(2,1)} custom-call(s32[128]{0:T(128)} %owner_ref.1, s32[128]{0:T(128)} %slot_ref.1, s32[1]{0:T(128)} %bitcast.mp_ref.place_ref, s32[1,128]{1,0:T(1,128)} %bitcast.18, bf16[2048,1024]{1,0:T(8,128)(2,1)} %patch_ref.1), custom_call_target="tpu_custom_call" | custom-call | tf_op jit(solution)/shard_map/send_pack/pallas_call | solution.py:61
  4.8 13.3 %all-to-all-start = ((bf16[64,72,128]{2,1,0:T(8,128)(2,1)}), bf16[64,72,128]{2,1,0:T(8,128)(2,1)S(1)}, u32[]{:S(2)}, u32[]{:S(2)}) async-start(bf16[64,72,128]{2,1,0:T(8,128)(2,1)} %send_pack.1), calls=%async_computation | async-start | bytes 2359296 | tf_op jit(solution)/shard_map/all_to_all | solution.py:376
  18.1 0.0 copy-start.2
  18.1 0.0 copy-start.4
  18.2 0.0 copy-start
  18.2 0.1 broadcast_select_fusion
  18.3 2.6 %collective-permute-start.8 = (bf16[1024,256]{1,0:T(8,128)(2,1)S(1)}, bf16[1024,256]{1,0:T(8,128)(2,1)S(1)}, u32[]{:S(2)}, u32[]{:S(2)}) collective-permute-start(bf16[1024,256]{1,0:T(8,128)(2,1)S(1)} %broadcast_select_fusion), channel_id=1, source_target_pairs={{0,3},{1,0},{2,1},{3,2},{4,7},{5,4},{6,5},{7,6},{8,11},{9,8},{10,9... | collective-permute-start | bytes 1572872 | tf_op jit(solution)/shard_map/ppermute | solution.py:369
  20.9 0.0 copy-done.2
  20.9 0.1 broadcast_select_fusion.1
  20.9 0.1 collective-permute-start.3
  21.0 1.1 collective-permute-start.4
  22.1 1.7 %collective-permute-start.7 = (bf16[1024,256]{1,0:T(8,128)(2,1)S(1)}, bf16[1024,256]{1,0:T(8,128)(2,1)S(1)}, u32[]{:S(2)}, u32[]{:S(2)}) collective-permute-start(bf16[1024,256]{1,0:T(8,128)(2,1)S(1)} %broadcast_select_fusion.1), channel_id=1, source_target_pairs={{0,3},{1,0},{2,1},{3,2},{4,7},{5,4},{6,5},{7,6},{8,11},{9,8},{10,9... | collective-permute-start | bytes 1572872 | tf_op jit(solution)/shard_map/ppermute | solution.py:369
  23.8 7.9 %collective-permute-done.8.b1 = bf16[1024,256]{1,0:T(8,128)(2,1)S(1)} collective-permute-done((bf16[1024,256]{1,0:T(8,128)(2,1)S(1)}, bf16[1024,256]{1,0:T(8,128)(2,1)S(1)}, u32[]{:S(2)}, u32[]{:S(2)}) %collective-permute-start.8) | collective-permute-done | bytes 524320 | tf_op jit(solution)/shard_map/ppermute | solution.py:369
  31.7 3.4 %collective-permute-start.12 = (bf16[1024,256]{1,0:T(8,128)(2,1)S(1)}, bf16[1024,256]{1,0:T(8,128)(2,1)}, u32[]{:S(2)}, u32[]{:S(2)}) collective-permute-start(bf16[1024,256]{1,0:T(8,128)(2,1)S(1)} %collective-permute-done.8.b1), channel_id=1, source_target_pairs={{0,3},{1,0},{2,1},{3,2},{4,7},{5,4},{6,5},{7,6},{8,11},{9,8},{10,9... | collective-permute-start | bytes 1572872 | tf_op jit(solution)/shard_map/ppermute | solution.py:371
  35.1 2.5 %collective-permute-start.10 = (bf16[1024,256]{1,0:T(8,128)(2,1)S(1)}, bf16[1024,256]{1,0:T(8,128)(2,1)S(1)}, u32[]{:S(2)}, u32[]{:S(2)}) collective-permute-start(bf16[1024,256]{1,0:T(8,128)(2,1)S(1)} %collective-permute-done.8.b1), channel_id=1, source_target_pairs={{0,4},{4,0},{8,12},{12,8},{16,20},{20,16},{24,28},{28,24},{32,36},... | collective-permute-start | bytes 1572872 | tf_op jit(solution)/shard_map/ppermute | solution.py:372
  37.6 0.0 collective-permute-done.3.a0
  37.6 0.0 collective-permute-start.11
  37.6 8.6 %collective-permute-done.4.a1 = bf16[1024,256]{1,0:T(8,128)(2,1)S(1)} collective-permute-done((bf16[1024,256]{1,0:T(8,128)(2,1)S(1)}, bf16[1024,256]{1,0:T(8,128)(2,1)S(1)}, u32[]{:S(2)}, u32[]{:S(2)}) %collective-permute-start.4) | collective-permute-done | bytes 524320 | tf_op jit(solution)/shard_map/ppermute | solution.py:368
  46.2 2.8 %collective-permute-start.6 = (bf16[1024,256]{1,0:T(8,128)(2,1)S(1)}, bf16[1024,256]{1,0:T(8,128)(2,1)}, u32[]{:S(2)}, u32[]{:S(2)}) collective-permute-start(bf16[1024,256]{1,0:T(8,128)(2,1)S(1)} %collective-permute-done.4.a1), channel_id=1, source_target_pairs={{0,4},{4,0},{8,12},{12,8},{16,20},{20,16},{24,28},{28,24},{32,36},... | collective-permute-start | bytes 1572872 | tf_op jit(solution)/shard_map/ppermute | solution.py:372
  49.0 0.0 collective-permute-done.7.b0
  49.0 0.1 collective-permute-start.9
  49.1 5.1 %collective-permute-done.12.c1 = bf16[1024,256]{1,0:T(8,128)(2,1)} collective-permute-done((bf16[1024,256]{1,0:T(8,128)(2,1)S(1)}, bf16[1024,256]{1,0:T(8,128)(2,1)}, u32[]{:S(2)}, u32[]{:S(2)}) %collective-permute-start.12) | collective-permute-done | bytes 524320 | tf_op jit(solution)/shard_map/ppermute | solution.py:371
  54.2 1.3 collective-permute-start.5
  55.5 0.0 collective-permute-done.10.b1x
  55.5 0.1 collective-permute-start.14
  55.6 2.0 %collective-permute-done.11.c0 = bf16[1024,256]{1,0:T(8,128)(2,1)} collective-permute-done((bf16[1024,256]{1,0:T(8,128)(2,1)S(1)}, bf16[1024,256]{1,0:T(8,128)(2,1)}, u32[]{:S(2)}, u32[]{:S(2)}) %collective-permute-start.11) | collective-permute-done | bytes 524320 | tf_op jit(solution)/shard_map/ppermute | solution.py:370
  57.6 1.6 collective-permute-start.13
  59.1 0.0 all-to-all-done.in_ref
  59.2 1.1 copy-done.1
  60.3 4.0 %arrive_sort.1 = (bf16[768,256]{1,0:T(8,128)(2,1)}, bf16[768,256]{1,0:T(8,128)(2,1)}, bf16[768,256]{1,0:T(8,128)(2,1)}, bf16[768,256]{1,0:T(8,128)(2,1)}, f32[8,128]{1,0:T(8,128)}) custom-call(s32[1]{0:T(128)} %bitcast.mp_ref.place_ref, bf16[64,72,128]{2,1,0:T(8,128)(2,1)} %copy-done.1), custom_call_target="tpu_custom_call" | custom-call | tf_op jit(solution)/shard_map/arrive_sort/pallas_call | solution.py:119
  64.2 0.0 collective-permute-done.6.a1x
  64.2 0.1 collective-permute-start
  64.3 0.0 collective-permute-done.9.b0x
  64.3 1.8 %collective-permute-start.1 = (bf16[768,256]{1,0:T(8,128)(2,1)}, bf16[768,256]{1,0:T(8,128)(2,1)S(1)}, u32[]{:S(2)}, u32[]{:S(2)}) collective-permute-start(bf16[768,256]{1,0:T(8,128)(2,1)} %get-tuple-element.16), channel_id=1, source_target_pairs={{0,2},{1,3},{2,0},{3,1},{4,6},{5,7},{6,4},{7,5},{8,10},{9,11},{10,... | collective-permute-start | bytes 1179656 | tf_op jit(solution)/shard_map/ppermute | solution.py:378
  66.2 0.0 collective-permute-done.5.a0x
  66.2 1.1 collective-permute-start.2
  67.3 0.6 pad_add_fusion.place_ref
  67.8 0.0 collective-permute-done.14.c1x
  67.8 0.0 collective-permute-done.13.c0x
  67.8 17.0 %collective-permute-done.x1 = bf16[768,256]{1,0:T(8,128)(2,1)S(1)} collective-permute-done((bf16[768,256]{1,0:T(8,128)(2,1)}, bf16[768,256]{1,0:T(8,128)(2,1)S(1)}, u32[]{:S(2)}, u32[]{:S(2)}) %collective-permute-start) | collective-permute-done | bytes 393248 | tf_op jit(solution)/shard_map/ppermute | solution.py:378
  84.8 0.0 collective-permute-done.1.x2
  84.8 0.3 collective-permute-done.2.x3
  85.2 0.4 copy-done.14
  85.6 0.1 copy-done.15
  85.8 0.2 copy-done.16
  85.9 31.7 %block.1 = (bf16[816,256]{1,0:T(8,128)(2,1)}, bf16[816,256]{1,0:T(8,128)(2,1)}, bf16[816,256]{1,0:T(8,128)(2,1)}, bf16[816,256]{1,0:T(8,128)(2,1)}, f32[4,256]{1,0:T(4,128)}) custom-call(s32[2]{0:T(128)} %pad_add_fusion.place_ref, s32[128]{0:T(128)} %image_ref.1, bf16[768,256]{1,0:T(8,128)(2,1)} %get-tuple-element.14.x0, bf16[768,256]{1,0:T(8,128)(2,1)} %copy-done.14, ...), custom_call_target="tpu_custom_call" | custom-call | tf_op jit(solution)/shard_map/block/pallas_call | solution.py:275
  117.7 0.7 broadcast_in_dim.23
  118.4 0.8 broadcast_in_dim.24
  119.1 10.3 %all-to-all-start.1 = ((f32[256,2,128]{2,1,0:T(2,128)}), f32[256,2,128]{2,1,0:T(2,128)S(1)}, u32[]{:S(2)}, u32[]{:S(2)}) async-start(f32[256,2,128]{2,1,0:T(2,128)} %bitcast.6), calls=%async_computation.1 | async-start | bytes 524288 | tf_op jit(solution)/shard_map/all_to_all | solution.py:382
  129.4 1.4 collective-permute-start.15
  130.8 2.4 %collective-permute-start.16 = (bf16[816,256]{1,0:T(8,128)(2,1)}, bf16[816,256]{1,0:T(8,128)(2,1)S(1)}, u32[]{:S(2)}, u32[]{:S(2)}) collective-permute-start(bf16[816,256]{1,0:T(8,128)(2,1)} %get-tuple-element.20), channel_id=1, source_target_pairs={{0,2},{1,3},{2,0},{3,1},{4,6},{5,7},{6,4},{7,5},{8,10},{9,11},{10,... | collective-permute-start | bytes 1253384 | tf_op jit(solution)/shard_map/ppermute | solution.py:380
  133.2 1.2 collective-permute-start.17
  134.4 0.1 fusion
  134.5 1.2 slice.3
  135.7 7.3 %collective-permute-done.15.r1 = bf16[816,256]{1,0:T(8,128)(2,1)S(1)} collective-permute-done((bf16[816,256]{1,0:T(8,128)(2,1)}, bf16[816,256]{1,0:T(8,128)(2,1)S(1)}, u32[]{:S(2)}, u32[]{:S(2)}) %collective-permute-start.15) | collective-permute-done | bytes 417824 | tf_op jit(solution)/shard_map/ppermute | solution.py:380
  143.0 11.2 %collective-permute-done.16.r2 = bf16[816,256]{1,0:T(8,128)(2,1)S(1)} collective-permute-done((bf16[816,256]{1,0:T(8,128)(2,1)}, bf16[816,256]{1,0:T(8,128)(2,1)S(1)}, u32[]{:S(2)}, u32[]{:S(2)}) %collective-permute-start.16) | collective-permute-done | bytes 417824 | tf_op jit(solution)/shard_map/ppermute | solution.py:380
  154.2 0.0 collective-permute-done.17.r3
  154.2 0.8 copy-done.12
  154.9 0.2 copy-done.13
  155.1 3.0 %finish.1 = (bf16[2048,256]{1,0:T(8,128)(2,1)}, f32[16,256]{1,0:T(8,128)}) custom-call(s32[1]{0:T(128)} %bitcast.mp_ref.place_ref, bf16[816,256]{1,0:T(8,128)(2,1)} %get-tuple-element.18.r0, bf16[816,256]{1,0:T(8,128)(2,1)} %copy-done.11, bf16[816,256]{1,0:T(8,128)(2,1)} %copy-done.12, bf16[816,256]{1,0:T(8,128)(2,1)} %copy-done.13), custom_call_target="tpu_custom_call" | custom-call | tf_op jit(solution)/shard_map/finish/pallas_call | solution.py:333
  158.1 0.0 all-to-all-done.1
  158.1 0.3 reduce_sum.9
  158.4 0.6 divide_bitcast_fusion
  159.0 1.4 select_convert_fusion
  (27 shorter events, 0.1 us)
Async XLA Ops:
  4.8 13.3 %copy-start.10 = (bf16[256,1024]{1,0:T(8,128)(2,1)S(1)}, bf16[256,1024]{1,0:T(8,128)(2,1)}, u32[]{:S(2)}) copy-start(bf16[256,1024]{1,0:T(8,128)(2,1)} %param.15) | copy-start | bytes 1572868
  4.8 13.4 %copy-start.3 = (bf16[1024,256]{1,0:T(8,128)(2,1)S(1)}, bf16[1024,256]{1,0:T(8,128)(2,1)}, u32[]{:S(2)}) copy-start(bf16[1024,256]{1,0:T(8,128)(2,1)} %wk.1) | copy-start | bytes 1572868
  4.8 54.3 %all-to-all-start = ((bf16[64,72,128]{2,1,0:T(8,128)(2,1)}), bf16[64,72,128]{2,1,0:T(8,128)(2,1)S(1)}, u32[]{:S(2)}, u32[]{:S(2)}) async-start(bf16[64,72,128]{2,1,0:T(8,128)(2,1)} %send_pack.1), calls=%async_computation | async-start | bytes 2359296 | tf_op jit(solution)/shard_map/all_to_all | solution.py:376
  18.1 2.7 %copy-start.2 = (bf16[1024,256]{1,0:T(8,128)(2,1)S(1)}, bf16[1024,256]{1,0:T(8,128)(2,1)}, u32[]{:S(2)}) copy-start(bf16[1024,256]{1,0:T(8,128)(2,1)} %wq.1) | copy-start | bytes 1572868
  18.1 2.7 %copy-start.4 = (bf16[1024,256]{1,0:T(8,128)(2,1)S(1)}, bf16[1024,256]{1,0:T(8,128)(2,1)}, u32[]{:S(2)}) copy-start(bf16[1024,256]{1,0:T(8,128)(2,1)} %wv.1) | copy-start | bytes 1572868
  18.2 2.7 %copy-start = (bf16[32,4,8,256]{3,2,0,1:T(8,128)(2,1)}, bf16[32,4,8,256]{3,2,0,1:T(8,128)(2,1)S(1)}, u32[]{:S(2)}) copy-start(bf16[32,4,8,256]{3,2,0,1:T(8,128)(2,1)S(1)} %copy.18) | copy-start | bytes 1572868
  18.3 13.4 %collective-permute-start.8 = (bf16[1024,256]{1,0:T(8,128)(2,1)S(1)}, bf16[1024,256]{1,0:T(8,128)(2,1)S(1)}, u32[]{:S(2)}, u32[]{:S(2)}) collective-permute-start(bf16[1024,256]{1,0:T(8,128)(2,1)S(1)} %broadcast_select_fusion), channel_id=1, source_target_pairs={{0,3},{1,0},{2,1},{3,2},{4,7},{5,4},{6,5},{7,6},{8,11},{9,8},{10,9... | collective-permute-start | bytes 1572872 | tf_op jit(solution)/shard_map/ppermute | solution.py:369
  20.9 16.7 %collective-permute-start.3 = (bf16[1024,256]{1,0:T(8,128)(2,1)S(1)}, bf16[1024,256]{1,0:T(8,128)(2,1)S(1)}, u32[]{:S(2)}, u32[]{:S(2)}) collective-permute-start(bf16[1024,256]{1,0:T(8,128)(2,1)S(1)} %broadcast_select_fusion.1), channel_id=1, source_target_pairs={{0,1},{1,2},{2,3},{3,0},{4,5},{5,6},{6,7},{7,4},{8,9},{9,10},{10,1... | collective-permute-start | bytes 1572872 | tf_op jit(solution)/shard_map/ppermute | solution.py:368
  21.0 25.2 %collective-permute-start.4 = (bf16[1024,256]{1,0:T(8,128)(2,1)S(1)}, bf16[1024,256]{1,0:T(8,128)(2,1)S(1)}, u32[]{:S(2)}, u32[]{:S(2)}) collective-permute-start(bf16[1024,256]{1,0:T(8,128)(2,1)S(1)} %broadcast_select_fusion), channel_id=1, source_target_pairs={{0,1},{1,2},{2,3},{3,0},{4,5},{5,6},{6,7},{7,4},{8,9},{9,10},{10,1... | collective-permute-start | bytes 1572872 | tf_op jit(solution)/shard_map/ppermute | solution.py:368
  22.1 26.9 %collective-permute-start.7 = (bf16[1024,256]{1,0:T(8,128)(2,1)S(1)}, bf16[1024,256]{1,0:T(8,128)(2,1)S(1)}, u32[]{:S(2)}, u32[]{:S(2)}) collective-permute-start(bf16[1024,256]{1,0:T(8,128)(2,1)S(1)} %broadcast_select_fusion.1), channel_id=1, source_target_pairs={{0,3},{1,0},{2,1},{3,2},{4,7},{5,4},{6,5},{7,6},{8,11},{9,8},{10,9... | collective-permute-start | bytes 1572872 | tf_op jit(solution)/shard_map/ppermute | solution.py:369
  31.7 53.5 %copy-start.5 = (bf16[1024,256]{1,0:T(8,128)(2,1)}, bf16[1024,256]{1,0:T(8,128)(2,1)S(1)}, u32[]{:S(2)}) copy-start(bf16[1024,256]{1,0:T(8,128)(2,1)S(1)} %collective-permute-done.8.b1) | copy-start | bytes 1572868
  31.7 22.5 %collective-permute-start.12 = (bf16[1024,256]{1,0:T(8,128)(2,1)S(1)}, bf16[1024,256]{1,0:T(8,128)(2,1)}, u32[]{:S(2)}, u32[]{:S(2)}) collective-permute-start(bf16[1024,256]{1,0:T(8,128)(2,1)S(1)} %collective-permute-done.8.b1), channel_id=1, source_target_pairs={{0,3},{1,0},{2,1},{3,2},{4,7},{5,4},{6,5},{7,6},{8,11},{9,8},{10,9... | collective-permute-start | bytes 1572872 | tf_op jit(solution)/shard_map/ppermute | solution.py:371
  35.1 20.4 %collective-permute-start.10 = (bf16[1024,256]{1,0:T(8,128)(2,1)S(1)}, bf16[1024,256]{1,0:T(8,128)(2,1)S(1)}, u32[]{:S(2)}, u32[]{:S(2)}) collective-permute-start(bf16[1024,256]{1,0:T(8,128)(2,1)S(1)} %collective-permute-done.8.b1), channel_id=1, source_target_pairs={{0,4},{4,0},{8,12},{12,8},{16,20},{20,16},{24,28},{28,24},{32,36},... | collective-permute-start | bytes 1572872 | tf_op jit(solution)/shard_map/ppermute | solution.py:372
  37.6 47.6 %copy-start.6 = (bf16[1024,256]{1,0:T(8,128)(2,1)}, bf16[1024,256]{1,0:T(8,128)(2,1)S(1)}, u32[]{:S(2)}) copy-start(bf16[1024,256]{1,0:T(8,128)(2,1)S(1)} %collective-permute-done.3.a0) | copy-start | bytes 1572868
  37.6 19.9 %collective-permute-start.11 = (bf16[1024,256]{1,0:T(8,128)(2,1)S(1)}, bf16[1024,256]{1,0:T(8,128)(2,1)}, u32[]{:S(2)}, u32[]{:S(2)}) collective-permute-start(bf16[1024,256]{1,0:T(8,128)(2,1)S(1)} %collective-permute-done.3.a0), channel_id=1, source_target_pairs={{0,1},{1,2},{2,3},{3,0},{4,5},{5,6},{6,7},{7,4},{8,9},{9,10},{10,1... | collective-permute-start | bytes 1572872 | tf_op jit(solution)/shard_map/ppermute | solution.py:370
  46.2 39.0 %copy-start.7 = (bf16[1024,256]{1,0:T(8,128)(2,1)}, bf16[1024,256]{1,0:T(8,128)(2,1)S(1)}, u32[]{:S(2)}) copy-start(bf16[1024,256]{1,0:T(8,128)(2,1)S(1)} %collective-permute-done.4.a1) | copy-start | bytes 1572868
  46.2 18.0 %collective-permute-start.6 = (bf16[1024,256]{1,0:T(8,128)(2,1)S(1)}, bf16[1024,256]{1,0:T(8,128)(2,1)}, u32[]{:S(2)}, u32[]{:S(2)}) collective-permute-start(bf16[1024,256]{1,0:T(8,128)(2,1)S(1)} %collective-permute-done.4.a1), channel_id=1, source_target_pairs={{0,4},{4,0},{8,12},{12,8},{16,20},{20,16},{24,28},{28,24},{32,36},... | collective-permute-start | bytes 1572872 | tf_op jit(solution)/shard_map/ppermute | solution.py:372
  49.0 36.2 %copy-start.8 = (bf16[1024,256]{1,0:T(8,128)(2,1)}, bf16[1024,256]{1,0:T(8,128)(2,1)S(1)}, u32[]{:S(2)}) copy-start(bf16[1024,256]{1,0:T(8,128)(2,1)S(1)} %collective-permute-done.7.b0) | copy-start | bytes 1572868
  49.0 15.3 %collective-permute-start.9 = (bf16[1024,256]{1,0:T(8,128)(2,1)S(1)}, bf16[1024,256]{1,0:T(8,128)(2,1)}, u32[]{:S(2)}, u32[]{:S(2)}) collective-permute-start(bf16[1024,256]{1,0:T(8,128)(2,1)S(1)} %collective-permute-done.7.b0), channel_id=1, source_target_pairs={{0,4},{4,0},{8,12},{12,8},{16,20},{20,16},{24,28},{28,24},{32,36},... | collective-permute-start | bytes 1572872 | tf_op jit(solution)/shard_map/ppermute | solution.py:372
  54.2 12.0 %collective-permute-start.5 = (bf16[1024,256]{1,0:T(8,128)(2,1)S(1)}, bf16[1024,256]{1,0:T(8,128)(2,1)}, u32[]{:S(2)}, u32[]{:S(2)}) collective-permute-start(bf16[1024,256]{1,0:T(8,128)(2,1)S(1)} %collective-permute-done.3.a0), channel_id=1, source_target_pairs={{0,4},{4,0},{8,12},{12,8},{16,20},{20,16},{24,28},{28,24},{32,36},... | collective-permute-start | bytes 1572872 | tf_op jit(solution)/shard_map/ppermute | solution.py:372
  55.5 2.1 %copy-start.9 = (bf16[1024,256]{1,0:T(8,128)(2,1)}, bf16[1024,256]{1,0:T(8,128)(2,1)S(1)}, u32[]{:S(2)}) copy-start(bf16[1024,256]{1,0:T(8,128)(2,1)S(1)} %collective-permute-done.10.b1x) | copy-start | bytes 1572868
  55.5 12.4 %collective-permute-start.14 = (bf16[1024,256]{1,0:T(8,128)(2,1)}, bf16[1024,256]{1,0:T(8,128)(2,1)}, u32[]{:S(2)}, u32[]{:S(2)}) collective-permute-start(bf16[1024,256]{1,0:T(8,128)(2,1)} %collective-permute-done.12.c1), channel_id=1, source_target_pairs={{0,4},{4,0},{8,12},{12,8},{16,20},{20,16},{24,28},{28,24},{32,36},... | collective-permute-start | bytes 1572872 | tf_op jit(solution)/shard_map/ppermute | solution.py:372
  57.6 10.3 %collective-permute-start.13 = (bf16[1024,256]{1,0:T(8,128)(2,1)}, bf16[1024,256]{1,0:T(8,128)(2,1)}, u32[]{:S(2)}, u32[]{:S(2)}) collective-permute-start(bf16[1024,256]{1,0:T(8,128)(2,1)} %collective-permute-done.11.c0), channel_id=1, source_target_pairs={{0,4},{4,0},{8,12},{12,8},{16,20},{20,16},{24,28},{28,24},{32,36},... | collective-permute-start | bytes 1572872 | tf_op jit(solution)/shard_map/ppermute | solution.py:372
  59.2 1.1 copy-start.1
  64.2 20.6 %collective-permute-start = (bf16[768,256]{1,0:T(8,128)(2,1)}, bf16[768,256]{1,0:T(8,128)(2,1)S(1)}, u32[]{:S(2)}, u32[]{:S(2)}) collective-permute-start(bf16[768,256]{1,0:T(8,128)(2,1)} %get-tuple-element.15), channel_id=1, source_target_pairs={{0,1},{1,2},{2,3},{3,0},{4,5},{5,6},{6,7},{7,4},{8,9},{9,10},{10,1... | collective-permute-start | bytes 1179656 | tf_op jit(solution)/shard_map/ppermute | solution.py:378
  64.3 20.5 %collective-permute-start.1 = (bf16[768,256]{1,0:T(8,128)(2,1)}, bf16[768,256]{1,0:T(8,128)(2,1)S(1)}, u32[]{:S(2)}, u32[]{:S(2)}) collective-permute-start(bf16[768,256]{1,0:T(8,128)(2,1)} %get-tuple-element.16), channel_id=1, source_target_pairs={{0,2},{1,3},{2,0},{3,1},{4,6},{5,7},{6,4},{7,5},{8,10},{9,11},{10,... | collective-permute-start | bytes 1179656 | tf_op jit(solution)/shard_map/ppermute | solution.py:378
  66.2 19.0 %collective-permute-start.2 = (bf16[768,256]{1,0:T(8,128)(2,1)}, bf16[768,256]{1,0:T(8,128)(2,1)S(1)}, u32[]{:S(2)}, u32[]{:S(2)}) collective-permute-start(bf16[768,256]{1,0:T(8,128)(2,1)} %get-tuple-element.17), channel_id=1, source_target_pairs={{0,3},{1,0},{2,1},{3,2},{4,7},{5,4},{6,5},{7,6},{8,11},{9,8},{10,9... | collective-permute-start | bytes 1179656 | tf_op jit(solution)/shard_map/ppermute | solution.py:378
  84.8 0.8 copy-start.14
  84.8 0.9 copy-start.15
  85.2 0.8 copy-start.16
  85.9 48.5 %copy-start.17 = (s32[128]{0:T(128)S(1)}, s32[128]{0:T(128)}, u32[]{:S(2)}) copy-start(s32[128]{0:T(128)} %image_ref.1) | copy-start | bytes 1540
  119.1 39.0 %all-to-all-start.1 = ((f32[256,2,128]{2,1,0:T(2,128)}), f32[256,2,128]{2,1,0:T(2,128)S(1)}, u32[]{:S(2)}, u32[]{:S(2)}) async-start(f32[256,2,128]{2,1,0:T(2,128)} %bitcast.6), calls=%async_computation.1 | async-start | bytes 524288 | tf_op jit(solution)/shard_map/all_to_all | solution.py:382
  129.4 13.6 %collective-permute-start.15 = (bf16[816,256]{1,0:T(8,128)(2,1)}, bf16[816,256]{1,0:T(8,128)(2,1)S(1)}, u32[]{:S(2)}, u32[]{:S(2)}) collective-permute-start(bf16[816,256]{1,0:T(8,128)(2,1)} %get-tuple-element.19), channel_id=1, source_target_pairs={{0,1},{1,2},{2,3},{3,0},{4,5},{5,6},{6,7},{7,4},{8,9},{9,10},{10,1... | collective-permute-start | bytes 1253384 | tf_op jit(solution)/shard_map/ppermute | solution.py:380
  130.8 23.3 %collective-permute-start.16 = (bf16[816,256]{1,0:T(8,128)(2,1)}, bf16[816,256]{1,0:T(8,128)(2,1)S(1)}, u32[]{:S(2)}, u32[]{:S(2)}) collective-permute-start(bf16[816,256]{1,0:T(8,128)(2,1)} %get-tuple-element.20), channel_id=1, source_target_pairs={{0,2},{1,3},{2,0},{3,1},{4,6},{5,7},{6,4},{7,5},{8,10},{9,11},{10,... | collective-permute-start | bytes 1253384 | tf_op jit(solution)/shard_map/ppermute | solution.py:380
  133.2 20.9 %collective-permute-start.17 = (bf16[816,256]{1,0:T(8,128)(2,1)}, bf16[816,256]{1,0:T(8,128)(2,1)S(1)}, u32[]{:S(2)}, u32[]{:S(2)}) collective-permute-start(bf16[816,256]{1,0:T(8,128)(2,1)} %get-tuple-element.21), channel_id=1, source_target_pairs={{0,3},{1,0},{2,1},{3,2},{4,7},{5,4},{6,5},{7,6},{8,11},{9,8},{10,9... | collective-permute-start | bytes 1253384 | tf_op jit(solution)/shard_map/ppermute | solution.py:380
  143.0 11.2 %copy-start.11 = (bf16[816,256]{1,0:T(8,128)(2,1)}, bf16[816,256]{1,0:T(8,128)(2,1)S(1)}, u32[]{:S(2)}) copy-start(bf16[816,256]{1,0:T(8,128)(2,1)S(1)} %collective-permute-done.15.r1) | copy-start | bytes 1253380
  154.2 0.8 copy-start.12
  154.2 0.9 copy-start.13

commit v3 on v2

--- a/solution.py
+++ b/solution.py
@@ -24,8 +24,24 @@
 VMEM = pltpu.CompilerParams(vmem_limit_bytes=56 * 1024 * 1024)
 
 
-def send_kernel(owner_ref, slot_ref, mp_ref, image_ref, patch_ref, out_ref, count_ref, place_ref):
+def send_kernel(owner_ref, slot_ref, mp_ref, image_ref, patch_ref, wq, wk, wv, wo, out_ref, s0, s1, count_ref, place_ref, sems):
     owners = out_ref.shape[0]
+    core = mp_ref[1]
+    even = [pltpu.make_async_copy(wq, s0, sems.at[0]), pltpu.make_async_copy(wk, s1, sems.at[1])]
+    odd = [pltpu.make_async_copy(wv, s0, sems.at[0])]
+    for n in range(PARTS):
+        block_rows = pl.ds(n * PW, PW)
+        odd.append(pltpu.make_async_copy(wo.at[:, block_rows], s1.at[block_rows, :], sems.at[1 + n]))
+
+    @pl.when(core == 0)
+    def _():
+        for copy in even:
+            copy.start()
+
+    @pl.when(core != 0)
+    def _():
+        for copy in odd:
+            copy.start()
 
     def clear(o, carry):
         count_ref[o] = 0
@@ -56,8 +72,18 @@
 
     lax.fori_loop(0, owners, label, 0, unroll=8)
 
-
-def send_pack(owner, slot, mp, image, patches, senders):
+    @pl.when(core == 0)
+    def _():
+        for copy in even:
+            copy.wait()
+
+    @pl.when(core != 0)
+    def _():
+        for copy in odd:
+            copy.wait()
+
+
+def send_pack(owner, slot, place, image, patches, weights, senders):
     return pl.pallas_call(
         send_kernel,
         grid_spec=pltpu.PrefetchScalarGridSpec(
@@ -66,14 +92,21 @@
             in_specs=[
                 pl.BlockSpec((1, SLOTS), lambda i, a, b, m: (0, 0)),
                 pl.BlockSpec((SLOTS * TILE, PW), lambda i, a, b, m: (0, m[0])),
+            ]
+            + [pl.BlockSpec(memory_space=pl.ANY)] * 4,
+            out_specs=[pl.BlockSpec((senders, PAY, 128), lambda i, a, b, m: (0, 0, 0))]
+            + [pl.BlockSpec(memory_space=pl.ANY)] * 2,
+            scratch_shapes=[
+                pltpu.SMEM((senders,), jnp.int32),
+                pltpu.SMEM((2 * senders,), jnp.int32),
+                pltpu.SemaphoreType.DMA((1 + PARTS,)),
             ],
-            out_specs=pl.BlockSpec((senders, PAY, 128), lambda i, a, b, m: (0, 0, 0)),
-            scratch_shapes=[pltpu.SMEM((senders,), jnp.int32), pltpu.SMEM((2 * senders,), jnp.int32)],
         ),
-        out_shape=jax.ShapeDtypeStruct((senders, PAY, 128), jnp.bfloat16),
+        out_shape=[jax.ShapeDtypeStruct((senders, PAY, 128), jnp.bfloat16)]
+        + [jax.ShapeDtypeStruct((D, PW), jnp.bfloat16)] * 2,
         compiler_params=VMEM,
         name="send_pack",
-    )(owner, slot, mp, image, patches)
+    )(owner, slot, place, image, patches, *weights)
 
 
 def arrive_kernel(mp_ref, in_ref, out0, out1, out2, out3, total_ref, sorted_ref, label_ref, slot_ref, sems):
@@ -137,7 +170,7 @@
 
 
 def block_kernel(place_ref, image_ref, x0, x1, x2, x3, wq, wk, wv, wo, a0, a1, a0x, a1x, b0, b1, b0x, b1x, c0, c1, c0x, c1x,
-                 out0, out1, out2, out3, sum_ref,
+                 out0, out1, out2, out3, sum0, sum1, sum2, sum3,
                  x_ref, norm_ref, q_ref, k_ref, v_ref, att_ref, w_refs, begin_ref, end_ref, xsem, wsem):
     part = place_ref[0]
     core = place_ref[1]
@@ -145,11 +178,14 @@
     for d, x in enumerate((x0, x1, x2, x3)):
         x_copies.append(pltpu.make_async_copy(x, x_ref.at[(part + PARTS - d) % PARTS], xsem.at[d]))
         x_copies[-1].start()
-    copies = [[pltpu.make_async_copy(w, w_refs.at[0, n], wsem.at[n]) for n, w in enumerate((wq, wk, wv, wo))]]
+    copies = [[pltpu.make_async_copy(w, w_refs.at[0, n], wsem.at[n]) for n, w in enumerate((wq, wk, wv))]]
+    for n in range(PARTS):
+        block_rows = pl.ds(n * PW, PW)
+        copies[0].append(pltpu.make_async_copy(wo.at[:, block_rows], w_refs.at[0, 3, block_rows, :], wsem.at[4 * PARTS - 1 + n]))
     for g, (m0, m1, o0, o1) in enumerate(((a0, a1, a0x, a1x), (b0, b1, b0x, b1x), (c0, c1, c0x, c1x))):
         group = []
         for n, (w, place) in enumerate(((m0, 2 * core), (m1, 2 * core + 1), (o0, 2 - 2 * core), (o1, 3 - 2 * core))):
-            group.append(pltpu.make_async_copy(w, w_refs.at[g + 1, place], wsem.at[4 * g + 4 + n]))
+            group.append(pltpu.make_async_copy(w, w_refs.at[g + 1, place], wsem.at[4 * g + 3 + n]))
         copies.append(group)
     for group in copies:
         for copy in group:
@@ -178,7 +214,7 @@
     for copy in x_copies:
         copy.wait()
 
-    chunk = 64
+    chunk = 128
 
     def norm(i, carry):
         at = pl.multiple_of(i * chunk, chunk)
@@ -206,27 +242,45 @@
         def image(i, carry):
             row = pl.multiple_of(begin_ref[i] * TILE, TILE)
             limit = (end_ref[i] - begin_ref[i]) * TILE
-            queries = q_ref[pl.ds(row, IMG_ROWS), :]
-            keys = k_ref[pl.ds(row, IMG_ROWS), :]
-            values = v_ref[pl.ds(row, IMG_ROWS), :]
-            allowed = upper < limit
-            nears, fars = [], []
-            for h in range(PW // HD):
-                inside = (lane >= h * HD) & (lane < (h + 1) * HD)
-                head_keys = jnp.where(inside, keys, jnp.zeros_like(keys))
-                head_values = jnp.where(inside, values, jnp.ones_like(values))
-                scores = lax.dot_general(queries, head_keys, (((1,), (1,)), ((), ())), preferred_element_type=jnp.float32)
-                always, maybe = scores[:, :128], jnp.where(allowed, scores[:, 128:], -1e30)
-                peak = jnp.max(jnp.maximum(always, maybe), axis=-1, keepdims=True)
-                raised = jnp.exp2((jnp.concatenate([always, maybe], axis=1) - peak) * EXP_SCALE).astype(jnp.bfloat16)
-                mixed = jnp.dot(raised, head_values, preferred_element_type=jnp.float32)
-                near, far = (mixed[:, :128], mixed[:, 128:]) if h < 2 else (mixed[:, 128:], mixed[:, :128])
-                nears.append(near)
-                fars.append(far)
-            for half in range(2):
-                top = jnp.where(low, nears[2 * half], nears[2 * half + 1])
-                bottom = jnp.where(low, fars[2 * half], fars[2 * half + 1])
-                att_ref[pl.ds(row, IMG_ROWS), g * PW + half * 128 : g * PW + (half + 1) * 128] = (top / bottom).astype(jnp.bfloat16)
+
+            def mix(size):
+                window = pl.ds(row, size)
+                queries = q_ref[window, :]
+                keys = k_ref[window, :]
+                values = v_ref[window, :]
+                allowed = lax.broadcasted_iota(jnp.int32, (size, size - 128), 1) + 128 < limit
+                lane = lax.broadcasted_iota(jnp.int32, (size, PW), 1)
+                low = lax.broadcasted_iota(jnp.int32, (size, 128), 1) < HD
+                heads = range(PW // HD)
+                inside = [(lane >= h * HD) & (lane < (h + 1) * HD) for h in heads]
+                nears, fars = [], []
+                scores = [
+                    lax.dot_general(queries, jnp.where(inside[h], keys, jnp.zeros_like(keys)), (((1,), (1,)), ((), ())), preferred_element_type=jnp.float32)
+                    for h in heads
+                ]
+                raised = []
+                for h in heads:
+                    always, maybe = scores[h][:, :128], jnp.where(allowed, scores[h][:, 128:], -1e30)
+                    peak = jnp.maximum(jnp.max(always, axis=-1, keepdims=True), jnp.max(maybe, axis=-1, keepdims=True))
+                    raised.append(jnp.exp2((jnp.concatenate([always, maybe], axis=1) - peak) * EXP_SCALE).astype(jnp.bfloat16))
+                for h in heads:
+                    mixed = jnp.dot(raised[h], jnp.where(inside[h], values, jnp.ones_like(values)), preferred_element_type=jnp.float32)
+                    near, far = (mixed[:, :128], mixed[:, 128:]) if h < 2 else (mixed[:, 128:], mixed[:, :128])
+                    nears.append(near)
+                    fars.append(far)
+                for half in range(2):
+                    top = jnp.where(low, nears[2 * half], nears[2 * half + 1])
+                    bottom = jnp.where(low, fars[2 * half], fars[2 * half + 1])
+                    att_ref[window, g * PW + half * 128 : g * PW + (half + 1) * 128] = (top / bottom).astype(jnp.bfloat16)
+
+            @pl.when(limit <= 192)
+            def _():
+                mix(192)
+
+            @pl.when(limit > 192)
+            def _():
+                mix(256)
+
             return carry
 
         lax.fori_loop(0, count, image, 0)
@@ -238,25 +292,27 @@
     end_row = end_row * TILE
     row_ids = lax.broadcasted_iota(jnp.int32, (ROWS_W, PW), 0)
     live = (row_ids >= start_row) & (row_ids < end_row)
-    image_ids = lax.broadcasted_iota(jnp.int32, (IMG, WIN), 0)
-    tile_ids = lax.broadcasted_iota(jnp.int32, (IMG, WIN), 1)
+    tile_ids = lax.broadcasted_iota(jnp.int32, (WIN, 8, PW), 0)
+    pooled_ids = lax.broadcasted_iota(jnp.int32, (IMG, PW), 0)
     lengths = jnp.ones((IMG, PW), jnp.float32)
-    pooled_ids = lax.broadcasted_iota(jnp.int32, (IMG, PW), 0)
-    member = jnp.zeros((IMG, WIN), jnp.float32)
+    tiles = []
     for i in range(MAX_LOCAL):
-        here = (image_ids == first + i) & (tile_ids >= begin_ref[i]) & (tile_ids < end_ref[i])
-        member = jnp.where(here, 1.0, member)
+        tiles.append((tile_ids >= begin_ref[i]) & (tile_ids < end_ref[i]))
         rows_i = ((end_ref[i] - begin_ref[i]) * TILE).astype(jnp.float32)
         lengths = jnp.where((pooled_ids == first + i) & (rows_i > 0), rows_i, lengths)
-    for d, out in enumerate((out0, out1, out2, out3)):
+    for d, (out, sum_ref) in enumerate(((out0, sum0), (out1, sum1), (out2, sum2), (out3, sum3))):
         n = (part + d) % PARTS
         block_rows = pl.ds(pl.multiple_of(n * PW, PW), PW)
         mix = jnp.concatenate([w_refs[g, 3, block_rows, :] for g in range(PARTS)], axis=0)
         projected = jnp.dot(att_ref[...], mix, preferred_element_type=jnp.float32)
         result = jnp.where(live, x_ref[n].astype(jnp.float32) + projected, 0.0)
         out[:ROWS_W, :] = result.astype(jnp.bfloat16)
-        tile_sums = jnp.sum(result.reshape(WIN, TILE, PW), axis=1)
-        sums = jnp.dot(member, tile_sums, precision=lax.Precision.HIGHEST, preferred_element_type=jnp.float32)
+        pairs = result.reshape(WIN, 2, 8, PW)
+        pairs = pairs[:, 0] + pairs[:, 1]
+        sums = jnp.zeros((IMG, PW), jnp.float32)
+        for i in range(MAX_LOCAL):
+            held = jnp.sum(jnp.where(tiles[i], pairs, 0.0), axis=0)
+            sums = jnp.where(pooled_ids == first + i, jnp.sum(held, axis=0, keepdims=True), sums)
         pooled = sums / lengths
         one = pooled.astype(jnp.bfloat16)
         rest = pooled - one.astype(jnp.float32)
@@ -265,7 +321,7 @@
         out[ROWS_W : ROWS_W + IMG, :] = one
         out[ROWS_W + IMG : ROWS_W + 2 * IMG, :] = two
         out[ROWS_W + 2 * IMG : ROWS_W + 3 * IMG, :] = three
-        sum_ref[pl.ds(n, 1), :] = jnp.sum(pooled, axis=0, keepdims=True)
+        sum_ref[...] = jnp.sum(pooled, axis=0, keepdims=True)
 
 
 def block(place, image, xs, weights):
@@ -278,7 +334,7 @@
             num_scalar_prefetch=2,
             grid=(1,),
             in_specs=[pl.BlockSpec(memory_space=pl.ANY)] * (len(xs) + len(weights)),
-            out_specs=[pl.BlockSpec((ROWS_W + EXTRA, PW), whole)] * PARTS + [pl.BlockSpec((PARTS, PW), whole)],
+            out_specs=[pl.BlockSpec((ROWS_W + EXTRA, PW), whole)] * PARTS + [pl.BlockSpec((1, PW), whole)] * PARTS,
             scratch_shapes=[
                 pltpu.VMEM((PARTS, ROWS_W, PW), jnp.bfloat16),
                 pltpu.VMEM((ROWS_W, D), jnp.bfloat16),
@@ -290,10 +346,10 @@
                 pltpu.SMEM((8,), jnp.int32),
                 pltpu.SMEM((8,), jnp.int32),
                 pltpu.SemaphoreType.DMA((PARTS,)),
-                pltpu.SemaphoreType.DMA((4 * PARTS,)),
+                pltpu.SemaphoreType.DMA((5 * PARTS - 1,)),
             ],
         ),
-        out_shape=[outs] * PARTS + [jax.ShapeDtypeStruct((PARTS, PW), jnp.float32)],
+        out_shape=[outs] * PARTS + [jax.ShapeDtypeStruct((1, PW), jnp.float32)] * PARTS,
         compiler_params=VMEM,
         name="block",
     )(place, image, *xs, *weights)
@@ -353,6 +409,22 @@
     )(place, *received)
 
 
+def pool_kernel(sums_ref, number_ref, pooled_ref, image_ref, out_ref):
+    total = jnp.sum(sums_ref[...], axis=0)
+    centre = jnp.concatenate([total[0:1], total[1:2]], axis=1) / number_ref[0:1, 0:1]
+    slots = lax.broadcasted_iota(jnp.int32, (IMG, SLOTS), 0) == image_ref[...]
+    present = jnp.max(jnp.where(slots, 1.0, 0.0), axis=1, keepdims=True) > 0.5
+    out_ref[...] = jnp.where(present, pooled_ref[...] - centre, 0.0).astype(jnp.bfloat16)
+
+
+def pool(sums, number, pooled, image):
+    return pl.pallas_call(
+        pool_kernel,
+        out_shape=jax.ShapeDtypeStruct((IMG, PW), jnp.bfloat16),
+        name="pool",
+    )(sums, number, pooled, image)
+
+
 def whole_block(patches, dest_owner, dest_slot, packed_image, w_query, w_key, w_value, w_out):
     senders = lax.axis_size("dp")
     splits = lax.axis_size("mp")
@@ -362,30 +434,27 @@
     shift = lambda d: [(i, (i + d) % splits) for i in range(splits)]
     swap = [(i, i ^ 1) for i in range(senders)]
 
-    out_blocks = w_out.reshape(PW, PARTS, PW).transpose(1, 0, 2).reshape(D, PW)
-    s0 = jnp.where(core == 0, w_query, w_value)
-    s1 = jnp.where(core == 0, w_key, out_blocks)
+    own = (w_query, w_key, w_value, w_out)
+    image = packed_image.reshape(1, SLOTS)
+    outgoing, s0, s1 = send_pack(dest_owner, dest_slot, place, image, patches, own, senders)
     a0, a1 = (lax.ppermute(s, "mp", shift(1)) for s in (s0, s1))
     b0, b1 = (lax.ppermute(s, "mp", shift(-1)) for s in (s0, s1))
     c0 = lax.ppermute(a0, "mp", shift(1))
     c1 = lax.ppermute(b1, "mp", shift(-1))
     a0x, a1x, b0x, b1x, c0x, c1x = (lax.ppermute(w, "dp", swap) for w in (a0, a1, b0, b1, c0, c1))
-    weights = (w_query, w_key, w_value, out_blocks, a0, a1, a0x, a1x, b0, b1, b0x, b1x, c0, c1, c0x, c1x)
-
-    outgoing = send_pack(dest_owner, dest_slot, place[:1], packed_image.reshape(1, SLOTS), patches, senders)
+    weights = own + (a0, a1, a0x, a1x, b0, b1, b0x, b1x, c0, c1, c0x, c1x)
+
     incoming = lax.all_to_all(outgoing, "dp", split_axis=0, concat_axis=0, tiled=True)
     *windows, number = arrive_sort(place[:1], incoming)
     rows = [windows[0]] + [lax.ppermute(windows[d], "mp", shift(d)) for d in (1, 2, 3)]
-    *results, local_sum = block(place, packed_image, rows, weights)
+    outcome = block(place, packed_image, rows, weights)
+    results, sums = outcome[:PARTS], outcome[PARTS:]
+    total = sums[0] + sum(lax.ppermute(sums[d], "mp", shift(d)) for d in (1, 2, 3))
     received = [results[0]] + [lax.ppermute(results[d], "mp", shift(d)) for d in (1, 2, 3)]
-    spread = jnp.broadcast_to(local_sum.reshape(1, PARTS, 2, PW // 2), (senders, PARTS, 2, PW // 2))
-    gathered = lax.all_to_all(
-        spread.reshape(senders * PARTS, 2, PW // 2), ("dp", "mp"), split_axis=0, concat_axis=0, tiled=True
-    )
+    spread = jnp.broadcast_to(total.reshape(1, 2, PW // 2), (senders, 2, PW // 2))
+    gathered = lax.all_to_all(spread, "dp", split_axis=0, concat_axis=0, tiled=True)
     packed_out, pooled = finish(place[:1], received)
-    centre = (jnp.sum(gathered, axis=0) / number[0, 0]).reshape(1, PW)
-    present = jnp.any(packed_image[None, :] == jnp.arange(IMG, dtype=jnp.int32)[:, None], axis=1, keepdims=True)
-    pooled_out = jnp.where(present, pooled - centre, 0.0).astype(jnp.bfloat16)
+    pooled_out = pool(gathered, number, pooled, image)
     return (packed_out, pooled_out)
 
 

time: 161 us -> 192 us (1.19)
  Pallas kernels: 42.9 us -> 69.2 us
  waiting for transfers between devices: 59.3 us -> 68.7 us
    pallas_call x1, Pallas kernels: 4.18 us -> 35.8 us  [send_pack(): pl.pallas_call(send_kernel, grid_spec=pltpu.PrefetchScalarGridSpec(num_sc...]
    ppermute x0 -> x3, waiting for transfers between devices: none -> 19 us  [whole_block(): lax.ppermute(sums[d], 'mp', shift(d))]
    ppermute x3, waiting for transfers between devices: 18.4 us -> 0.01 us  [whole_block(): lax.ppermute(results[d], 'mp', shift(d))]
    ppermute x2, waiting for transfers between devices: 7.91 us -> 16.6 us  [whole_block(): b0, b1 = (lax.ppermute(s, 'mp', shift(-1)) for s in (s0, s1))]
    ppermute x2, waiting for transfers between devices: 8.6 us -> 0.8 us  [whole_block(): a0, a1 = (lax.ppermute(s, 'mp', shift(1)) for s in (s0, s1))]
    pallas_call x1, Pallas kernels: 31.7 us -> 24.8 us  [block(): pl.pallas_call(block_kernel, grid_spec=pltpu.PrefetchScalarGridSpec(num_s...]
    ppermute x1, waiting for transfers between devices: 1.99 us -> 8.45 us  [whole_block(): c0 = lax.ppermute(a0, 'mp', shift(1))]
    all_to_all x1, waiting for transfers between devices: 0.01 us -> 5.95 us  [whole_block(): lax.all_to_all(spread, 'dp', split_axis=0, concat_axis=0, tiled=True)]
  transfers between devices with their start and end apart: 20 -> 23, of which waited for: 8 -> 9; matrix products, arithmetic and copies ran while one was open for 1% -> 1% of each run, Pallas kernels for 4% -> 4%
where the time goes in v3:
time: 192 us
  Pallas kernels  69.2 us (36%)
  waiting for transfers between devices  68.7 us (36%)
  starting transfers between devices  47.7 us (25%)
  local copies, waits for them, and re-layouts  4.36 us (2%)
    pallas_call x1, Pallas kernels, send_pack(): pl.pallas_call(send_kernel, grid_spec=pltpu.PrefetchScalarGridSpec(num_sc...  35.8 us
    pallas_call x1, Pallas kernels, block(): pl.pallas_call(block_kernel, grid_spec=pltpu.PrefetchScalarGridSpec(num_s...  24.8 us
    ppermute x3, waiting for transfers between devices, whole_block(): lax.ppermute(sums[d], 'mp', shift(d))  19 us
    ppermute x3, waiting for transfers between devices, whole_block(): lax.ppermute(windows[d], 'mp', shift(d))  17.8 us
    ppermute x2, waiting for transfers between devices, whole_block(): b0, b1 = (lax.ppermute(s, 'mp', shift(-1)) for s in (s0, s1))  16.6 us
    all_to_all x1, starting transfers between devices, whole_block(): lax.all_to_all(outgoing, 'dp', split_axis=0, concat_axis=0, tiled=True)  13.2 us
    all_to_all x1, starting transfers between devices, whole_block(): lax.all_to_all(spread, 'dp', split_axis=0, concat_axis=0, tiled=True)  10.1 us
    ppermute x1, waiting for transfers between devices, whole_block(): c0 = lax.ppermute(a0, 'mp', shift(1))  8.45 us
  transfers between devices with their start and end apart: 23, of which 9 were waited for; matrix products, arithmetic and copies ran while one was open for 1% of the time, Pallas kernels for 4%

profile of v3, /device:TPU:1, one launch (start us, length us, event | category | flops | bytes accessed | tf_op | source)
XLA Modules:
  0.0 192.1 jit_solution(2424150650713949821)
XLA Ops:
  0.6 0.6 pad_add_fusion.mp_ref.place_ref
  1.3 35.8 %send_pack.1 = (bf16[64,72,128]{2,1,0:T(8,128)(2,1)}, bf16[1024,256]{1,0:T(8,128)(2,1)}, bf16[1024,256]{1,0:T(8,128)(2,1)}) custom-call(s32[128]{0:T(128)} %owner_ref.1, s32[128]{0:T(128)} %slot_ref.1, s32[2]{0:T(128)} %pad_add_fusion.mp_ref.place_ref, s32[1,128]{1,0:T(1,128)} %bitcast.4, bf16[2048,1024]{1,0:T(8,128)(2,1)} %patch_ref.1, ...), custom_call_target="tpu_custom_call" | custom-call | tf_op jit(solution)/shard_map/send_pack/pallas_call | solution.py:87
  37.1 13.2 %all-to-all-start = ((bf16[64,72,128]{2,1,0:T(8,128)(2,1)}), bf16[64,72,128]{2,1,0:T(8,128)(2,1)S(1)}, u32[]{:S(2)}, u32[]{:S(2)}) async-start(bf16[64,72,128]{2,1,0:T(8,128)(2,1)} %get-tuple-element.20), calls=%async_computation | async-start | bytes 2359296 | tf_op jit(solution)/shard_map/all_to_all | solution.py:447
  50.3 2.6 %collective-permute-start.7 = (bf16[1024,256]{1,0:T(8,128)(2,1)}, bf16[1024,256]{1,0:T(8,128)(2,1)S(1)}, u32[]{:S(2)}, u32[]{:S(2)}) collective-permute-start(bf16[1024,256]{1,0:T(8,128)(2,1)} %get-tuple-element.25), channel_id=1, source_target_pairs={{0,3},{1,0},{2,1},{3,2},{4,7},{5,4},{6,5},{7,6},{8,11},{9,8},{10,9... | collective-permute-start | bytes 1572872 | tf_op jit(solution)/shard_map/ppermute | solution.py:441
  52.8 0.0 collective-permute-start.3
  52.8 2.7 %collective-permute-start.8 = (bf16[1024,256]{1,0:T(8,128)(2,1)}, bf16[1024,256]{1,0:T(8,128)(2,1)S(1)}, u32[]{:S(2)}, u32[]{:S(2)}) collective-permute-start(bf16[1024,256]{1,0:T(8,128)(2,1)} %get-tuple-element.26), channel_id=1, source_target_pairs={{0,3},{1,0},{2,1},{3,2},{4,7},{5,4},{6,5},{7,6},{8,11},{9,8},{10,9... | collective-permute-start | bytes 1572872 | tf_op jit(solution)/shard_map/ppermute | solution.py:441
  55.5 0.0 collective-permute-start.4
  55.5 8.5 %collective-permute-done.7.b0 = bf16[1024,256]{1,0:T(8,128)(2,1)S(1)} collective-permute-done((bf16[1024,256]{1,0:T(8,128)(2,1)}, bf16[1024,256]{1,0:T(8,128)(2,1)S(1)}, u32[]{:S(2)}, u32[]{:S(2)}) %collective-permute-start.7) | collective-permute-done | bytes 524320 | tf_op jit(solution)/shard_map/ppermute | solution.py:441
  64.0 2.2 %collective-permute-start.9 = (bf16[1024,256]{1,0:T(8,128)(2,1)S(1)}, bf16[1024,256]{1,0:T(8,128)(2,1)S(1)}, u32[]{:S(2)}, u32[]{:S(2)}) collective-permute-start(bf16[1024,256]{1,0:T(8,128)(2,1)S(1)} %collective-permute-done.7.b0), channel_id=1, source_target_pairs={{0,4},{4,0},{8,12},{12,8},{16,20},{20,16},{24,28},{28,24},{32,36},... | collective-permute-start | bytes 1572872 | tf_op jit(solution)/shard_map/ppermute | solution.py:444
  66.2 0.8 collective-permute-done.3.a0
  67.0 0.0 collective-permute-start.11
  67.0 8.2 %collective-permute-done.8.b1 = bf16[1024,256]{1,0:T(8,128)(2,1)S(1)} collective-permute-done((bf16[1024,256]{1,0:T(8,128)(2,1)}, bf16[1024,256]{1,0:T(8,128)(2,1)S(1)}, u32[]{:S(2)}, u32[]{:S(2)}) %collective-permute-start.8) | collective-permute-done | bytes 524320 | tf_op jit(solution)/shard_map/ppermute | solution.py:441
  75.2 3.3 %collective-permute-start.12 = (bf16[1024,256]{1,0:T(8,128)(2,1)S(1)}, bf16[1024,256]{1,0:T(8,128)(2,1)}, u32[]{:S(2)}, u32[]{:S(2)}) collective-permute-start(bf16[1024,256]{1,0:T(8,128)(2,1)S(1)} %collective-permute-done.8.b1), channel_id=1, source_target_pairs={{0,3},{1,0},{2,1},{3,2},{4,7},{5,4},{6,5},{7,6},{8,11},{9,8},{10,9... | collective-permute-start | bytes 1572872 | tf_op jit(solution)/shard_map/ppermute | solution.py:443
  78.5 1.6 collective-permute-start.5
  80.1 0.0 collective-permute-done.4.a1
  80.1 0.9 collective-permute-start.10
  81.0 0.0 collective-permute-done.9.b0x
  81.0 0.1 collective-permute-start.6
  81.1 8.5 %collective-permute-done.11.c0 = bf16[1024,256]{1,0:T(8,128)(2,1)} collective-permute-done((bf16[1024,256]{1,0:T(8,128)(2,1)S(1)}, bf16[1024,256]{1,0:T(8,128)(2,1)}, u32[]{:S(2)}, u32[]{:S(2)}) %collective-permute-start.11) | collective-permute-done | bytes 524320 | tf_op jit(solution)/shard_map/ppermute | solution.py:442
  89.6 1.6 collective-permute-start.13
  91.2 0.0 collective-permute-done.12.c1
  91.2 0.0 copy-done.5
  91.2 0.1 collective-permute-start.14
  91.3 0.0 all-to-all-done.in_ref
  91.3 1.1 copy-done
  92.4 4.0 %arrive_sort.1 = (bf16[768,256]{1,0:T(8,128)(2,1)}, bf16[768,256]{1,0:T(8,128)(2,1)}, bf16[768,256]{1,0:T(8,128)(2,1)}, bf16[768,256]{1,0:T(8,128)(2,1)}, f32[8,128]{1,0:T(8,128)}) custom-call(s32[1]{0:T(128)} %bitcast.mp_ref.place_ref, bf16[64,72,128]{2,1,0:T(8,128)(2,1)} %copy-done), custom_call_target="tpu_custom_call" | custom-call | tf_op jit(solution)/shard_map/arrive_sort/pallas_call | solution.py:152
  96.4 0.0 collective-permute-done.5.a0x
  96.4 0.1 collective-permute-start
  96.5 0.0 collective-permute-done.10.b1x
  96.5 4.1 %collective-permute-start.1 = (bf16[768,256]{1,0:T(8,128)(2,1)}, bf16[768,256]{1,0:T(8,128)(2,1)S(1)}, u32[]{:S(2)}, u32[]{:S(2)}) collective-permute-start(bf16[768,256]{1,0:T(8,128)(2,1)} %get-tuple-element.23), channel_id=1, source_target_pairs={{0,2},{1,3},{2,0},{3,1},{4,6},{5,7},{6,4},{7,5},{8,10},{9,11},{10,... | collective-permute-start | bytes 1179656 | tf_op jit(solution)/shard_map/ppermute | solution.py:449
  100.6 0.0 collective-permute-done.6.a1x
  100.6 0.0 collective-permute-start.2
  100.6 0.0 collective-permute-done.13.c0x
  100.6 0.0 collective-permute-done.14.c1x
  100.6 8.0 %collective-permute-done.x1 = bf16[768,256]{1,0:T(8,128)(2,1)S(1)} collective-permute-done((bf16[768,256]{1,0:T(8,128)(2,1)}, bf16[768,256]{1,0:T(8,128)(2,1)S(1)}, u32[]{:S(2)}, u32[]{:S(2)}) %collective-permute-start) | collective-permute-done | bytes 393248 | tf_op jit(solution)/shard_map/ppermute | solution.py:449
  108.6 9.8 %collective-permute-done.1.x2 = bf16[768,256]{1,0:T(8,128)(2,1)S(1)} collective-permute-done((bf16[768,256]{1,0:T(8,128)(2,1)}, bf16[768,256]{1,0:T(8,128)(2,1)S(1)}, u32[]{:S(2)}, u32[]{:S(2)}) %collective-permute-start.1) | collective-permute-done | bytes 393248 | tf_op jit(solution)/shard_map/ppermute | solution.py:449
  118.4 0.0 collective-permute-done.2.x3
  118.4 0.0 copy-done.1
  118.5 0.7 copy-done.10
  119.2 0.2 copy-done.11
  119.3 24.8 %block.1 = (bf16[816,256]{1,0:T(8,128)(2,1)}, bf16[816,256]{1,0:T(8,128)(2,1)}, bf16[816,256]{1,0:T(8,128)(2,1)}, bf16[816,256]{1,0:T(8,128)(2,1)}, f32[1,256]{1...) custom-call(s32[2]{0:T(128)} %pad_add_fusion.mp_ref.place_ref, s32[128]{0:T(128)} %image_ref.1, ...), custom_call_target="tpu_custom_call" | custom-call | tf_op jit(solution)/shard_map/block/pallas_call | solution.py:331
  144.2 0.2 collective-permute-start.15
  144.4 3.1 %collective-permute-start.16 = (bf16[816,256]{1,0:T(8,128)(2,1)}, bf16[816,256]{1,0:T(8,128)(2,1)S(1)}, u32[]{:S(2)}, u32[]{:S(2)}) collective-permute-start(bf16[816,256]{1,0:T(8,128)(2,1)} %get-tuple-element.29), channel_id=1, source_target_pairs={{0,2},{1,3},{2,0},{3,1},{4,6},{5,7},{6,4},{7,5},{8,10},{9,11},{10,... | collective-permute-start | bytes 1253384 | tf_op jit(solution)/shard_map/ppermute | solution.py:453
  147.5 0.0 collective-permute-start.17
  147.5 1.5 collective-permute-start.18
  149.0 0.3 collective-permute-start.19
  149.3 16.4 %collective-permute-done.18 = f32[1,256]{1,0:T(1,128)S(1)} collective-permute-done((f32[1,256]{1,0:T(1,128)}, f32[1,256]{1,0:T(1,128)S(1)}, u32[]{:S(2)}, u32[]{:S(2)}) %collective-permute-start.18) | collective-permute-done | bytes 1056 | tf_op jit(solution)/shard_map/ppermute | solution.py:452
  165.7 0.1 collective-permute-start.20
  165.8 0.0 collective-permute-done.19
  165.8 2.6 %collective-permute-done.20 = f32[1,256]{1,0:T(1,128)S(1)} collective-permute-done((f32[1,256]{1,0:T(1,128)}, f32[1,256]{1,0:T(1,128)S(1)}, u32[]{:S(2)}, u32[]{:S(2)}) %collective-permute-start.20) | collective-permute-done | bytes 1056 | tf_op jit(solution)/shard_map/ppermute | solution.py:452
  168.3 0.7 add_add_fusion
  169.0 0.6 broadcast_in_dim.8
  169.7 10.1 %all-to-all-start.1 = ((f32[64,2,128]{2,1,0:T(2,128)}), f32[64,2,128]{2,1,0:T(2,128)S(1)}, u32[]{:S(2)}, u32[]{:S(2)}) async-start(f32[64,2,128]{2,1,0:T(2,128)} %broadcast_in_dim.8), calls=%async_computation.1 | async-start | bytes 131072 | tf_op jit(solution)/shard_map/all_to_all | solution.py:455
  179.8 0.0 collective-permute-done.15.r1
  179.8 0.0 copy-start.6
  179.8 0.0 collective-permute-done.16.r2
  179.9 0.0 collective-permute-done.17.r3
  179.9 0.7 copy-done.6
  180.6 0.2 copy-done.7
  180.8 0.2 copy-done.8
  180.9 3.0 %finish.1 = (bf16[2048,256]{1,0:T(8,128)(2,1)}, f32[16,256]{1,0:T(8,128)}) custom-call(s32[1]{0:T(128)} %bitcast.mp_ref.place_ref, bf16[816,256]{1,0:T(8,128)(2,1)} %get-tuple-element.27.r0, bf16[816,256]{1,0:T(8,128)(2,1)} %copy-done.6, bf16[816,256]{1,0:T(8,128)(2,1)} %copy-done.7, bf16[816,256]{1,0:T(8,128)(2,1)} %copy-done.8), custom_call_target="tpu_custom_call" | custom-call | tf_op jit(solution)/shard_map/finish/pallas_call | solution.py:389
  184.0 6.0 %all-to-all-done.1.sums_ref = f32[64,2,128]{2,1,0:T(2,128)S(1)} async-done(((f32[64,2,128]{2,1,0:T(2,128)}), f32[64,2,128]{2,1,0:T(2,128)S(1)}, u32[]{:S(2)}, u32[]{:S(2)}) %all-to-all-start.1) | async-done | bytes 65568 | tf_op jit(solution)/shard_map/all_to_all | solution.py:455
  189.9 0.6 copy-done.12
  190.5 1.5 pool.1
  (16 shorter events, 0.0 us)
Async XLA Ops:
  37.1 54.2 %all-to-all-start = ((bf16[64,72,128]{2,1,0:T(8,128)(2,1)}), bf16[64,72,128]{2,1,0:T(8,128)(2,1)S(1)}, u32[]{:S(2)}, u32[]{:S(2)}) async-start(bf16[64,72,128]{2,1,0:T(8,128)(2,1)} %get-tuple-element.20), calls=%async_computation | async-start | bytes 2359296 | tf_op jit(solution)/shard_map/all_to_all | solution.py:447
  50.3 13.7 %collective-permute-start.7 = (bf16[1024,256]{1,0:T(8,128)(2,1)}, bf16[1024,256]{1,0:T(8,128)(2,1)S(1)}, u32[]{:S(2)}, u32[]{:S(2)}) collective-permute-start(bf16[1024,256]{1,0:T(8,128)(2,1)} %get-tuple-element.25), channel_id=1, source_target_pairs={{0,3},{1,0},{2,1},{3,2},{4,7},{5,4},{6,5},{7,6},{8,11},{9,8},{10,9... | collective-permute-start | bytes 1572872 | tf_op jit(solution)/shard_map/ppermute | solution.py:441
  52.8 14.2 %collective-permute-start.3 = (bf16[1024,256]{1,0:T(8,128)(2,1)}, bf16[1024,256]{1,0:T(8,128)(2,1)S(1)}, u32[]{:S(2)}, u32[]{:S(2)}) collective-permute-start(bf16[1024,256]{1,0:T(8,128)(2,1)} %get-tuple-element.25), channel_id=1, source_target_pairs={{0,1},{1,2},{2,3},{3,0},{4,5},{5,6},{6,7},{7,4},{8,9},{9,10},{10,1... | collective-permute-start | bytes 1572872 | tf_op jit(solution)/shard_map/ppermute | solution.py:440
  52.8 22.4 %collective-permute-start.8 = (bf16[1024,256]{1,0:T(8,128)(2,1)}, bf16[1024,256]{1,0:T(8,128)(2,1)S(1)}, u32[]{:S(2)}, u32[]{:S(2)}) collective-permute-start(bf16[1024,256]{1,0:T(8,128)(2,1)} %get-tuple-element.26), channel_id=1, source_target_pairs={{0,3},{1,0},{2,1},{3,2},{4,7},{5,4},{6,5},{7,6},{8,11},{9,8},{10,9... | collective-permute-start | bytes 1572872 | tf_op jit(solution)/shard_map/ppermute | solution.py:441
  55.5 24.6 %collective-permute-start.4 = (bf16[1024,256]{1,0:T(8,128)(2,1)}, bf16[1024,256]{1,0:T(8,128)(2,1)S(1)}, u32[]{:S(2)}, u32[]{:S(2)}) collective-permute-start(bf16[1024,256]{1,0:T(8,128)(2,1)} %get-tuple-element.26), channel_id=1, source_target_pairs={{0,1},{1,2},{2,3},{3,0},{4,5},{5,6},{6,7},{7,4},{8,9},{9,10},{10,1... | collective-permute-start | bytes 1572872 | tf_op jit(solution)/shard_map/ppermute | solution.py:440
  64.0 54.4 %copy-start.1 = (bf16[1024,256]{1,0:T(8,128)(2,1)}, bf16[1024,256]{1,0:T(8,128)(2,1)S(1)}, u32[]{:S(2)}) copy-start(bf16[1024,256]{1,0:T(8,128)(2,1)S(1)} %collective-permute-done.7.b0) | copy-start | bytes 1572868
  64.0 17.0 %collective-permute-start.9 = (bf16[1024,256]{1,0:T(8,128)(2,1)S(1)}, bf16[1024,256]{1,0:T(8,128)(2,1)S(1)}, u32[]{:S(2)}, u32[]{:S(2)}) collective-permute-start(bf16[1024,256]{1,0:T(8,128)(2,1)S(1)} %collective-permute-done.7.b0), channel_id=1, source_target_pairs={{0,4},{4,0},{8,12},{12,8},{16,20},{20,16},{24,28},{28,24},{32,36},... | collective-permute-start | bytes 1572872 | tf_op jit(solution)/shard_map/ppermute | solution.py:444
  67.0 51.4 %copy-start.2 = (bf16[1024,256]{1,0:T(8,128)(2,1)}, bf16[1024,256]{1,0:T(8,128)(2,1)S(1)}, u32[]{:S(2)}) copy-start(bf16[1024,256]{1,0:T(8,128)(2,1)S(1)} %collective-permute-done.3.a0) | copy-start | bytes 1572868
  67.0 22.6 %collective-permute-start.11 = (bf16[1024,256]{1,0:T(8,128)(2,1)S(1)}, bf16[1024,256]{1,0:T(8,128)(2,1)}, u32[]{:S(2)}, u32[]{:S(2)}) collective-permute-start(bf16[1024,256]{1,0:T(8,128)(2,1)S(1)} %collective-permute-done.3.a0), channel_id=1, source_target_pairs={{0,1},{1,2},{2,3},{3,0},{4,5},{5,6},{6,7},{7,4},{8,9},{9,10},{10,1... | collective-permute-start | bytes 1572872 | tf_op jit(solution)/shard_map/ppermute | solution.py:442
  75.2 43.2 %copy-start.3 = (bf16[1024,256]{1,0:T(8,128)(2,1)}, bf16[1024,256]{1,0:T(8,128)(2,1)S(1)}, u32[]{:S(2)}) copy-start(bf16[1024,256]{1,0:T(8,128)(2,1)S(1)} %collective-permute-done.8.b1) | copy-start | bytes 1572868
  75.2 16.0 %collective-permute-start.12 = (bf16[1024,256]{1,0:T(8,128)(2,1)S(1)}, bf16[1024,256]{1,0:T(8,128)(2,1)}, u32[]{:S(2)}, u32[]{:S(2)}) collective-permute-start(bf16[1024,256]{1,0:T(8,128)(2,1)S(1)} %collective-permute-done.8.b1), channel_id=1, source_target_pairs={{0,3},{1,0},{2,1},{3,2},{4,7},{5,4},{6,5},{7,6},{8,11},{9,8},{10,9... | collective-permute-start | bytes 1572872 | tf_op jit(solution)/shard_map/ppermute | solution.py:443
  78.5 17.9 %collective-permute-start.5 = (bf16[1024,256]{1,0:T(8,128)(2,1)S(1)}, bf16[1024,256]{1,0:T(8,128)(2,1)}, u32[]{:S(2)}, u32[]{:S(2)}) collective-permute-start(bf16[1024,256]{1,0:T(8,128)(2,1)S(1)} %collective-permute-done.3.a0), channel_id=1, source_target_pairs={{0,4},{4,0},{8,12},{12,8},{16,20},{20,16},{24,28},{28,24},{32,36},... | collective-permute-start | bytes 1572872 | tf_op jit(solution)/shard_map/ppermute | solution.py:444
  80.1 38.3 %copy-start.4 = (bf16[1024,256]{1,0:T(8,128)(2,1)}, bf16[1024,256]{1,0:T(8,128)(2,1)S(1)}, u32[]{:S(2)}) copy-start(bf16[1024,256]{1,0:T(8,128)(2,1)S(1)} %collective-permute-done.4.a1) | copy-start | bytes 1572868
  80.1 16.4 %collective-permute-start.10 = (bf16[1024,256]{1,0:T(8,128)(2,1)S(1)}, bf16[1024,256]{1,0:T(8,128)(2,1)}, u32[]{:S(2)}, u32[]{:S(2)}) collective-permute-start(bf16[1024,256]{1,0:T(8,128)(2,1)S(1)} %collective-permute-done.8.b1), channel_id=1, source_target_pairs={{0,4},{4,0},{8,12},{12,8},{16,20},{20,16},{24,28},{28,24},{32,36},... | collective-permute-start | bytes 1572872 | tf_op jit(solution)/shard_map/ppermute | solution.py:444
  81.0 10.2 %copy-start.5 = (bf16[1024,256]{1,0:T(8,128)(2,1)}, bf16[1024,256]{1,0:T(8,128)(2,1)S(1)}, u32[]{:S(2)}) copy-start(bf16[1024,256]{1,0:T(8,128)(2,1)S(1)} %collective-permute-done.9.b0x) | copy-start | bytes 1572868
  81.0 19.5 %collective-permute-start.6 = (bf16[1024,256]{1,0:T(8,128)(2,1)S(1)}, bf16[1024,256]{1,0:T(8,128)(2,1)}, u32[]{:S(2)}, u32[]{:S(2)}) collective-permute-start(bf16[1024,256]{1,0:T(8,128)(2,1)S(1)} %collective-permute-done.4.a1), channel_id=1, source_target_pairs={{0,4},{4,0},{8,12},{12,8},{16,20},{20,16},{24,28},{28,24},{32,36},... | collective-permute-start | bytes 1572872 | tf_op jit(solution)/shard_map/ppermute | solution.py:444
  89.6 11.0 %collective-permute-start.13 = (bf16[1024,256]{1,0:T(8,128)(2,1)}, bf16[1024,256]{1,0:T(8,128)(2,1)}, u32[]{:S(2)}, u32[]{:S(2)}) collective-permute-start(bf16[1024,256]{1,0:T(8,128)(2,1)} %collective-permute-done.11.c0), channel_id=1, source_target_pairs={{0,4},{4,0},{8,12},{12,8},{16,20},{20,16},{24,28},{28,24},{32,36},... | collective-permute-start | bytes 1572872 | tf_op jit(solution)/shard_map/ppermute | solution.py:444
  91.2 9.4 %collective-permute-start.14 = (bf16[1024,256]{1,0:T(8,128)(2,1)}, bf16[1024,256]{1,0:T(8,128)(2,1)}, u32[]{:S(2)}, u32[]{:S(2)}) collective-permute-start(bf16[1024,256]{1,0:T(8,128)(2,1)} %collective-permute-done.12.c1), channel_id=1, source_target_pairs={{0,4},{4,0},{8,12},{12,8},{16,20},{20,16},{24,28},{28,24},{32,36},... | collective-permute-start | bytes 1572872 | tf_op jit(solution)/shard_map/ppermute | solution.py:444
  91.3 1.1 copy-start
  96.4 12.2 %collective-permute-start = (bf16[768,256]{1,0:T(8,128)(2,1)}, bf16[768,256]{1,0:T(8,128)(2,1)S(1)}, u32[]{:S(2)}, u32[]{:S(2)}) collective-permute-start(bf16[768,256]{1,0:T(8,128)(2,1)} %get-tuple-element.22), channel_id=1, source_target_pairs={{0,1},{1,2},{2,3},{3,0},{4,5},{5,6},{6,7},{7,4},{8,9},{9,10},{10,1... | collective-permute-start | bytes 1179656 | tf_op jit(solution)/shard_map/ppermute | solution.py:449
  96.5 21.9 %collective-permute-start.1 = (bf16[768,256]{1,0:T(8,128)(2,1)}, bf16[768,256]{1,0:T(8,128)(2,1)S(1)}, u32[]{:S(2)}, u32[]{:S(2)}) collective-permute-start(bf16[768,256]{1,0:T(8,128)(2,1)} %get-tuple-element.23), channel_id=1, source_target_pairs={{0,2},{1,3},{2,0},{3,1},{4,6},{5,7},{6,4},{7,5},{8,10},{9,11},{10,... | collective-permute-start | bytes 1179656 | tf_op jit(solution)/shard_map/ppermute | solution.py:449
  100.6 17.8 %collective-permute-start.2 = (bf16[768,256]{1,0:T(8,128)(2,1)}, bf16[768,256]{1,0:T(8,128)(2,1)S(1)}, u32[]{:S(2)}, u32[]{:S(2)}) collective-permute-start(bf16[768,256]{1,0:T(8,128)(2,1)} %get-tuple-element.24), channel_id=1, source_target_pairs={{0,3},{1,0},{2,1},{3,2},{4,7},{5,4},{6,5},{7,6},{8,11},{9,8},{10,9... | collective-permute-start | bytes 1179656 | tf_op jit(solution)/shard_map/ppermute | solution.py:449
  108.6 9.8 %copy-start.9 = (bf16[768,256]{1,0:T(8,128)(2,1)}, bf16[768,256]{1,0:T(8,128)(2,1)S(1)}, u32[]{:S(2)}) copy-start(bf16[768,256]{1,0:T(8,128)(2,1)S(1)} %collective-permute-done.x1) | copy-start | bytes 1179652
  118.4 0.8 copy-start.10
  118.4 0.9 copy-start.11
  144.2 35.7 %collective-permute-start.15 = (bf16[816,256]{1,0:T(8,128)(2,1)}, bf16[816,256]{1,0:T(8,128)(2,1)S(1)}, u32[]{:S(2)}, u32[]{:S(2)}) collective-permute-start(bf16[816,256]{1,0:T(8,128)(2,1)} %get-tuple-element.28), channel_id=1, source_target_pairs={{0,1},{1,2},{2,3},{3,0},{4,5},{5,6},{6,7},{7,4},{8,9},{9,10},{10,1... | collective-permute-start | bytes 1253384 | tf_op jit(solution)/shard_map/ppermute | solution.py:453
  144.4 35.4 %collective-permute-start.16 = (bf16[816,256]{1,0:T(8,128)(2,1)}, bf16[816,256]{1,0:T(8,128)(2,1)S(1)}, u32[]{:S(2)}, u32[]{:S(2)}) collective-permute-start(bf16[816,256]{1,0:T(8,128)(2,1)} %get-tuple-element.29), channel_id=1, source_target_pairs={{0,2},{1,3},{2,0},{3,1},{4,6},{5,7},{6,4},{7,5},{8,10},{9,11},{10,... | collective-permute-start | bytes 1253384 | tf_op jit(solution)/shard_map/ppermute | solution.py:453
  147.5 32.3 %collective-permute-start.17 = (bf16[816,256]{1,0:T(8,128)(2,1)}, bf16[816,256]{1,0:T(8,128)(2,1)S(1)}, u32[]{:S(2)}, u32[]{:S(2)}) collective-permute-start(bf16[816,256]{1,0:T(8,128)(2,1)} %get-tuple-element.30), channel_id=1, source_target_pairs={{0,3},{1,0},{2,1},{3,2},{4,7},{5,4},{6,5},{7,6},{8,11},{9,8},{10,9... | collective-permute-start | bytes 1253384 | tf_op jit(solution)/shard_map/ppermute | solution.py:453
  147.5 18.2 %collective-permute-start.18 = (f32[1,256]{1,0:T(1,128)}, f32[1,256]{1,0:T(1,128)S(1)}, u32[]{:S(2)}, u32[]{:S(2)}) collective-permute-start(f32[1,256]{1,0:T(1,128)} %get-tuple-element.33), channel_id=1, source_target_pairs={{0,1},{1,2},{2,3},{3,0},{4,5},{5,6},{6,7},{7,4},{8,9},{9,10},{10,1... | collective-permute-start | bytes 3080 | tf_op jit(solution)/shard_map/ppermute | solution.py:452
  149.0 16.8 %collective-permute-start.19 = (f32[1,256]{1,0:T(1,128)}, f32[1,256]{1,0:T(1,128)S(1)}, u32[]{:S(2)}, u32[]{:S(2)}) collective-permute-start(f32[1,256]{1,0:T(1,128)} %get-tuple-element.34), channel_id=1, source_target_pairs={{0,2},{1,3},{2,0},{3,1},{4,6},{5,7},{6,4},{7,5},{8,10},{9,11},{10,... | collective-permute-start | bytes 3080 | tf_op jit(solution)/shard_map/ppermute | solution.py:452
  165.7 2.6 %collective-permute-start.20 = (f32[1,256]{1,0:T(1,128)}, f32[1,256]{1,0:T(1,128)S(1)}, u32[]{:S(2)}, u32[]{:S(2)}) collective-permute-start(f32[1,256]{1,0:T(1,128)} %get-tuple-element.35), channel_id=1, source_target_pairs={{0,3},{1,0},{2,1},{3,2},{4,7},{5,4},{6,5},{7,6},{8,11},{9,8},{10,9... | collective-permute-start | bytes 3080 | tf_op jit(solution)/shard_map/ppermute | solution.py:452
  169.7 20.2 %all-to-all-start.1 = ((f32[64,2,128]{2,1,0:T(2,128)}), f32[64,2,128]{2,1,0:T(2,128)S(1)}, u32[]{:S(2)}, u32[]{:S(2)}) async-start(f32[64,2,128]{2,1,0:T(2,128)} %broadcast_in_dim.8), calls=%async_computation.1 | async-start | bytes 131072 | tf_op jit(solution)/shard_map/all_to_all | solution.py:455
  179.8 0.8 copy-start.6
  179.9 0.9 copy-start.7
  179.9 1.1 copy-start.8
  189.9 0.6 copy-start.12

commit v4 on v3

--- a/solution.py
+++ b/solution.py
@@ -95,7 +95,7 @@
             ]
             + [pl.BlockSpec(memory_space=pl.ANY)] * 4,
             out_specs=[pl.BlockSpec((senders, PAY, 128), lambda i, a, b, m: (0, 0, 0))]
-            + [pl.BlockSpec(memory_space=pl.ANY)] * 2,
+            + [pl.BlockSpec((D, PW), lambda i, a, b, m: (0, 0))] * 2,
             scratch_shapes=[
                 pltpu.SMEM((senders,), jnp.int32),
                 pltpu.SMEM((2 * senders,), jnp.int32),
@@ -425,6 +425,13 @@
     )(sums, number, pooled, image)
 
 
+def passed_on(pieces, shift):
+    got = []
+    for d in (1, 2, 3):
+        got.append(lax.ppermute(pieces[d], "mp", shift(d)))
+    return got
+
+
 def whole_block(patches, dest_owner, dest_slot, packed_image, w_query, w_key, w_value, w_out):
     senders = lax.axis_size("dp")
     splits = lax.axis_size("mp")
@@ -446,11 +453,11 @@
 
     incoming = lax.all_to_all(outgoing, "dp", split_axis=0, concat_axis=0, tiled=True)
     *windows, number = arrive_sort(place[:1], incoming)
-    rows = [windows[0]] + [lax.ppermute(windows[d], "mp", shift(d)) for d in (1, 2, 3)]
+    rows = [windows[0]] + passed_on(windows, shift)
     outcome = block(place, packed_image, rows, weights)
     results, sums = outcome[:PARTS], outcome[PARTS:]
     total = sums[0] + sum(lax.ppermute(sums[d], "mp", shift(d)) for d in (1, 2, 3))
-    received = [results[0]] + [lax.ppermute(results[d], "mp", shift(d)) for d in (1, 2, 3)]
+    received = [results[0]] + passed_on(results, shift)
     spread = jnp.broadcast_to(total.reshape(1, 2, PW // 2), (senders, 2, PW // 2))
     gathered = lax.all_to_all(spread, "dp", split_axis=0, concat_axis=0, tiled=True)
     packed_out, pooled = finish(place[:1], received)

time: 192 us -> 161 us (0.84)
  Pallas kernels: 69.2 us -> 38 us
    pallas_call x1, Pallas kernels: 35.8 us -> 4.61 us  [send_pack(): pl.pallas_call(send_kernel, grid_spec=pltpu.PrefetchScalarGridSpec(num_sc...]
where the time goes in v4:
time: 161 us
  waiting for transfers between devices  68.7 us (43%)
  starting transfers between devices  47.7 us (30%)
  Pallas kernels  38 us (24%)
  local copies, waits for them, and re-layouts  4.36 us (3%)
    pallas_call x1, Pallas kernels, block(): pl.pallas_call(block_kernel, grid_spec=pltpu.PrefetchScalarGridSpec(num_s...  24.8 us
    ppermute x3, waiting for transfers between devices, whole_block(): lax.ppermute(sums[d], 'mp', shift(d))  19 us
    ppermute x6, waiting for transfers between devices, passed_on(): got.append(lax.ppermute(pieces[d], 'mp', shift(d)))  17.8 us
    ppermute x2, waiting for transfers between devices, whole_block(): b0, b1 = (lax.ppermute(s, 'mp', shift(-1)) for s in (s0, s1))  16.6 us
    all_to_all x1, starting transfers between devices, whole_block(): lax.all_to_all(outgoing, 'dp', split_axis=0, concat_axis=0, tiled=True)  13.2 us
    all_to_all x1, starting transfers between devices, whole_block(): lax.all_to_all(spread, 'dp', split_axis=0, concat_axis=0, tiled=True)  10.1 us
    ppermute x1, waiting for transfers between devices, whole_block(): c0 = lax.ppermute(a0, 'mp', shift(1))  8.45 us
    ppermute x6, starting transfers between devices, passed_on(): got.append(lax.ppermute(pieces[d], 'mp', shift(d)))  7.53 us
  transfers between devices with their start and end apart: 23, of which 9 were waited for; matrix products, arithmetic and copies ran while one was open for 1% of the time, Pallas kernels for 4%

profile of v4, /device:TPU:1, one launch (start us, length us, event | category | flops | bytes accessed | tf_op | source)
XLA Modules:
  0.0 160.8 jit_solution(17679447382220376192)
XLA Ops:
  0.6 0.6 pad_add_fusion.mp_ref.place_ref
  1.3 4.6 %send_pack.1 = (bf16[64,72,128]{2,1,0:T(8,128)(2,1)}, bf16[1024,256]{1,0:T(8,128)(2,1)}, bf16[1024,256]{1,0:T(8,128)(2,1)}) custom-call(s32[128]{0:T(128)} %owner_ref.1, s32[128]{0:T(128)} %slot_ref.1, s32[2]{0:T(128)} %pad_add_fusion.mp_ref.place_ref, s32[1,128]{1,0:T(1,128)} %bitcast.4, bf16[2048,1024]{1,0:T(8,128)(2,1)} %patch_ref.1, ...), custom_call_target="tpu_custom_call" | custom-call | tf_op jit(solution)/shard_map/send_pack/pallas_call | solution.py:87
  5.9 13.2 %all-to-all-start = ((bf16[64,72,128]{2,1,0:T(8,128)(2,1)}), bf16[64,72,128]{2,1,0:T(8,128)(2,1)S(1)}, u32[]{:S(2)}, u32[]{:S(2)}) async-start(bf16[64,72,128]{2,1,0:T(8,128)(2,1)} %get-tuple-element.20), calls=%async_computation | async-start | bytes 2359296 | tf_op jit(solution)/shard_map/all_to_all | solution.py:454
  19.0 2.6 %collective-permute-start.7 = (bf16[1024,256]{1,0:T(8,128)(2,1)}, bf16[1024,256]{1,0:T(8,128)(2,1)S(1)}, u32[]{:S(2)}, u32[]{:S(2)}) collective-permute-start(bf16[1024,256]{1,0:T(8,128)(2,1)} %get-tuple-element.25), channel_id=1, source_target_pairs={{0,3},{1,0},{2,1},{3,2},{4,7},{5,4},{6,5},{7,6},{8,11},{9,8},{10,9... | collective-permute-start | bytes 1572872 | tf_op jit(solution)/shard_map/ppermute | solution.py:448
  21.6 0.0 collective-permute-start.3
  21.6 2.7 %collective-permute-start.8 = (bf16[1024,256]{1,0:T(8,128)(2,1)}, bf16[1024,256]{1,0:T(8,128)(2,1)S(1)}, u32[]{:S(2)}, u32[]{:S(2)}) collective-permute-start(bf16[1024,256]{1,0:T(8,128)(2,1)} %get-tuple-element.26), channel_id=1, source_target_pairs={{0,3},{1,0},{2,1},{3,2},{4,7},{5,4},{6,5},{7,6},{8,11},{9,8},{10,9... | collective-permute-start | bytes 1572872 | tf_op jit(solution)/shard_map/ppermute | solution.py:448
  24.3 0.0 collective-permute-start.4
  24.3 8.5 %collective-permute-done.7.b0 = bf16[1024,256]{1,0:T(8,128)(2,1)S(1)} collective-permute-done((bf16[1024,256]{1,0:T(8,128)(2,1)}, bf16[1024,256]{1,0:T(8,128)(2,1)S(1)}, u32[]{:S(2)}, u32[]{:S(2)}) %collective-permute-start.7) | collective-permute-done | bytes 524320 | tf_op jit(solution)/shard_map/ppermute | solution.py:448
  32.7 2.2 %collective-permute-start.9 = (bf16[1024,256]{1,0:T(8,128)(2,1)S(1)}, bf16[1024,256]{1,0:T(8,128)(2,1)S(1)}, u32[]{:S(2)}, u32[]{:S(2)}) collective-permute-start(bf16[1024,256]{1,0:T(8,128)(2,1)S(1)} %collective-permute-done.7.b0), channel_id=1, source_target_pairs={{0,4},{4,0},{8,12},{12,8},{16,20},{20,16},{24,28},{28,24},{32,36},... | collective-permute-start | bytes 1572872 | tf_op jit(solution)/shard_map/ppermute | solution.py:451
  35.0 0.8 collective-permute-done.3.a0
  35.8 0.0 collective-permute-start.11
  35.8 8.2 %collective-permute-done.8.b1 = bf16[1024,256]{1,0:T(8,128)(2,1)S(1)} collective-permute-done((bf16[1024,256]{1,0:T(8,128)(2,1)}, bf16[1024,256]{1,0:T(8,128)(2,1)S(1)}, u32[]{:S(2)}, u32[]{:S(2)}) %collective-permute-start.8) | collective-permute-done | bytes 524320 | tf_op jit(solution)/shard_map/ppermute | solution.py:448
  44.0 3.3 %collective-permute-start.12 = (bf16[1024,256]{1,0:T(8,128)(2,1)S(1)}, bf16[1024,256]{1,0:T(8,128)(2,1)}, u32[]{:S(2)}, u32[]{:S(2)}) collective-permute-start(bf16[1024,256]{1,0:T(8,128)(2,1)S(1)} %collective-permute-done.8.b1), channel_id=1, source_target_pairs={{0,3},{1,0},{2,1},{3,2},{4,7},{5,4},{6,5},{7,6},{8,11},{9,8},{10,9... | collective-permute-start | bytes 1572872 | tf_op jit(solution)/shard_map/ppermute | solution.py:450
  47.3 1.6 collective-permute-start.5
  48.9 0.0 collective-permute-done.4.a1
  48.9 0.9 collective-permute-start.10
  49.8 0.0 collective-permute-done.9.b0x
  49.8 0.1 collective-permute-start.6
  49.9 8.5 %collective-permute-done.11.c0 = bf16[1024,256]{1,0:T(8,128)(2,1)} collective-permute-done((bf16[1024,256]{1,0:T(8,128)(2,1)S(1)}, bf16[1024,256]{1,0:T(8,128)(2,1)}, u32[]{:S(2)}, u32[]{:S(2)}) %collective-permute-start.11) | collective-permute-done | bytes 524320 | tf_op jit(solution)/shard_map/ppermute | solution.py:449
  58.3 1.6 collective-permute-start.13
  59.9 0.0 collective-permute-done.12.c1
  59.9 0.0 copy-done.5
  59.9 0.1 collective-permute-start.14
  60.0 0.0 all-to-all-done.in_ref
  60.0 1.1 copy-done
  61.2 4.0 %arrive_sort.1 = (bf16[768,256]{1,0:T(8,128)(2,1)}, bf16[768,256]{1,0:T(8,128)(2,1)}, bf16[768,256]{1,0:T(8,128)(2,1)}, bf16[768,256]{1,0:T(8,128)(2,1)}, f32[8,128]{1,0:T(8,128)}) custom-call(s32[1]{0:T(128)} %bitcast.mp_ref.place_ref, bf16[64,72,128]{2,1,0:T(8,128)(2,1)} %copy-done), custom_call_target="tpu_custom_call" | custom-call | tf_op jit(solution)/shard_map/arrive_sort/pallas_call | solution.py:152
  65.1 0.0 collective-permute-done.5.a0x
  65.2 0.1 collective-permute-start
  65.2 0.0 collective-permute-done.10.b1x
  65.3 4.1 %collective-permute-start.1 = (bf16[768,256]{1,0:T(8,128)(2,1)}, bf16[768,256]{1,0:T(8,128)(2,1)S(1)}, u32[]{:S(2)}, u32[]{:S(2)}) collective-permute-start(bf16[768,256]{1,0:T(8,128)(2,1)} %get-tuple-element.23), channel_id=1, source_target_pairs={{0,2},{1,3},{2,0},{3,1},{4,6},{5,7},{6,4},{7,5},{8,10},{9,11},{10,... | collective-permute-start | bytes 1179656 | tf_op jit(solution)/shard_map/ppermute | solution.py:431
  69.3 0.0 collective-permute-done.6.a1x
  69.3 0.0 collective-permute-start.2
  69.3 0.0 collective-permute-done.13.c0x
  69.3 0.0 collective-permute-done.14.c1x
  69.4 8.0 %collective-permute-done.x1 = bf16[768,256]{1,0:T(8,128)(2,1)S(1)} collective-permute-done((bf16[768,256]{1,0:T(8,128)(2,1)}, bf16[768,256]{1,0:T(8,128)(2,1)S(1)}, u32[]{:S(2)}, u32[]{:S(2)}) %collective-permute-start) | collective-permute-done | bytes 393248 | tf_op jit(solution)/shard_map/ppermute | solution.py:431
  77.4 9.8 %collective-permute-done.1.x2 = bf16[768,256]{1,0:T(8,128)(2,1)S(1)} collective-permute-done((bf16[768,256]{1,0:T(8,128)(2,1)}, bf16[768,256]{1,0:T(8,128)(2,1)S(1)}, u32[]{:S(2)}, u32[]{:S(2)}) %collective-permute-start.1) | collective-permute-done | bytes 393248 | tf_op jit(solution)/shard_map/ppermute | solution.py:431
  87.2 0.0 collective-permute-done.2.x3
  87.2 0.0 copy-done.1
  87.2 0.7 copy-done.10
  87.9 0.2 copy-done.11
  88.1 24.8 %block.1 = (bf16[816,256]{1,0:T(8,128)(2,1)}, bf16[816,256]{1,0:T(8,128)(2,1)}, bf16[816,256]{1,0:T(8,128)(2,1)}, bf16[816,256]{1,0:T(8,128)(2,1)}, f32[1,256]{1...) custom-call(s32[2]{0:T(128)} %pad_add_fusion.mp_ref.place_ref, s32[128]{0:T(128)} %image_ref.1, ...), custom_call_target="tpu_custom_call" | custom-call | tf_op jit(solution)/shard_map/block/pallas_call | solution.py:331
  112.9 0.2 collective-permute-start.15
  113.2 3.1 %collective-permute-start.16 = (bf16[816,256]{1,0:T(8,128)(2,1)}, bf16[816,256]{1,0:T(8,128)(2,1)S(1)}, u32[]{:S(2)}, u32[]{:S(2)}) collective-permute-start(bf16[816,256]{1,0:T(8,128)(2,1)} %get-tuple-element.29), channel_id=1, source_target_pairs={{0,2},{1,3},{2,0},{3,1},{4,6},{5,7},{6,4},{7,5},{8,10},{9,11},{10,... | collective-permute-start | bytes 1253384 | tf_op jit(solution)/shard_map/ppermute | solution.py:431
  116.3 0.0 collective-permute-start.17
  116.3 1.5 collective-permute-start.18
  117.8 0.3 collective-permute-start.19
  118.1 16.4 %collective-permute-done.18 = f32[1,256]{1,0:T(1,128)S(1)} collective-permute-done((f32[1,256]{1,0:T(1,128)}, f32[1,256]{1,0:T(1,128)S(1)}, u32[]{:S(2)}, u32[]{:S(2)}) %collective-permute-start.18) | collective-permute-done | bytes 1056 | tf_op jit(solution)/shard_map/ppermute | solution.py:459
  134.5 0.1 collective-permute-start.20
  134.5 0.0 collective-permute-done.19
  134.5 2.6 %collective-permute-done.20 = f32[1,256]{1,0:T(1,128)S(1)} collective-permute-done((f32[1,256]{1,0:T(1,128)}, f32[1,256]{1,0:T(1,128)S(1)}, u32[]{:S(2)}, u32[]{:S(2)}) %collective-permute-start.20) | collective-permute-done | bytes 1056 | tf_op jit(solution)/shard_map/ppermute | solution.py:459
  137.1 0.7 add_add_fusion
  137.8 0.6 broadcast_in_dim.8
  138.4 10.1 %all-to-all-start.1 = ((f32[64,2,128]{2,1,0:T(2,128)}), f32[64,2,128]{2,1,0:T(2,128)S(1)}, u32[]{:S(2)}, u32[]{:S(2)}) async-start(f32[64,2,128]{2,1,0:T(2,128)} %broadcast_in_dim.8), calls=%async_computation.1 | async-start | bytes 131072 | tf_op jit(solution)/shard_map/all_to_all | solution.py:462
  148.6 0.0 collective-permute-done.15.r1
  148.6 0.0 collective-permute-done.16.r2
  148.6 0.0 copy-start.7
  148.6 0.0 collective-permute-done.17.r3
  148.6 0.7 copy-done.6
  149.4 0.2 copy-done.7
  149.5 0.2 copy-done.8
  149.7 3.0 %finish.1 = (bf16[2048,256]{1,0:T(8,128)(2,1)}, f32[16,256]{1,0:T(8,128)}) custom-call(s32[1]{0:T(128)} %bitcast.mp_ref.place_ref, bf16[816,256]{1,0:T(8,128)(2,1)} %get-tuple-element.27.r0, bf16[816,256]{1,0:T(8,128)(2,1)} %copy-done.6, bf16[816,256]{1,0:T(8,128)(2,1)} %copy-done.7, bf16[816,256]{1,0:T(8,128)(2,1)} %copy-done.8), custom_call_target="tpu_custom_call" | custom-call | tf_op jit(solution)/shard_map/finish/pallas_call | solution.py:389
  152.7 6.0 %all-to-all-done.1.sums_ref = f32[64,2,128]{2,1,0:T(2,128)S(1)} async-done(((f32[64,2,128]{2,1,0:T(2,128)}), f32[64,2,128]{2,1,0:T(2,128)S(1)}, u32[]{:S(2)}, u32[]{:S(2)}) %all-to-all-start.1) | async-done | bytes 65568 | tf_op jit(solution)/shard_map/all_to_all | solution.py:462
  158.7 0.6 copy-done.12
  159.3 1.5 pool.1
  (16 shorter events, 0.0 us)
Async XLA Ops:
  5.9 54.2 %all-to-all-start = ((bf16[64,72,128]{2,1,0:T(8,128)(2,1)}), bf16[64,72,128]{2,1,0:T(8,128)(2,1)S(1)}, u32[]{:S(2)}, u32[]{:S(2)}) async-start(bf16[64,72,128]{2,1,0:T(8,128)(2,1)} %get-tuple-element.20), calls=%async_computation | async-start | bytes 2359296 | tf_op jit(solution)/shard_map/all_to_all | solution.py:454
  19.0 13.7 %collective-permute-start.7 = (bf16[1024,256]{1,0:T(8,128)(2,1)}, bf16[1024,256]{1,0:T(8,128)(2,1)S(1)}, u32[]{:S(2)}, u32[]{:S(2)}) collective-permute-start(bf16[1024,256]{1,0:T(8,128)(2,1)} %get-tuple-element.25), channel_id=1, source_target_pairs={{0,3},{1,0},{2,1},{3,2},{4,7},{5,4},{6,5},{7,6},{8,11},{9,8},{10,9... | collective-permute-start | bytes 1572872 | tf_op jit(solution)/shard_map/ppermute | solution.py:448
  21.6 14.2 %collective-permute-start.3 = (bf16[1024,256]{1,0:T(8,128)(2,1)}, bf16[1024,256]{1,0:T(8,128)(2,1)S(1)}, u32[]{:S(2)}, u32[]{:S(2)}) collective-permute-start(bf16[1024,256]{1,0:T(8,128)(2,1)} %get-tuple-element.25), channel_id=1, source_target_pairs={{0,1},{1,2},{2,3},{3,0},{4,5},{5,6},{6,7},{7,4},{8,9},{9,10},{10,1... | collective-permute-start | bytes 1572872 | tf_op jit(solution)/shard_map/ppermute | solution.py:447
  21.6 22.4 %collective-permute-start.8 = (bf16[1024,256]{1,0:T(8,128)(2,1)}, bf16[1024,256]{1,0:T(8,128)(2,1)S(1)}, u32[]{:S(2)}, u32[]{:S(2)}) collective-permute-start(bf16[1024,256]{1,0:T(8,128)(2,1)} %get-tuple-element.26), channel_id=1, source_target_pairs={{0,3},{1,0},{2,1},{3,2},{4,7},{5,4},{6,5},{7,6},{8,11},{9,8},{10,9... | collective-permute-start | bytes 1572872 | tf_op jit(solution)/shard_map/ppermute | solution.py:448
  24.3 24.6 %collective-permute-start.4 = (bf16[1024,256]{1,0:T(8,128)(2,1)}, bf16[1024,256]{1,0:T(8,128)(2,1)S(1)}, u32[]{:S(2)}, u32[]{:S(2)}) collective-permute-start(bf16[1024,256]{1,0:T(8,128)(2,1)} %get-tuple-element.26), channel_id=1, source_target_pairs={{0,1},{1,2},{2,3},{3,0},{4,5},{5,6},{6,7},{7,4},{8,9},{9,10},{10,1... | collective-permute-start | bytes 1572872 | tf_op jit(solution)/shard_map/ppermute | solution.py:447
  32.7 54.4 %copy-start.1 = (bf16[1024,256]{1,0:T(8,128)(2,1)}, bf16[1024,256]{1,0:T(8,128)(2,1)S(1)}, u32[]{:S(2)}) copy-start(bf16[1024,256]{1,0:T(8,128)(2,1)S(1)} %collective-permute-done.7.b0) | copy-start | bytes 1572868
  32.7 17.0 %collective-permute-start.9 = (bf16[1024,256]{1,0:T(8,128)(2,1)S(1)}, bf16[1024,256]{1,0:T(8,128)(2,1)S(1)}, u32[]{:S(2)}, u32[]{:S(2)}) collective-permute-start(bf16[1024,256]{1,0:T(8,128)(2,1)S(1)} %collective-permute-done.7.b0), channel_id=1, source_target_pairs={{0,4},{4,0},{8,12},{12,8},{16,20},{20,16},{24,28},{28,24},{32,36},... | collective-permute-start | bytes 1572872 | tf_op jit(solution)/shard_map/ppermute | solution.py:451
  35.8 51.4 %copy-start.2 = (bf16[1024,256]{1,0:T(8,128)(2,1)}, bf16[1024,256]{1,0:T(8,128)(2,1)S(1)}, u32[]{:S(2)}) copy-start(bf16[1024,256]{1,0:T(8,128)(2,1)S(1)} %collective-permute-done.3.a0) | copy-start | bytes 1572868
  35.8 22.6 %collective-permute-start.11 = (bf16[1024,256]{1,0:T(8,128)(2,1)S(1)}, bf16[1024,256]{1,0:T(8,128)(2,1)}, u32[]{:S(2)}, u32[]{:S(2)}) collective-permute-start(bf16[1024,256]{1,0:T(8,128)(2,1)S(1)} %collective-permute-done.3.a0), channel_id=1, source_target_pairs={{0,1},{1,2},{2,3},{3,0},{4,5},{5,6},{6,7},{7,4},{8,9},{9,10},{10,1... | collective-permute-start | bytes 1572872 | tf_op jit(solution)/shard_map/ppermute | solution.py:449
  44.0 43.2 %copy-start.3 = (bf16[1024,256]{1,0:T(8,128)(2,1)}, bf16[1024,256]{1,0:T(8,128)(2,1)S(1)}, u32[]{:S(2)}) copy-start(bf16[1024,256]{1,0:T(8,128)(2,1)S(1)} %collective-permute-done.8.b1) | copy-start | bytes 1572868
  44.0 16.0 %collective-permute-start.12 = (bf16[1024,256]{1,0:T(8,128)(2,1)S(1)}, bf16[1024,256]{1,0:T(8,128)(2,1)}, u32[]{:S(2)}, u32[]{:S(2)}) collective-permute-start(bf16[1024,256]{1,0:T(8,128)(2,1)S(1)} %collective-permute-done.8.b1), channel_id=1, source_target_pairs={{0,3},{1,0},{2,1},{3,2},{4,7},{5,4},{6,5},{7,6},{8,11},{9,8},{10,9... | collective-permute-start | bytes 1572872 | tf_op jit(solution)/shard_map/ppermute | solution.py:450
  47.3 17.9 %collective-permute-start.5 = (bf16[1024,256]{1,0:T(8,128)(2,1)S(1)}, bf16[1024,256]{1,0:T(8,128)(2,1)}, u32[]{:S(2)}, u32[]{:S(2)}) collective-permute-start(bf16[1024,256]{1,0:T(8,128)(2,1)S(1)} %collective-permute-done.3.a0), channel_id=1, source_target_pairs={{0,4},{4,0},{8,12},{12,8},{16,20},{20,16},{24,28},{28,24},{32,36},... | collective-permute-start | bytes 1572872 | tf_op jit(solution)/shard_map/ppermute | solution.py:451
  48.9 38.3 %copy-start.4 = (bf16[1024,256]{1,0:T(8,128)(2,1)}, bf16[1024,256]{1,0:T(8,128)(2,1)S(1)}, u32[]{:S(2)}) copy-start(bf16[1024,256]{1,0:T(8,128)(2,1)S(1)} %collective-permute-done.4.a1) | copy-start | bytes 1572868
  48.9 16.4 %collective-permute-start.10 = (bf16[1024,256]{1,0:T(8,128)(2,1)S(1)}, bf16[1024,256]{1,0:T(8,128)(2,1)}, u32[]{:S(2)}, u32[]{:S(2)}) collective-permute-start(bf16[1024,256]{1,0:T(8,128)(2,1)S(1)} %collective-permute-done.8.b1), channel_id=1, source_target_pairs={{0,4},{4,0},{8,12},{12,8},{16,20},{20,16},{24,28},{28,24},{32,36},... | collective-permute-start | bytes 1572872 | tf_op jit(solution)/shard_map/ppermute | solution.py:451
  49.8 10.2 %copy-start.5 = (bf16[1024,256]{1,0:T(8,128)(2,1)}, bf16[1024,256]{1,0:T(8,128)(2,1)S(1)}, u32[]{:S(2)}) copy-start(bf16[1024,256]{1,0:T(8,128)(2,1)S(1)} %collective-permute-done.9.b0x) | copy-start | bytes 1572868
  49.8 19.5 %collective-permute-start.6 = (bf16[1024,256]{1,0:T(8,128)(2,1)S(1)}, bf16[1024,256]{1,0:T(8,128)(2,1)}, u32[]{:S(2)}, u32[]{:S(2)}) collective-permute-start(bf16[1024,256]{1,0:T(8,128)(2,1)S(1)} %collective-permute-done.4.a1), channel_id=1, source_target_pairs={{0,4},{4,0},{8,12},{12,8},{16,20},{20,16},{24,28},{28,24},{32,36},... | collective-permute-start | bytes 1572872 | tf_op jit(solution)/shard_map/ppermute | solution.py:451
  58.3 11.0 %collective-permute-start.13 = (bf16[1024,256]{1,0:T(8,128)(2,1)}, bf16[1024,256]{1,0:T(8,128)(2,1)}, u32[]{:S(2)}, u32[]{:S(2)}) collective-permute-start(bf16[1024,256]{1,0:T(8,128)(2,1)} %collective-permute-done.11.c0), channel_id=1, source_target_pairs={{0,4},{4,0},{8,12},{12,8},{16,20},{20,16},{24,28},{28,24},{32,36},... | collective-permute-start | bytes 1572872 | tf_op jit(solution)/shard_map/ppermute | solution.py:451
  59.9 9.4 %collective-permute-start.14 = (bf16[1024,256]{1,0:T(8,128)(2,1)}, bf16[1024,256]{1,0:T(8,128)(2,1)}, u32[]{:S(2)}, u32[]{:S(2)}) collective-permute-start(bf16[1024,256]{1,0:T(8,128)(2,1)} %collective-permute-done.12.c1), channel_id=1, source_target_pairs={{0,4},{4,0},{8,12},{12,8},{16,20},{20,16},{24,28},{28,24},{32,36},... | collective-permute-start | bytes 1572872 | tf_op jit(solution)/shard_map/ppermute | solution.py:451
  60.0 1.1 copy-start
  65.2 12.2 %collective-permute-start = (bf16[768,256]{1,0:T(8,128)(2,1)}, bf16[768,256]{1,0:T(8,128)(2,1)S(1)}, u32[]{:S(2)}, u32[]{:S(2)}) collective-permute-start(bf16[768,256]{1,0:T(8,128)(2,1)} %get-tuple-element.22), channel_id=1, source_target_pairs={{0,1},{1,2},{2,3},{3,0},{4,5},{5,6},{6,7},{7,4},{8,9},{9,10},{10,1... | collective-permute-start | bytes 1179656 | tf_op jit(solution)/shard_map/ppermute | solution.py:431
  65.3 21.9 %collective-permute-start.1 = (bf16[768,256]{1,0:T(8,128)(2,1)}, bf16[768,256]{1,0:T(8,128)(2,1)S(1)}, u32[]{:S(2)}, u32[]{:S(2)}) collective-permute-start(bf16[768,256]{1,0:T(8,128)(2,1)} %get-tuple-element.23), channel_id=1, source_target_pairs={{0,2},{1,3},{2,0},{3,1},{4,6},{5,7},{6,4},{7,5},{8,10},{9,11},{10,... | collective-permute-start | bytes 1179656 | tf_op jit(solution)/shard_map/ppermute | solution.py:431
  69.3 17.8 %collective-permute-start.2 = (bf16[768,256]{1,0:T(8,128)(2,1)}, bf16[768,256]{1,0:T(8,128)(2,1)S(1)}, u32[]{:S(2)}, u32[]{:S(2)}) collective-permute-start(bf16[768,256]{1,0:T(8,128)(2,1)} %get-tuple-element.24), channel_id=1, source_target_pairs={{0,3},{1,0},{2,1},{3,2},{4,7},{5,4},{6,5},{7,6},{8,11},{9,8},{10,9... | collective-permute-start | bytes 1179656 | tf_op jit(solution)/shard_map/ppermute | solution.py:431
  77.4 9.8 %copy-start.9 = (bf16[768,256]{1,0:T(8,128)(2,1)}, bf16[768,256]{1,0:T(8,128)(2,1)S(1)}, u32[]{:S(2)}) copy-start(bf16[768,256]{1,0:T(8,128)(2,1)S(1)} %collective-permute-done.x1) | copy-start | bytes 1179652
  87.2 0.8 copy-start.10
  87.2 0.9 copy-start.11
  112.9 35.7 %collective-permute-start.15 = (bf16[816,256]{1,0:T(8,128)(2,1)}, bf16[816,256]{1,0:T(8,128)(2,1)S(1)}, u32[]{:S(2)}, u32[]{:S(2)}) collective-permute-start(bf16[816,256]{1,0:T(8,128)(2,1)} %get-tuple-element.28), channel_id=1, source_target_pairs={{0,1},{1,2},{2,3},{3,0},{4,5},{5,6},{6,7},{7,4},{8,9},{9,10},{10,1... | collective-permute-start | bytes 1253384 | tf_op jit(solution)/shard_map/ppermute | solution.py:431
  113.2 35.4 %collective-permute-start.16 = (bf16[816,256]{1,0:T(8,128)(2,1)}, bf16[816,256]{1,0:T(8,128)(2,1)S(1)}, u32[]{:S(2)}, u32[]{:S(2)}) collective-permute-start(bf16[816,256]{1,0:T(8,128)(2,1)} %get-tuple-element.29), channel_id=1, source_target_pairs={{0,2},{1,3},{2,0},{3,1},{4,6},{5,7},{6,4},{7,5},{8,10},{9,11},{10,... | collective-permute-start | bytes 1253384 | tf_op jit(solution)/shard_map/ppermute | solution.py:431
  116.3 32.3 %collective-permute-start.17 = (bf16[816,256]{1,0:T(8,128)(2,1)}, bf16[816,256]{1,0:T(8,128)(2,1)S(1)}, u32[]{:S(2)}, u32[]{:S(2)}) collective-permute-start(bf16[816,256]{1,0:T(8,128)(2,1)} %get-tuple-element.30), channel_id=1, source_target_pairs={{0,3},{1,0},{2,1},{3,2},{4,7},{5,4},{6,5},{7,6},{8,11},{9,8},{10,9... | collective-permute-start | bytes 1253384 | tf_op jit(solution)/shard_map/ppermute | solution.py:431
  116.3 18.2 %collective-permute-start.18 = (f32[1,256]{1,0:T(1,128)}, f32[1,256]{1,0:T(1,128)S(1)}, u32[]{:S(2)}, u32[]{:S(2)}) collective-permute-start(f32[1,256]{1,0:T(1,128)} %get-tuple-element.33), channel_id=1, source_target_pairs={{0,1},{1,2},{2,3},{3,0},{4,5},{5,6},{6,7},{7,4},{8,9},{9,10},{10,1... | collective-permute-start | bytes 3080 | tf_op jit(solution)/shard_map/ppermute | solution.py:459
  117.8 16.8 %collective-permute-start.19 = (f32[1,256]{1,0:T(1,128)}, f32[1,256]{1,0:T(1,128)S(1)}, u32[]{:S(2)}, u32[]{:S(2)}) collective-permute-start(f32[1,256]{1,0:T(1,128)} %get-tuple-element.34), channel_id=1, source_target_pairs={{0,2},{1,3},{2,0},{3,1},{4,6},{5,7},{6,4},{7,5},{8,10},{9,11},{10,... | collective-permute-start | bytes 3080 | tf_op jit(solution)/shard_map/ppermute | solution.py:459
  134.5 2.6 %collective-permute-start.20 = (f32[1,256]{1,0:T(1,128)}, f32[1,256]{1,0:T(1,128)S(1)}, u32[]{:S(2)}, u32[]{:S(2)}) collective-permute-start(f32[1,256]{1,0:T(1,128)} %get-tuple-element.35), channel_id=1, source_target_pairs={{0,3},{1,0},{2,1},{3,2},{4,7},{5,4},{6,5},{7,6},{8,11},{9,8},{10,9... | collective-permute-start | bytes 3080 | tf_op jit(solution)/shard_map/ppermute | solution.py:459
  138.4 20.2 %all-to-all-start.1 = ((f32[64,2,128]{2,1,0:T(2,128)}), f32[64,2,128]{2,1,0:T(2,128)S(1)}, u32[]{:S(2)}, u32[]{:S(2)}) async-start(f32[64,2,128]{2,1,0:T(2,128)} %broadcast_in_dim.8), calls=%async_computation.1 | async-start | bytes 131072 | tf_op jit(solution)/shard_map/all_to_all | solution.py:462
  148.6 0.8 copy-start.6
  148.6 0.9 copy-start.7
  148.6 1.1 copy-start.8
  158.7 0.6 copy-start.12

commit v5 on v4

--- a/solution.py
+++ b/solution.py
@@ -12,21 +12,20 @@
 PARTS = 4
 PW = D // PARTS
 PART_SLOTS = SLOTS // PARTS
-WIN = PART_SLOTS + 16
+WIN = PART_SLOTS + 15
 ROWS_W = WIN * TILE
 IMG = 16
 EXTRA = 3 * IMG
 HD = 64
 MAX_LOCAL = 4
 PAY = 72
-IMG_ROWS = 256
 EXP_SCALE = HD ** (-0.5) * 1.4426950408889634
 VMEM = pltpu.CompilerParams(vmem_limit_bytes=56 * 1024 * 1024)
 
 
-def send_kernel(owner_ref, slot_ref, mp_ref, image_ref, patch_ref, wq, wk, wv, wo, out_ref, s0, s1, count_ref, place_ref, sems):
+def send_kernel(owner_ref, slot_ref, mp_ref, core_ref, image_ref, patch_ref, wq, wk, wv, wo, out_ref, s0, s1, count_ref, place_ref, sems):
     owners = out_ref.shape[0]
-    core = mp_ref[1]
+    core = core_ref[0]
     even = [pltpu.make_async_copy(wq, s0, sems.at[0]), pltpu.make_async_copy(wk, s1, sems.at[1])]
     odd = [pltpu.make_async_copy(wv, s0, sems.at[0])]
     for n in range(PARTS):
@@ -83,19 +82,19 @@
             copy.wait()
 
 
-def send_pack(owner, slot, place, image, patches, weights, senders):
+def send_pack(owner, slot, part, core, image, patches, weights, senders):
     return pl.pallas_call(
         send_kernel,
         grid_spec=pltpu.PrefetchScalarGridSpec(
-            num_scalar_prefetch=3,
+            num_scalar_prefetch=4,
             grid=(1,),
             in_specs=[
-                pl.BlockSpec((1, SLOTS), lambda i, a, b, m: (0, 0)),
-                pl.BlockSpec((SLOTS * TILE, PW), lambda i, a, b, m: (0, m[0])),
+                pl.BlockSpec((1, SLOTS), lambda i, a, b, m, c: (0, 0)),
+                pl.BlockSpec((SLOTS * TILE, PW), lambda i, a, b, m, c: (0, m[0])),
             ]
             + [pl.BlockSpec(memory_space=pl.ANY)] * 4,
-            out_specs=[pl.BlockSpec((senders, PAY, 128), lambda i, a, b, m: (0, 0, 0))]
-            + [pl.BlockSpec((D, PW), lambda i, a, b, m: (0, 0))] * 2,
+            out_specs=[pl.BlockSpec((senders, PAY, 128), lambda i, a, b, m, c: (0, 0, 0))]
+            + [pl.BlockSpec((D, PW), lambda i, a, b, m, c: (0, 0))] * 2,
             scratch_shapes=[
                 pltpu.SMEM((senders,), jnp.int32),
                 pltpu.SMEM((2 * senders,), jnp.int32),
@@ -106,7 +105,7 @@
         + [jax.ShapeDtypeStruct((D, PW), jnp.bfloat16)] * 2,
         compiler_params=VMEM,
         name="send_pack",
-    )(owner, slot, place, image, patches, *weights)
+    )(owner, slot, part, core, image, patches, *weights)
 
 
 def arrive_kernel(mp_ref, in_ref, out0, out1, out2, out3, total_ref, sorted_ref, label_ref, slot_ref, sems):
@@ -154,7 +153,7 @@
         grid_spec=pltpu.PrefetchScalarGridSpec(
             num_scalar_prefetch=1,
             grid=(1,),
-            in_specs=[pl.BlockSpec(incoming.shape, lambda i, a: (0, 0, 0))],
+            in_specs=[pl.BlockSpec(memory_space=pltpu.VMEM)],
             out_specs=[pl.BlockSpec(memory_space=pl.ANY)] * PARTS + [pl.BlockSpec((8, 128), lambda i, a: (0, 0))],
             scratch_shapes=[
                 pltpu.VMEM((SLOTS * TILE + ROWS_W - PART_SLOTS * TILE, PW), jnp.bfloat16),
@@ -169,15 +168,12 @@
     )(mp, incoming)
 
 
-def block_kernel(place_ref, image_ref, x0, x1, x2, x3, wq, wk, wv, wo, a0, a1, a0x, a1x, b0, b1, b0x, b1x, c0, c1, c0x, c1x,
+def block_kernel(part_ref, core_ref, image_ref, x0, x1, x2, x3, wq, wk, wv, wo, a0, a1, a0x, a1x, b0, b1, b0x, b1x, c0, c1, c0x, c1x,
                  out0, out1, out2, out3, sum0, sum1, sum2, sum3,
-                 x_ref, norm_ref, q_ref, k_ref, v_ref, att_ref, w_refs, begin_ref, end_ref, xsem, wsem):
-    part = place_ref[0]
-    core = place_ref[1]
-    x_copies = []
-    for d, x in enumerate((x0, x1, x2, x3)):
-        x_copies.append(pltpu.make_async_copy(x, x_ref.at[(part + PARTS - d) % PARTS], xsem.at[d]))
-        x_copies[-1].start()
+                 norm_ref, q_ref, k_ref, v_ref, att_ref, w_refs, begin_ref, end_ref, wsem):
+    part = part_ref[0]
+    core = core_ref[0]
+    xs = (x0, x1, x2, x3)
     copies = [[pltpu.make_async_copy(w, w_refs.at[0, n], wsem.at[n]) for n, w in enumerate((wq, wk, wv))]]
     for n in range(PARTS):
         block_rows = pl.ds(n * PW, PW)
@@ -210,34 +206,30 @@
         return label, count, first, mine
 
     before = jnp.where(part > 0, image_ref[jnp.maximum(window - 1, 0)], -1)
-    _, count, first, _ = lax.fori_loop(0, WIN, scan, (before, jnp.int32(0), jnp.int32(0), jnp.int32(0)), unroll=4)
-    for copy in x_copies:
-        copy.wait()
+    _, count, first, _ = lax.fori_loop(0, WIN + 1, scan, (before, jnp.int32(0), jnp.int32(0), jnp.int32(0)), unroll=4)
 
     chunk = 128
 
     def norm(i, carry):
-        at = pl.multiple_of(i * chunk, chunk)
-        rows = [x_ref[p, pl.ds(at, chunk), :].astype(jnp.float32) for p in range(PARTS)]
+        at = pl.multiple_of(jnp.minimum(i * chunk, ROWS_W - chunk), TILE)
+        rows = [x[pl.ds(at, chunk), :].astype(jnp.float32) for x in xs]
         mean = jnp.sum(rows[0] + rows[1] + rows[2] + rows[3], axis=-1, keepdims=True) * (1.0 / D)
         centred = [r - mean for r in rows]
         squares = [r * r for r in centred]
         spread = jnp.sum(squares[0] + squares[1] + squares[2] + squares[3], axis=-1, keepdims=True) * (1.0 / D)
         scale = lax.rsqrt(spread + EPSILON)
-        for p in range(PARTS):
-            norm_ref[pl.ds(at, chunk), p * PW : (p + 1) * PW] = (centred[p] * scale).astype(jnp.bfloat16)
+        for d in range(PARTS):
+            norm_ref[(part + PARTS - d) % PARTS, pl.ds(at, chunk), :] = (centred[d] * scale).astype(jnp.bfloat16)
         return carry
 
-    lax.fori_loop(0, ROWS_W // chunk, norm, 0)
-    lane = lax.broadcasted_iota(jnp.int32, (IMG_ROWS, PW), 1)
-    upper = lax.broadcasted_iota(jnp.int32, (IMG_ROWS, 128), 1) + 128
-    low = lax.broadcasted_iota(jnp.int32, (IMG_ROWS, 128), 1) < HD
+    lax.fori_loop(0, pl.cdiv(ROWS_W, chunk), norm, 0)
 
     for g in range(PARTS):
         for copy in copies[g]:
             copy.wait()
         for n, ref in enumerate((q_ref, k_ref, v_ref)):
-            ref[...] = jnp.dot(norm_ref[...], w_refs[g, n], preferred_element_type=jnp.float32).astype(jnp.bfloat16)
+            normed = jnp.concatenate([norm_ref[p] for p in range(PARTS)], axis=1)
+            ref[...] = jnp.dot(normed, w_refs[g, n], preferred_element_type=jnp.float32).astype(jnp.bfloat16)
 
         def image(i, carry):
             row = pl.multiple_of(begin_ref[i] * TILE, TILE)
@@ -305,7 +297,7 @@
         block_rows = pl.ds(pl.multiple_of(n * PW, PW), PW)
         mix = jnp.concatenate([w_refs[g, 3, block_rows, :] for g in range(PARTS)], axis=0)
         projected = jnp.dot(att_ref[...], mix, preferred_element_type=jnp.float32)
-        result = jnp.where(live, x_ref[n].astype(jnp.float32) + projected, 0.0)
+        result = jnp.where(live, xs[-d % PARTS][...].astype(jnp.float32) + projected, 0.0)
         out[:ROWS_W, :] = result.astype(jnp.bfloat16)
         pairs = result.reshape(WIN, 2, 8, PW)
         pairs = pairs[:, 0] + pairs[:, 1]
@@ -324,20 +316,20 @@
         sum_ref[...] = jnp.sum(pooled, axis=0, keepdims=True)
 
 
-def block(place, image, xs, weights):
+def block(part, core, image, xs, weights):
     outs = jax.ShapeDtypeStruct((ROWS_W + EXTRA, PW), jnp.bfloat16)
-    whole = lambda i, a, b: (0, 0)
+    whole = lambda i, a, b, c: (0, 0)
     wide = pltpu.VMEM((ROWS_W, PW), jnp.bfloat16)
     return pl.pallas_call(
         block_kernel,
         grid_spec=pltpu.PrefetchScalarGridSpec(
-            num_scalar_prefetch=2,
+            num_scalar_prefetch=3,
             grid=(1,),
-            in_specs=[pl.BlockSpec(memory_space=pl.ANY)] * (len(xs) + len(weights)),
+            in_specs=[pl.BlockSpec(memory_space=pltpu.VMEM)] * len(xs)
+            + [pl.BlockSpec(memory_space=pl.ANY)] * len(weights),
             out_specs=[pl.BlockSpec((ROWS_W + EXTRA, PW), whole)] * PARTS + [pl.BlockSpec((1, PW), whole)] * PARTS,
             scratch_shapes=[
                 pltpu.VMEM((PARTS, ROWS_W, PW), jnp.bfloat16),
-                pltpu.VMEM((ROWS_W, D), jnp.bfloat16),
                 wide,
                 wide,
                 wide,
@@ -345,58 +337,48 @@
                 pltpu.VMEM((PARTS, 4, D, PW), jnp.bfloat16),
                 pltpu.SMEM((8,), jnp.int32),
                 pltpu.SMEM((8,), jnp.int32),
-                pltpu.SemaphoreType.DMA((PARTS,)),
                 pltpu.SemaphoreType.DMA((5 * PARTS - 1,)),
             ],
         ),
         out_shape=[outs] * PARTS + [jax.ShapeDtypeStruct((1, PW), jnp.float32)] * PARTS,
         compiler_params=VMEM,
         name="block",
-    )(place, image, *xs, *weights)
-
-
-def finish_kernel(place_ref, r0, r1, r2, r3, out_ref, pooled_ref, in_ref, out_vmem, sems, out_sems):
+    )(part, core, image, *xs, *weights)
+
+
+def finish_kernel(part_ref, r0, r1, r2, r3, out_ref, pooled_ref, out_vmem, sems):
     size = PART_SLOTS * TILE
     halo = ROWS_W - size
-    part = place_ref[0]
-    copies = []
-    for d, r in enumerate((r0, r1, r2, r3)):
-        copies.append(pltpu.make_async_copy(r, in_ref.at[(part + PARTS - d) % PARTS], sems.at[d]))
-    for copy in copies:
-        copy.start()
-    for copy in copies:
-        copy.wait()
+    received = (r0, r1, r2, r3)
     writes = []
-    for p in range(PARTS):
-        start = in_ref[p, :halo, :]
-        if p:
-            start = start + in_ref[p - 1, size:ROWS_W, :]
-        out_vmem[p * size : p * size + halo, :] = start
-        out_vmem[p * size + halo : (p + 1) * size, :] = in_ref[p, halo:size, :]
-        rows = pl.ds(p * size, size)
-        writes.append(pltpu.make_async_copy(out_vmem.at[rows, :], out_ref.at[rows, :], out_sems.at[p]))
+    pooled = jnp.zeros((IMG, PW), jnp.float32)
+    for d, r in enumerate(received):
+        p = (part_ref[0] + PARTS - d) % PARTS
+        base = pl.multiple_of(p * size, size)
+        before = received[(d + 1) % PARTS][size:ROWS_W, :]
+        start = r[:halo, :] + jnp.where(p > 0, before, jnp.zeros_like(before))
+        out_vmem[pl.ds(base, halo), :] = start
+        out_vmem[pl.ds(pl.multiple_of(base + halo, TILE), size - halo), :] = r[halo:size, :]
+        rows = pl.ds(base, size)
+        writes.append(pltpu.make_async_copy(out_vmem.at[rows, :], out_ref.at[rows, :], sems.at[d]))
         writes[-1].start()
-    pooled = jnp.zeros((IMG, PW), jnp.float32)
-    for p in range(PARTS):
         for n in range(3):
-            pooled = pooled + in_ref[p, ROWS_W + n * IMG : ROWS_W + (n + 1) * IMG, :].astype(jnp.float32)
+            pooled = pooled + r[ROWS_W + n * IMG : ROWS_W + (n + 1) * IMG, :].astype(jnp.float32)
     pooled_ref[...] = pooled
     for write in writes:
         write.wait()
 
 
-def finish(place, received):
+def finish(part, received):
     return pl.pallas_call(
         finish_kernel,
         grid_spec=pltpu.PrefetchScalarGridSpec(
             num_scalar_prefetch=1,
             grid=(1,),
-            in_specs=[pl.BlockSpec(memory_space=pl.ANY)] * PARTS,
+            in_specs=[pl.BlockSpec(memory_space=pltpu.VMEM)] * PARTS,
             out_specs=[pl.BlockSpec(memory_space=pl.ANY), pl.BlockSpec((IMG, PW), lambda i, a: (0, 0))],
             scratch_shapes=[
-                pltpu.VMEM((PARTS, ROWS_W + EXTRA, PW), jnp.bfloat16),
                 pltpu.VMEM((SLOTS * TILE, PW), jnp.bfloat16),
-                pltpu.SemaphoreType.DMA((PARTS,)),
                 pltpu.SemaphoreType.DMA((PARTS,)),
             ],
         ),
@@ -406,7 +388,7 @@
         ],
         compiler_params=VMEM,
         name="finish",
-    )(place, *received)
+    )(part, *received)
 
 
 def pool_kernel(sums_ref, number_ref, pooled_ref, image_ref, out_ref):
@@ -420,6 +402,7 @@
 def pool(sums, number, pooled, image):
     return pl.pallas_call(
         pool_kernel,
+        in_specs=[pl.BlockSpec(memory_space=pltpu.VMEM)] * 4,
         out_shape=jax.ShapeDtypeStruct((IMG, PW), jnp.bfloat16),
         name="pool",
     )(sums, number, pooled, image)
@@ -435,15 +418,15 @@
 def whole_block(patches, dest_owner, dest_slot, packed_image, w_query, w_key, w_value, w_out):
     senders = lax.axis_size("dp")
     splits = lax.axis_size("mp")
-    mp = lax.axis_index("mp").astype(jnp.int32)
-    core = (lax.axis_index("dp") % 2).astype(jnp.int32)
-    place = jnp.stack([mp, core])
+    part = lax.axis_index("mp").astype(jnp.int32).reshape(1)
+    core = (lax.axis_index("dp").astype(jnp.int32) & 1).reshape(1)
+    near = lambda array: pltpu.with_memory_space_constraint(array, pltpu.VMEM)
     shift = lambda d: [(i, (i + d) % splits) for i in range(splits)]
     swap = [(i, i ^ 1) for i in range(senders)]
 
     own = (w_query, w_key, w_value, w_out)
     image = packed_image.reshape(1, SLOTS)
-    outgoing, s0, s1 = send_pack(dest_owner, dest_slot, place, image, patches, own, senders)
+    outgoing, s0, s1 = send_pack(dest_owner, dest_slot, part, core, image, patches, own, senders)
     a0, a1 = (lax.ppermute(s, "mp", shift(1)) for s in (s0, s1))
     b0, b1 = (lax.ppermute(s, "mp", shift(-1)) for s in (s0, s1))
     c0 = lax.ppermute(a0, "mp", shift(1))
@@ -452,16 +435,16 @@
     weights = own + (a0, a1, a0x, a1x, b0, b1, b0x, b1x, c0, c1, c0x, c1x)
 
     incoming = lax.all_to_all(outgoing, "dp", split_axis=0, concat_axis=0, tiled=True)
-    *windows, number = arrive_sort(place[:1], incoming)
+    *windows, number = arrive_sort(part, near(incoming))
     rows = [windows[0]] + passed_on(windows, shift)
-    outcome = block(place, packed_image, rows, weights)
+    outcome = block(part, core, packed_image, [near(r) for r in rows], weights)
     results, sums = outcome[:PARTS], outcome[PARTS:]
     total = sums[0] + sum(lax.ppermute(sums[d], "mp", shift(d)) for d in (1, 2, 3))
     received = [results[0]] + passed_on(results, shift)
     spread = jnp.broadcast_to(total.reshape(1, 2, PW // 2), (senders, 2, PW // 2))
     gathered = lax.all_to_all(spread, "dp", split_axis=0, concat_axis=0, tiled=True)
-    packed_out, pooled = finish(place[:1], received)
-    pooled_out = pool(gathered, number, pooled, image)
+    packed_out, pooled = finish(part, [near(r) for r in received])
+    pooled_out = pool(near(gathered), number, pooled, image)
     return (packed_out, pooled_out)
 
 

time: 161 us -> 153 us (0.950)
  Pallas kernels: 38 us -> 31.9 us
  local copies, waits for them, and re-layouts: 4.36 us -> 2.63 us
    pallas_call x1, Pallas kernels: 24.8 us -> 21.6 us  [block(): pl.pallas_call(block_kernel, grid_spec=pltpu.PrefetchScalarGridSpec(num_s...]
    unnamed x26 -> x14, local copies, waits for them, and re-layouts: 3.71 us -> 2 us
  transfers between devices with their start and end apart: 23 -> 23, of which waited for: 9 -> 9; matrix products, arithmetic and copies ran while one was open for 1% -> 1% of each run, Pallas kernels for 4% -> 3%
where the time goes in v5:
time: 153 us
  waiting for transfers between devices  69.3 us (45%)
  starting transfers between devices  47.8 us (31%)
  Pallas kernels  31.9 us (21%)
  local copies, waits for them, and re-layouts  2.63 us (2%)
    pallas_call x1, Pallas kernels, block(): pl.pallas_call(block_kernel, grid_spec=pltpu.PrefetchScalarGridSpec(num_s...  21.6 us
    ppermute x3, waiting for transfers between devices, whole_block(): lax.ppermute(sums[d], 'mp', shift(d))  18.4 us
    ppermute x6, waiting for transfers between devices, passed_on(): got.append(lax.ppermute(pieces[d], 'mp', shift(d)))  17.5 us
    ppermute x2, waiting for transfers between devices, whole_block(): b0, b1 = (lax.ppermute(s, 'mp', shift(-1)) for s in (s0, s1))  16.6 us
    all_to_all x1, starting transfers between devices, whole_block(): lax.all_to_all(outgoing, 'dp', split_axis=0, concat_axis=0, tiled=True)  13.2 us
    all_to_all x1, starting transfers between devices, whole_block(): lax.all_to_all(spread, 'dp', split_axis=0, concat_axis=0, tiled=True)  10 us
    ppermute x1, waiting for transfers between devices, whole_block(): c0 = lax.ppermute(a0, 'mp', shift(1))  8.45 us
    ppermute x6, starting transfers between devices, passed_on(): got.append(lax.ppermute(pieces[d], 'mp', shift(d)))  7.71 us
  transfers between devices with their start and end apart: 23, of which 9 were waited for; matrix products, arithmetic and copies ran while one was open for 1% of the time, Pallas kernels for 3%

profile of v5, /device:TPU:1, one launch (start us, length us, event | category | flops | bytes accessed | tf_op | source)
XLA Modules:
  0.0 153.0 jit_solution(11490729289544484792)
XLA Ops:
  0.6 4.6 %send_pack.1 = (bf16[64,72,128]{2,1,0:T(8,128)(2,1)}, bf16[1024,256]{1,0:T(8,128)(2,1)}, bf16[1024,256]{1,0:T(8,128)(2,1)}) custom-call(s32[128]{0:T(128)} %owner_ref.1, s32[128]{0:T(128)} %slot_ref.1, s32[1]{0:T(128)} %bitcast.mp_ref.part_ref, s32[1]{0:T(128)} %bitcast.1.core_ref, s32[1,128]{1,0:T(1,128)} %bitcast.4, bf16[2048,1024]{1,0:T(8,128)(2,1)} %patch_ref.1, ...), custom_call_target="tpu_custom_call" | custom-call | tf_op jit(solution)/shard_map/send_pack/pallas_call | solution.py:86
  5.2 13.2 %all-to-all-start = ((bf16[64,72,128]{2,1,0:T(8,128)(2,1)}), bf16[64,72,128]{2,1,0:T(8,128)(2,1)S(1)}, u32[]{:S(2)}, u32[]{:S(2)}) async-start(bf16[64,72,128]{2,1,0:T(8,128)(2,1)} %get-tuple-element.20), calls=%async_computation | async-start | bytes 2359296 | tf_op jit(solution)/shard_map/all_to_all | solution.py:437
  18.4 2.6 %collective-permute-start.7 = (bf16[1024,256]{1,0:T(8,128)(2,1)}, bf16[1024,256]{1,0:T(8,128)(2,1)S(1)}, u32[]{:S(2)}, u32[]{:S(2)}) collective-permute-start(bf16[1024,256]{1,0:T(8,128)(2,1)} %get-tuple-element.25), channel_id=1, source_target_pairs={{0,3},{1,0},{2,1},{3,2},{4,7},{5,4},{6,5},{7,6},{8,11},{9,8},{10,9... | collective-permute-start | bytes 1572872 | tf_op jit(solution)/shard_map/ppermute | solution.py:431
  20.9 0.0 collective-permute-start.3
  20.9 2.7 %collective-permute-start.8 = (bf16[1024,256]{1,0:T(8,128)(2,1)}, bf16[1024,256]{1,0:T(8,128)(2,1)S(1)}, u32[]{:S(2)}, u32[]{:S(2)}) collective-permute-start(bf16[1024,256]{1,0:T(8,128)(2,1)} %get-tuple-element.26), channel_id=1, source_target_pairs={{0,3},{1,0},{2,1},{3,2},{4,7},{5,4},{6,5},{7,6},{8,11},{9,8},{10,9... | collective-permute-start | bytes 1572872 | tf_op jit(solution)/shard_map/ppermute | solution.py:431
  23.6 0.0 collective-permute-start.4
  23.6 8.5 %collective-permute-done.7.b0 = bf16[1024,256]{1,0:T(8,128)(2,1)S(1)} collective-permute-done((bf16[1024,256]{1,0:T(8,128)(2,1)}, bf16[1024,256]{1,0:T(8,128)(2,1)S(1)}, u32[]{:S(2)}, u32[]{:S(2)}) %collective-permute-start.7) | collective-permute-done | bytes 524320 | tf_op jit(solution)/shard_map/ppermute | solution.py:431
  32.1 0.0 copy-start.2
  32.1 2.2 %collective-permute-start.9 = (bf16[1024,256]{1,0:T(8,128)(2,1)S(1)}, bf16[1024,256]{1,0:T(8,128)(2,1)S(1)}, u32[]{:S(2)}, u32[]{:S(2)}) collective-permute-start(bf16[1024,256]{1,0:T(8,128)(2,1)S(1)} %collective-permute-done.7.b0), channel_id=1, source_target_pairs={{0,4},{4,0},{8,12},{12,8},{16,20},{20,16},{24,28},{28,24},{32,36},... | collective-permute-start | bytes 1572872 | tf_op jit(solution)/shard_map/ppermute | solution.py:434
  34.3 0.8 collective-permute-done.3.a0
  35.1 0.0 copy-start.3
  35.1 0.0 collective-permute-start.11
  35.1 8.2 %collective-permute-done.8.b1 = bf16[1024,256]{1,0:T(8,128)(2,1)S(1)} collective-permute-done((bf16[1024,256]{1,0:T(8,128)(2,1)}, bf16[1024,256]{1,0:T(8,128)(2,1)S(1)}, u32[]{:S(2)}, u32[]{:S(2)}) %collective-permute-start.8) | collective-permute-done | bytes 524320 | tf_op jit(solution)/shard_map/ppermute | solution.py:431
  43.3 3.3 %collective-permute-start.12 = (bf16[1024,256]{1,0:T(8,128)(2,1)S(1)}, bf16[1024,256]{1,0:T(8,128)(2,1)}, u32[]{:S(2)}, u32[]{:S(2)}) collective-permute-start(bf16[1024,256]{1,0:T(8,128)(2,1)S(1)} %collective-permute-done.8.b1), channel_id=1, source_target_pairs={{0,3},{1,0},{2,1},{3,2},{4,7},{5,4},{6,5},{7,6},{8,11},{9,8},{10,9... | collective-permute-start | bytes 1572872 | tf_op jit(solution)/shard_map/ppermute | solution.py:433
  46.6 1.6 %collective-permute-start.5 = (bf16[1024,256]{1,0:T(8,128)(2,1)S(1)}, bf16[1024,256]{1,0:T(8,128)(2,1)}, u32[]{:S(2)}, u32[]{:S(2)}) collective-permute-start(bf16[1024,256]{1,0:T(8,128)(2,1)S(1)} %collective-permute-done.3.a0), channel_id=1, source_target_pairs={{0,4},{4,0},{8,12},{12,8},{16,20},{20,16},{24,28},{28,24},{32,36},... | collective-permute-start | bytes 1572872 | tf_op jit(solution)/shard_map/ppermute | solution.py:434
  48.2 0.0 collective-permute-done.4.a1
  48.2 0.9 collective-permute-start.10
  49.1 0.0 collective-permute-done.9.b0x
  49.1 0.1 collective-permute-start.6
  49.2 8.5 %collective-permute-done.11.c0 = bf16[1024,256]{1,0:T(8,128)(2,1)} collective-permute-done((bf16[1024,256]{1,0:T(8,128)(2,1)S(1)}, bf16[1024,256]{1,0:T(8,128)(2,1)}, u32[]{:S(2)}, u32[]{:S(2)}) %collective-permute-start.11) | collective-permute-done | bytes 524320 | tf_op jit(solution)/shard_map/ppermute | solution.py:432
  57.7 1.6 %collective-permute-start.13 = (bf16[1024,256]{1,0:T(8,128)(2,1)}, bf16[1024,256]{1,0:T(8,128)(2,1)}, u32[]{:S(2)}, u32[]{:S(2)}) collective-permute-start(bf16[1024,256]{1,0:T(8,128)(2,1)} %collective-permute-done.11.c0), channel_id=1, source_target_pairs={{0,4},{4,0},{8,12},{12,8},{16,20},{20,16},{24,28},{28,24},{32,36},... | collective-permute-start | bytes 1572872 | tf_op jit(solution)/shard_map/ppermute | solution.py:434
  59.3 0.0 collective-permute-done.12.c1
  59.3 0.0 copy-done.6
  59.3 0.1 collective-permute-start.14
  59.4 0.0 all-to-all-done.in_ref
  59.4 2.7 %arrive_sort.1 = (bf16[752,256]{1,0:T(8,128)(2,1)}, bf16[752,256]{1,0:T(8,128)(2,1)}, bf16[752,256]{1,0:T(8,128)(2,1)}, bf16[752,256]{1,0:T(8,128)(2,1)}, f32[8,128]{1,0:T(8,128)}) custom-call(s32[1]{0:T(128)} %bitcast.mp_ref.part_ref, bf16[64,72,128]{2,1,0:T(8,128)(2,1)S(1)} %all-to-all-done.in_ref), custom_call_target="tpu_custom_call" | custom-call | tf_op jit(solution)/shard_map/arrive_sort/pallas_call | solution.py:151
  62.1 0.0 collective-permute-done.5.a0x
  62.1 0.1 collective-permute-start
  62.2 0.0 collective-permute-done.10.b1x
  62.2 4.1 %collective-permute-start.1 = (bf16[752,256]{1,0:T(8,128)(2,1)}, bf16[752,256]{1,0:T(8,128)(2,1)S(1)}, u32[]{:S(2)}, u32[]{:S(2)}) collective-permute-start(bf16[752,256]{1,0:T(8,128)(2,1)} %get-tuple-element.23), channel_id=1, source_target_pairs={{0,2},{1,3},{2,0},{3,1},{4,6},{5,7},{6,4},{7,5},{8,10},{9,11},{10,... | collective-permute-start | bytes 1155080 | tf_op jit(solution)/shard_map/ppermute | solution.py:414
  66.3 0.0 collective-permute-done.6.a1x
  66.3 0.0 collective-permute-start.2
  66.3 0.0 collective-permute-done.13.c0x
  66.3 0.0 collective-permute-done.14.c1x
  66.3 7.9 %collective-permute-done.x1 = bf16[752,256]{1,0:T(8,128)(2,1)S(1)} collective-permute-done((bf16[752,256]{1,0:T(8,128)(2,1)}, bf16[752,256]{1,0:T(8,128)(2,1)S(1)}, u32[]{:S(2)}, u32[]{:S(2)}) %collective-permute-start) | collective-permute-done | bytes 385056 | tf_op jit(solution)/shard_map/ppermute | solution.py:414
  74.1 9.6 %collective-permute-done.1.x2 = bf16[752,256]{1,0:T(8,128)(2,1)S(1)} collective-permute-done((bf16[752,256]{1,0:T(8,128)(2,1)}, bf16[752,256]{1,0:T(8,128)(2,1)S(1)}, u32[]{:S(2)}, u32[]{:S(2)}) %collective-permute-start.1) | collective-permute-done | bytes 385056 | tf_op jit(solution)/shard_map/ppermute | solution.py:414
  83.7 0.0 collective-permute-done.2.x3
  83.7 0.0 copy-done.2
  83.7 0.0 copy-done.3
  83.8 0.0 copy-done.4
  83.8 0.0 copy-done.5
  83.8 0.0 copy-start.1
  83.8 1.0 copy-done.1
  84.8 21.6 %block.1 = (bf16[800,256]{1,0:T(8,128)(2,1)}, bf16[800,256]{1,0:T(8,128)(2,1)}, bf16[800,256]{1,0:T(8,128)(2,1)}, bf16[800,256]{1,0:T(8,128)(2,1)}, f32[1,256]{1...) custom-call(s32[1]{0:T(128)} %bitcast.mp_ref.part_ref, s32[1]{0:T(128)} %bitcast.1.core_ref, ...), custom_call_target="tpu_custom_call" | custom-call | tf_op jit(solution)/shard_map/block/pallas_call | solution.py:323
  106.3 0.4 collective-permute-start.15
  106.8 3.1 %collective-permute-start.16 = (bf16[800,256]{1,0:T(8,128)(2,1)}, bf16[800,256]{1,0:T(8,128)(2,1)S(1)}, u32[]{:S(2)}, u32[]{:S(2)}) collective-permute-start(bf16[800,256]{1,0:T(8,128)(2,1)} %get-tuple-element.29), channel_id=1, source_target_pairs={{0,2},{1,3},{2,0},{3,1},{4,6},{5,7},{6,4},{7,5},{8,10},{9,11},{10,... | collective-permute-start | bytes 1228808 | tf_op jit(solution)/shard_map/ppermute | solution.py:414
  109.9 0.0 collective-permute-start.17
  109.9 1.5 collective-permute-start.18
  111.3 0.1 collective-permute-start.19
  111.5 16.1 %collective-permute-done.18 = f32[1,256]{1,0:T(1,128)S(1)} collective-permute-done((f32[1,256]{1,0:T(1,128)}, f32[1,256]{1,0:T(1,128)S(1)}, u32[]{:S(2)}, u32[]{:S(2)}) %collective-permute-start.18) | collective-permute-done | bytes 1056 | tf_op jit(solution)/shard_map/ppermute | solution.py:442
  127.5 0.2 collective-permute-start.20
  127.8 0.0 collective-permute-done.19
  127.8 2.4 %collective-permute-done.20 = f32[1,256]{1,0:T(1,128)S(1)} collective-permute-done((f32[1,256]{1,0:T(1,128)}, f32[1,256]{1,0:T(1,128)S(1)}, u32[]{:S(2)}, u32[]{:S(2)}) %collective-permute-start.20) | collective-permute-done | bytes 1056 | tf_op jit(solution)/shard_map/ppermute | solution.py:442
  130.2 0.7 add_add_fusion
  130.8 0.6 broadcast_in_dim.8
  131.5 10.0 %all-to-all-start.1 = ((f32[64,2,128]{2,1,0:T(2,128)}), f32[64,2,128]{2,1,0:T(2,128)S(1)}, u32[]{:S(2)}, u32[]{:S(2)}) async-start(f32[64,2,128]{2,1,0:T(2,128)} %broadcast_in_dim.8), calls=%async_computation.1 | async-start | bytes 131072 | tf_op jit(solution)/shard_map/all_to_all | solution.py:445
  141.5 0.0 collective-permute-done.15.r1
  141.5 0.0 collective-permute-done.16.r2
  141.5 0.0 collective-permute-done.17.r3
  141.5 0.0 copy-start
  141.5 1.0 copy-done
  142.5 1.6 %finish.1 = (bf16[2048,256]{1,0:T(8,128)(2,1)}, f32[16,256]{1,0:T(8,128)}) custom-call(s32[1]{0:T(128)} %bitcast.mp_ref.part_ref, bf16[800,256]{1,0:T(8,128)(2,1)S(1)} %copy-done, bf16[800,256]{1,0:T(8,128)(2,1)S(1)} %collective-permute-done.15.r1, bf16[800,256]{1,0:T(8,128)(2,1)S(1)} %collective-permute-done.16.r2, ...), custom_call_target="tpu_custom_call" | custom-call | tf_op jit(solution)/shard_map/finish/pallas_call | solution.py:373
  144.2 7.4 %all-to-all-done.1.sums_ref = f32[64,2,128]{2,1,0:T(2,128)S(1)} async-done(((f32[64,2,128]{2,1,0:T(2,128)}), f32[64,2,128]{2,1,0:T(2,128)S(1)}, u32[]{:S(2)}, u32[]{:S(2)}) %all-to-all-start.1) | async-done | bytes 65568 | tf_op jit(solution)/shard_map/all_to_all | solution.py:445
  151.6 1.4 pool.1
  (3 shorter events, 0.0 us)
Async XLA Ops:
  5.2 54.2 %all-to-all-start = ((bf16[64,72,128]{2,1,0:T(8,128)(2,1)}), bf16[64,72,128]{2,1,0:T(8,128)(2,1)S(1)}, u32[]{:S(2)}, u32[]{:S(2)}) async-start(bf16[64,72,128]{2,1,0:T(8,128)(2,1)} %get-tuple-element.20), calls=%async_computation | async-start | bytes 2359296 | tf_op jit(solution)/shard_map/all_to_all | solution.py:437
  18.4 13.7 %collective-permute-start.7 = (bf16[1024,256]{1,0:T(8,128)(2,1)}, bf16[1024,256]{1,0:T(8,128)(2,1)S(1)}, u32[]{:S(2)}, u32[]{:S(2)}) collective-permute-start(bf16[1024,256]{1,0:T(8,128)(2,1)} %get-tuple-element.25), channel_id=1, source_target_pairs={{0,3},{1,0},{2,1},{3,2},{4,7},{5,4},{6,5},{7,6},{8,11},{9,8},{10,9... | collective-permute-start | bytes 1572872 | tf_op jit(solution)/shard_map/ppermute | solution.py:431
  20.9 14.2 %collective-permute-start.3 = (bf16[1024,256]{1,0:T(8,128)(2,1)}, bf16[1024,256]{1,0:T(8,128)(2,1)S(1)}, u32[]{:S(2)}, u32[]{:S(2)}) collective-permute-start(bf16[1024,256]{1,0:T(8,128)(2,1)} %get-tuple-element.25), channel_id=1, source_target_pairs={{0,1},{1,2},{2,3},{3,0},{4,5},{5,6},{6,7},{7,4},{8,9},{9,10},{10,1... | collective-permute-start | bytes 1572872 | tf_op jit(solution)/shard_map/ppermute | solution.py:430
  20.9 22.4 %collective-permute-start.8 = (bf16[1024,256]{1,0:T(8,128)(2,1)}, bf16[1024,256]{1,0:T(8,128)(2,1)S(1)}, u32[]{:S(2)}, u32[]{:S(2)}) collective-permute-start(bf16[1024,256]{1,0:T(8,128)(2,1)} %get-tuple-element.26), channel_id=1, source_target_pairs={{0,3},{1,0},{2,1},{3,2},{4,7},{5,4},{6,5},{7,6},{8,11},{9,8},{10,9... | collective-permute-start | bytes 1572872 | tf_op jit(solution)/shard_map/ppermute | solution.py:431
  23.6 24.6 %collective-permute-start.4 = (bf16[1024,256]{1,0:T(8,128)(2,1)}, bf16[1024,256]{1,0:T(8,128)(2,1)S(1)}, u32[]{:S(2)}, u32[]{:S(2)}) collective-permute-start(bf16[1024,256]{1,0:T(8,128)(2,1)} %get-tuple-element.26), channel_id=1, source_target_pairs={{0,1},{1,2},{2,3},{3,0},{4,5},{5,6},{6,7},{7,4},{8,9},{9,10},{10,1... | collective-permute-start | bytes 1572872 | tf_op jit(solution)/shard_map/ppermute | solution.py:430
  32.1 51.7 %copy-start.2 = (bf16[1024,256]{1,0:T(8,128)(2,1)}, bf16[1024,256]{1,0:T(8,128)(2,1)S(1)}, u32[]{:S(2)}) copy-start(bf16[1024,256]{1,0:T(8,128)(2,1)S(1)} %collective-permute-done.7.b0) | copy-start | bytes 1572868
  32.1 17.0 %collective-permute-start.9 = (bf16[1024,256]{1,0:T(8,128)(2,1)S(1)}, bf16[1024,256]{1,0:T(8,128)(2,1)S(1)}, u32[]{:S(2)}, u32[]{:S(2)}) collective-permute-start(bf16[1024,256]{1,0:T(8,128)(2,1)S(1)} %collective-permute-done.7.b0), channel_id=1, source_target_pairs={{0,4},{4,0},{8,12},{12,8},{16,20},{20,16},{24,28},{28,24},{32,36},... | collective-permute-start | bytes 1572872 | tf_op jit(solution)/shard_map/ppermute | solution.py:434
  35.1 48.6 %copy-start.3 = (bf16[1024,256]{1,0:T(8,128)(2,1)}, bf16[1024,256]{1,0:T(8,128)(2,1)S(1)}, u32[]{:S(2)}) copy-start(bf16[1024,256]{1,0:T(8,128)(2,1)S(1)} %collective-permute-done.3.a0) | copy-start | bytes 1572868
  35.1 22.6 %collective-permute-start.11 = (bf16[1024,256]{1,0:T(8,128)(2,1)S(1)}, bf16[1024,256]{1,0:T(8,128)(2,1)}, u32[]{:S(2)}, u32[]{:S(2)}) collective-permute-start(bf16[1024,256]{1,0:T(8,128)(2,1)S(1)} %collective-permute-done.3.a0), channel_id=1, source_target_pairs={{0,1},{1,2},{2,3},{3,0},{4,5},{5,6},{6,7},{7,4},{8,9},{9,10},{10,1... | collective-permute-start | bytes 1572872 | tf_op jit(solution)/shard_map/ppermute | solution.py:432
  43.3 40.4 %copy-start.4 = (bf16[1024,256]{1,0:T(8,128)(2,1)}, bf16[1024,256]{1,0:T(8,128)(2,1)S(1)}, u32[]{:S(2)}) copy-start(bf16[1024,256]{1,0:T(8,128)(2,1)S(1)} %collective-permute-done.8.b1) | copy-start | bytes 1572868
  43.3 16.0 %collective-permute-start.12 = (bf16[1024,256]{1,0:T(8,128)(2,1)S(1)}, bf16[1024,256]{1,0:T(8,128)(2,1)}, u32[]{:S(2)}, u32[]{:S(2)}) collective-permute-start(bf16[1024,256]{1,0:T(8,128)(2,1)S(1)} %collective-permute-done.8.b1), channel_id=1, source_target_pairs={{0,3},{1,0},{2,1},{3,2},{4,7},{5,4},{6,5},{7,6},{8,11},{9,8},{10,9... | collective-permute-start | bytes 1572872 | tf_op jit(solution)/shard_map/ppermute | solution.py:433
  46.6 15.5 %collective-permute-start.5 = (bf16[1024,256]{1,0:T(8,128)(2,1)S(1)}, bf16[1024,256]{1,0:T(8,128)(2,1)}, u32[]{:S(2)}, u32[]{:S(2)}) collective-permute-start(bf16[1024,256]{1,0:T(8,128)(2,1)S(1)} %collective-permute-done.3.a0), channel_id=1, source_target_pairs={{0,4},{4,0},{8,12},{12,8},{16,20},{20,16},{24,28},{28,24},{32,36},... | collective-permute-start | bytes 1572872 | tf_op jit(solution)/shard_map/ppermute | solution.py:434
  48.2 35.5 %copy-start.5 = (bf16[1024,256]{1,0:T(8,128)(2,1)}, bf16[1024,256]{1,0:T(8,128)(2,1)S(1)}, u32[]{:S(2)}) copy-start(bf16[1024,256]{1,0:T(8,128)(2,1)S(1)} %collective-permute-done.4.a1) | copy-start | bytes 1572868
  48.2 14.0 %collective-permute-start.10 = (bf16[1024,256]{1,0:T(8,128)(2,1)S(1)}, bf16[1024,256]{1,0:T(8,128)(2,1)}, u32[]{:S(2)}, u32[]{:S(2)}) collective-permute-start(bf16[1024,256]{1,0:T(8,128)(2,1)S(1)} %collective-permute-done.8.b1), channel_id=1, source_target_pairs={{0,4},{4,0},{8,12},{12,8},{16,20},{20,16},{24,28},{28,24},{32,36},... | collective-permute-start | bytes 1572872 | tf_op jit(solution)/shard_map/ppermute | solution.py:434
  49.1 10.2 %copy-start.6 = (bf16[1024,256]{1,0:T(8,128)(2,1)}, bf16[1024,256]{1,0:T(8,128)(2,1)S(1)}, u32[]{:S(2)}) copy-start(bf16[1024,256]{1,0:T(8,128)(2,1)S(1)} %collective-permute-done.9.b0x) | copy-start | bytes 1572868
  49.1 17.1 %collective-permute-start.6 = (bf16[1024,256]{1,0:T(8,128)(2,1)S(1)}, bf16[1024,256]{1,0:T(8,128)(2,1)}, u32[]{:S(2)}, u32[]{:S(2)}) collective-permute-start(bf16[1024,256]{1,0:T(8,128)(2,1)S(1)} %collective-permute-done.4.a1), channel_id=1, source_target_pairs={{0,4},{4,0},{8,12},{12,8},{16,20},{20,16},{24,28},{28,24},{32,36},... | collective-permute-start | bytes 1572872 | tf_op jit(solution)/shard_map/ppermute | solution.py:434
  57.7 8.6 %collective-permute-start.13 = (bf16[1024,256]{1,0:T(8,128)(2,1)}, bf16[1024,256]{1,0:T(8,128)(2,1)}, u32[]{:S(2)}, u32[]{:S(2)}) collective-permute-start(bf16[1024,256]{1,0:T(8,128)(2,1)} %collective-permute-done.11.c0), channel_id=1, source_target_pairs={{0,4},{4,0},{8,12},{12,8},{16,20},{20,16},{24,28},{28,24},{32,36},... | collective-permute-start | bytes 1572872 | tf_op jit(solution)/shard_map/ppermute | solution.py:434
  59.3 7.0 %collective-permute-start.14 = (bf16[1024,256]{1,0:T(8,128)(2,1)}, bf16[1024,256]{1,0:T(8,128)(2,1)}, u32[]{:S(2)}, u32[]{:S(2)}) collective-permute-start(bf16[1024,256]{1,0:T(8,128)(2,1)} %collective-permute-done.12.c1), channel_id=1, source_target_pairs={{0,4},{4,0},{8,12},{12,8},{16,20},{20,16},{24,28},{28,24},{32,36},... | collective-permute-start | bytes 1572872 | tf_op jit(solution)/shard_map/ppermute | solution.py:434
  62.1 12.1 %collective-permute-start = (bf16[752,256]{1,0:T(8,128)(2,1)}, bf16[752,256]{1,0:T(8,128)(2,1)S(1)}, u32[]{:S(2)}, u32[]{:S(2)}) collective-permute-start(bf16[752,256]{1,0:T(8,128)(2,1)} %get-tuple-element.22), channel_id=1, source_target_pairs={{0,1},{1,2},{2,3},{3,0},{4,5},{5,6},{6,7},{7,4},{8,9},{9,10},{10,1... | collective-permute-start | bytes 1155080 | tf_op jit(solution)/shard_map/ppermute | solution.py:414
  62.2 21.6 %collective-permute-start.1 = (bf16[752,256]{1,0:T(8,128)(2,1)}, bf16[752,256]{1,0:T(8,128)(2,1)S(1)}, u32[]{:S(2)}, u32[]{:S(2)}) collective-permute-start(bf16[752,256]{1,0:T(8,128)(2,1)} %get-tuple-element.23), channel_id=1, source_target_pairs={{0,2},{1,3},{2,0},{3,1},{4,6},{5,7},{6,4},{7,5},{8,10},{9,11},{10,... | collective-permute-start | bytes 1155080 | tf_op jit(solution)/shard_map/ppermute | solution.py:414
  66.3 17.5 %collective-permute-start.2 = (bf16[752,256]{1,0:T(8,128)(2,1)}, bf16[752,256]{1,0:T(8,128)(2,1)S(1)}, u32[]{:S(2)}, u32[]{:S(2)}) collective-permute-start(bf16[752,256]{1,0:T(8,128)(2,1)} %get-tuple-element.24), channel_id=1, source_target_pairs={{0,3},{1,0},{2,1},{3,2},{4,7},{5,4},{6,5},{7,6},{8,11},{9,8},{10,9... | collective-permute-start | bytes 1155080 | tf_op jit(solution)/shard_map/ppermute | solution.py:414
  83.8 1.0 copy-start.1
  106.3 35.2 %collective-permute-start.15 = (bf16[800,256]{1,0:T(8,128)(2,1)}, bf16[800,256]{1,0:T(8,128)(2,1)S(1)}, u32[]{:S(2)}, u32[]{:S(2)}) collective-permute-start(bf16[800,256]{1,0:T(8,128)(2,1)} %get-tuple-element.28), channel_id=1, source_target_pairs={{0,1},{1,2},{2,3},{3,0},{4,5},{5,6},{6,7},{7,4},{8,9},{9,10},{10,1... | collective-permute-start | bytes 1228808 | tf_op jit(solution)/shard_map/ppermute | solution.py:414
  106.8 34.8 %collective-permute-start.16 = (bf16[800,256]{1,0:T(8,128)(2,1)}, bf16[800,256]{1,0:T(8,128)(2,1)S(1)}, u32[]{:S(2)}, u32[]{:S(2)}) collective-permute-start(bf16[800,256]{1,0:T(8,128)(2,1)} %get-tuple-element.29), channel_id=1, source_target_pairs={{0,2},{1,3},{2,0},{3,1},{4,6},{5,7},{6,4},{7,5},{8,10},{9,11},{10,... | collective-permute-start | bytes 1228808 | tf_op jit(solution)/shard_map/ppermute | solution.py:414
  109.9 31.6 %collective-permute-start.17 = (bf16[800,256]{1,0:T(8,128)(2,1)}, bf16[800,256]{1,0:T(8,128)(2,1)S(1)}, u32[]{:S(2)}, u32[]{:S(2)}) collective-permute-start(bf16[800,256]{1,0:T(8,128)(2,1)} %get-tuple-element.30), channel_id=1, source_target_pairs={{0,3},{1,0},{2,1},{3,2},{4,7},{5,4},{6,5},{7,6},{8,11},{9,8},{10,9... | collective-permute-start | bytes 1228808 | tf_op jit(solution)/shard_map/ppermute | solution.py:414
  109.9 17.6 %collective-permute-start.18 = (f32[1,256]{1,0:T(1,128)}, f32[1,256]{1,0:T(1,128)S(1)}, u32[]{:S(2)}, u32[]{:S(2)}) collective-permute-start(f32[1,256]{1,0:T(1,128)} %get-tuple-element.33), channel_id=1, source_target_pairs={{0,1},{1,2},{2,3},{3,0},{4,5},{5,6},{6,7},{7,4},{8,9},{9,10},{10,1... | collective-permute-start | bytes 3080 | tf_op jit(solution)/shard_map/ppermute | solution.py:442
  111.3 16.4 %collective-permute-start.19 = (f32[1,256]{1,0:T(1,128)}, f32[1,256]{1,0:T(1,128)S(1)}, u32[]{:S(2)}, u32[]{:S(2)}) collective-permute-start(f32[1,256]{1,0:T(1,128)} %get-tuple-element.34), channel_id=1, source_target_pairs={{0,2},{1,3},{2,0},{3,1},{4,6},{5,7},{6,4},{7,5},{8,10},{9,11},{10,... | collective-permute-start | bytes 3080 | tf_op jit(solution)/shard_map/ppermute | solution.py:442
  127.5 2.6 %collective-permute-start.20 = (f32[1,256]{1,0:T(1,128)}, f32[1,256]{1,0:T(1,128)S(1)}, u32[]{:S(2)}, u32[]{:S(2)}) collective-permute-start(f32[1,256]{1,0:T(1,128)} %get-tuple-element.35), channel_id=1, source_target_pairs={{0,3},{1,0},{2,1},{3,2},{4,7},{5,4},{6,5},{7,6},{8,11},{9,8},{10,9... | collective-permute-start | bytes 3080 | tf_op jit(solution)/shard_map/ppermute | solution.py:442
  131.5 20.1 %all-to-all-start.1 = ((f32[64,2,128]{2,1,0:T(2,128)}), f32[64,2,128]{2,1,0:T(2,128)S(1)}, u32[]{:S(2)}, u32[]{:S(2)}) async-start(f32[64,2,128]{2,1,0:T(2,128)} %broadcast_in_dim.8), calls=%async_computation.1 | async-start | bytes 131072 | tf_op jit(solution)/shard_map/all_to_all | solution.py:445
  141.5 1.0 copy-start

commit v6 on v5

--- a/solution.py
+++ b/solution.py
@@ -21,6 +21,8 @@
 PAY = 72
 EXP_SCALE = HD ** (-0.5) * 1.4426950408889634
 VMEM = pltpu.CompilerParams(vmem_limit_bytes=56 * 1024 * 1024)
+MIDDLE = pltpu.CompilerParams(vmem_limit_bytes=32 * 1024 * 1024)
+SMALL = pltpu.CompilerParams(vmem_limit_bytes=16 * 1024 * 1024)
 
 
 def send_kernel(owner_ref, slot_ref, mp_ref, core_ref, image_ref, patch_ref, wq, wk, wv, wo, out_ref, s0, s1, count_ref, place_ref, sems):
@@ -108,7 +110,7 @@
     )(owner, slot, part, core, image, patches, *weights)
 
 
-def arrive_kernel(mp_ref, in_ref, out0, out1, out2, out3, total_ref, sorted_ref, label_ref, slot_ref, sems):
+def arrive_kernel(mp_ref, in_ref, out0, out1, out2, out3, total_ref, sorted_ref, label_ref, slot_ref, sem):
     senders = in_ref.shape[0]
     row = lax.broadcasted_iota(jnp.int32, (8, 128), 0)
     lane = lax.broadcasted_iota(jnp.int32, (8, 128), 1)
@@ -121,7 +123,7 @@
     odd = (lane & 1) == 1
     own = jnp.where(row == jnp.where(odd, 1, 0), picked, 0.0)
     label_ref[...] = jnp.broadcast_to(jnp.sum(own, axis=0, keepdims=True), (8, 128)).astype(jnp.int32)
-    copy = pltpu.make_async_copy(label_ref, slot_ref, sems.at[4])
+    copy = pltpu.make_async_copy(label_ref, slot_ref, sem)
     copy.start()
     total_ref[...] = jnp.broadcast_to(jnp.sum(jnp.where(row == 2, total, 0.0), axis=0, keepdims=True), (8, 128))
     sorted_ref[SLOTS * TILE :, :] = jnp.zeros((ROWS_W - PART_SLOTS * TILE, PW), jnp.bfloat16)
@@ -135,15 +137,10 @@
         return carry
 
     lax.fori_loop(0, senders, move, 0, unroll=8)
-    copies = []
     for d, out in enumerate((out0, out1, out2, out3)):
         part = (mp_ref[0] + d) % PARTS
         at = pl.multiple_of(part * PART_SLOTS * TILE, TILE)
-        copies.append(pltpu.make_async_copy(sorted_ref.at[pl.ds(at, ROWS_W), :], out, sems.at[d]))
-    for copy in copies:
-        copy.start()
-    for copy in copies:
-        copy.wait()
+        out[...] = sorted_ref[pl.ds(at, ROWS_W), :]
 
 
 def arrive_sort(mp, incoming):
@@ -154,16 +151,16 @@
             num_scalar_prefetch=1,
             grid=(1,),
             in_specs=[pl.BlockSpec(memory_space=pltpu.VMEM)],
-            out_specs=[pl.BlockSpec(memory_space=pl.ANY)] * PARTS + [pl.BlockSpec((8, 128), lambda i, a: (0, 0))],
+            out_specs=[pl.BlockSpec(memory_space=pltpu.VMEM)] * (PARTS + 1),
             scratch_shapes=[
                 pltpu.VMEM((SLOTS * TILE + ROWS_W - PART_SLOTS * TILE, PW), jnp.bfloat16),
                 pltpu.VMEM((8, 128), jnp.int32),
                 pltpu.SMEM((8, 128), jnp.int32),
-                pltpu.SemaphoreType.DMA((5,)),
+                pltpu.SemaphoreType.DMA,
             ],
         ),
         out_shape=[window] * PARTS + [jax.ShapeDtypeStruct((8, 128), jnp.float32)],
-        compiler_params=VMEM,
+        compiler_params=SMALL,
         name="arrive_sort",
     )(mp, incoming)
 
@@ -313,12 +310,13 @@
         out[ROWS_W : ROWS_W + IMG, :] = one
         out[ROWS_W + IMG : ROWS_W + 2 * IMG, :] = two
         out[ROWS_W + 2 * IMG : ROWS_W + 3 * IMG, :] = three
-        sum_ref[...] = jnp.sum(pooled, axis=0, keepdims=True)
+        line = jnp.sum(pooled, axis=0, keepdims=True)
+        sum_ref[0:1, :] = line[:, : PW // 2]
+        sum_ref[1:2, :] = line[:, PW // 2 :]
 
 
 def block(part, core, image, xs, weights):
     outs = jax.ShapeDtypeStruct((ROWS_W + EXTRA, PW), jnp.bfloat16)
-    whole = lambda i, a, b, c: (0, 0)
     wide = pltpu.VMEM((ROWS_W, PW), jnp.bfloat16)
     return pl.pallas_call(
         block_kernel,
@@ -326,8 +324,8 @@
             num_scalar_prefetch=3,
             grid=(1,),
             in_specs=[pl.BlockSpec(memory_space=pltpu.VMEM)] * len(xs)
-            + [pl.BlockSpec(memory_space=pl.ANY)] * len(weights),
-            out_specs=[pl.BlockSpec((ROWS_W + EXTRA, PW), whole)] * PARTS + [pl.BlockSpec((1, PW), whole)] * PARTS,
+            + [pl.BlockSpec(memory_space=pltpu.HBM)] * len(weights),
+            out_specs=[pl.BlockSpec(memory_space=pltpu.VMEM)] * (2 * PARTS),
             scratch_shapes=[
                 pltpu.VMEM((PARTS, ROWS_W, PW), jnp.bfloat16),
                 wide,
@@ -340,8 +338,8 @@
                 pltpu.SemaphoreType.DMA((5 * PARTS - 1,)),
             ],
         ),
-        out_shape=[outs] * PARTS + [jax.ShapeDtypeStruct((1, PW), jnp.float32)] * PARTS,
-        compiler_params=VMEM,
+        out_shape=[outs] * PARTS + [jax.ShapeDtypeStruct((2, PW // 2), jnp.float32)] * PARTS,
+        compiler_params=MIDDLE,
         name="block",
     )(part, core, image, *xs, *weights)
 
@@ -421,6 +419,7 @@
     part = lax.axis_index("mp").astype(jnp.int32).reshape(1)
     core = (lax.axis_index("dp").astype(jnp.int32) & 1).reshape(1)
     near = lambda array: pltpu.with_memory_space_constraint(array, pltpu.VMEM)
+    far = lambda array: pltpu.with_memory_space_constraint(array, pltpu.HBM)
     shift = lambda d: [(i, (i + d) % splits) for i in range(splits)]
     swap = [(i, i ^ 1) for i in range(senders)]
 
@@ -437,11 +436,11 @@
     incoming = lax.all_to_all(outgoing, "dp", split_axis=0, concat_axis=0, tiled=True)
     *windows, number = arrive_sort(part, near(incoming))
     rows = [windows[0]] + passed_on(windows, shift)
-    outcome = block(part, core, packed_image, [near(r) for r in rows], weights)
+    outcome = block(part, core, packed_image, [near(r) for r in rows], [far(w) for w in weights])
     results, sums = outcome[:PARTS], outcome[PARTS:]
     total = sums[0] + sum(lax.ppermute(sums[d], "mp", shift(d)) for d in (1, 2, 3))
     received = [results[0]] + passed_on(results, shift)
-    spread = jnp.broadcast_to(total.reshape(1, 2, PW // 2), (senders, 2, PW // 2))
+    spread = jnp.broadcast_to(total[None], (senders, 2, PW // 2))
     gathered = lax.all_to_all(spread, "dp", split_axis=0, concat_axis=0, tiled=True)
     packed_out, pooled = finish(part, [near(r) for r in received])
     pooled_out = pool(near(gathered), number, pooled, image)

time: 153 us -> 149 us (0.974)
  Pallas kernels: 31.9 us -> 29.3 us
  local copies, waits for them, and re-layouts: 2.63 us -> 0.67 us
    unnamed x14 -> x12, local copies, waits for them, and re-layouts: 2 us -> 0.03 us
    pallas_call x1, Pallas kernels: 2.69 us -> 1.02 us  [arrive_sort(): pl.pallas_call(arrive_kernel, grid_spec=pltpu.PrefetchScalarGridSpec(num_...]
  transfers between devices with their start and end apart: 23 -> 23, of which waited for: 9 -> 9; matrix products, arithmetic and copies ran while one was open for 1% -> 0% of each run, Pallas kernels for 3% -> 2%
where the time goes in v6:
time: 149 us
  waiting for transfers between devices  69.5 us (47%)
  starting transfers between devices  48.5 us (33%)
  Pallas kernels  29.3 us (20%)
    pallas_call x1, Pallas kernels, block(): pl.pallas_call(block_kernel, grid_spec=pltpu.PrefetchScalarGridSpec(num_s...  20.6 us
    ppermute x3, waiting for transfers between devices, whole_block(): lax.ppermute(sums[d], 'mp', shift(d))  18.1 us
    ppermute x6, waiting for transfers between devices, passed_on(): got.append(lax.ppermute(pieces[d], 'mp', shift(d)))  17.3 us
    ppermute x2, waiting for transfers between devices, whole_block(): b0, b1 = (lax.ppermute(s, 'mp', shift(-1)) for s in (s0, s1))  16.5 us
    all_to_all x1, starting transfers between devices, whole_block(): lax.all_to_all(outgoing, 'dp', split_axis=0, concat_axis=0, tiled=True)  13.3 us
    all_to_all x1, starting transfers between devices, whole_block(): lax.all_to_all(spread, 'dp', split_axis=0, concat_axis=0, tiled=True)  10.1 us
    all_to_all x1, waiting for transfers between devices, whole_block(): lax.all_to_all(spread, 'dp', split_axis=0, concat_axis=0, tiled=True)  8.42 us
    ppermute x1, waiting for transfers between devices, whole_block(): c0 = lax.ppermute(a0, 'mp', shift(1))  8.36 us
  transfers between devices with their start and end apart: 23, of which 9 were waited for; matrix products, arithmetic and copies ran while one was open for 0% of the time, Pallas kernels for 2%

profile of v6, /device:TPU:1, one launch (start us, length us, event | category | flops | bytes accessed | tf_op | source)
XLA Modules:
  0.0 148.7 jit_solution(15133355466720558757)
XLA Ops:
  0.6 4.6 %send_pack.1 = (bf16[64,72,128]{2,1,0:T(8,128)(2,1)}, bf16[1024,256]{1,0:T(8,128)(2,1)}, bf16[1024,256]{1,0:T(8,128)(2,1)}) custom-call(s32[128]{0:T(128)} %owner_ref.1, s32[128]{0:T(128)} %slot_ref.1, s32[1]{0:T(128)} %bitcast.mp_ref.part_ref, s32[1]{0:T(128)} %bitcast.1.core_ref, s32[1,128]{1,0:T(1,128)} %bitcast.3, bf16[2048,1024]{1,0:T(8,128)(2,1)} %patch_ref.1, ...), custom_call_target="tpu_custom_call" | custom-call | tf_op jit(solution)/shard_map/send_pack/pallas_call | solution.py:88
  5.2 0.0 copy-start.5
  5.2 13.3 %all-to-all-start = ((bf16[64,72,128]{2,1,0:T(8,128)(2,1)}), bf16[64,72,128]{2,1,0:T(8,128)(2,1)S(1)}, u32[]{:S(2)}, u32[]{:S(2)}) async-start(bf16[64,72,128]{2,1,0:T(8,128)(2,1)} %get-tuple-element.20), calls=%async_computation | async-start | bytes 2359296 | tf_op jit(solution)/shard_map/all_to_all | solution.py:436
  18.5 0.0 copy-start
  18.5 2.6 %collective-permute-start.7 = (bf16[1024,256]{1,0:T(8,128)(2,1)}, bf16[1024,256]{1,0:T(8,128)(2,1)S(1)}, u32[]{:S(2)}, u32[]{:S(2)}) collective-permute-start(bf16[1024,256]{1,0:T(8,128)(2,1)} %get-tuple-element.25), channel_id=1, source_target_pairs={{0,3},{1,0},{2,1},{3,2},{4,7},{5,4},{6,5},{7,6},{8,11},{9,8},{10,9... | collective-permute-start | bytes 1572872 | tf_op jit(solution)/shard_map/ppermute | solution.py:430
  21.1 0.0 collective-permute-start.3
  21.1 0.0 copy-done.5
  21.1 2.7 %collective-permute-start.8 = (bf16[1024,256]{1,0:T(8,128)(2,1)S(1)}, bf16[1024,256]{1,0:T(8,128)(2,1)}, u32[]{:S(2)}, u32[]{:S(2)}) collective-permute-start(bf16[1024,256]{1,0:T(8,128)(2,1)S(1)} %copy-done.5), channel_id=1, source_target_pairs={{0,3},{1,0},{2,1},{3,2},{4,7},{5,4},{6,5},{7,6},{8,11},{9,8},{10,9... | collective-permute-start | bytes 1572872 | tf_op jit(solution)/shard_map/ppermute | solution.py:430
  23.8 0.0 collective-permute-start.4
  23.8 8.5 %collective-permute-done.7.b0 = bf16[1024,256]{1,0:T(8,128)(2,1)S(1)} collective-permute-done((bf16[1024,256]{1,0:T(8,128)(2,1)}, bf16[1024,256]{1,0:T(8,128)(2,1)S(1)}, u32[]{:S(2)}, u32[]{:S(2)}) %collective-permute-start.7) | collective-permute-done | bytes 524320 | tf_op jit(solution)/shard_map/ppermute | solution.py:430
  32.2 0.0 copy-start.2
  32.2 2.2 %collective-permute-start.9 = (bf16[1024,256]{1,0:T(8,128)(2,1)S(1)}, bf16[1024,256]{1,0:T(8,128)(2,1)S(1)}, u32[]{:S(2)}, u32[]{:S(2)}) collective-permute-start(bf16[1024,256]{1,0:T(8,128)(2,1)S(1)} %collective-permute-done.7.b0), channel_id=1, source_target_pairs={{0,4},{4,0},{8,12},{12,8},{16,20},{20,16},{24,28},{28,24},{32,36},... | collective-permute-start | bytes 1572872 | tf_op jit(solution)/shard_map/ppermute | solution.py:433
  34.5 0.8 collective-permute-done.3.a0
  35.3 0.0 copy-start.3
  35.3 0.0 collective-permute-start.11
  35.3 8.1 %collective-permute-done.8.b1 = bf16[1024,256]{1,0:T(8,128)(2,1)} collective-permute-done((bf16[1024,256]{1,0:T(8,128)(2,1)S(1)}, bf16[1024,256]{1,0:T(8,128)(2,1)}, u32[]{:S(2)}, u32[]{:S(2)}) %collective-permute-start.8) | collective-permute-done | bytes 524320 | tf_op jit(solution)/shard_map/ppermute | solution.py:430
  43.4 3.5 %collective-permute-start.12 = (bf16[1024,256]{1,0:T(8,128)(2,1)}, bf16[1024,256]{1,0:T(8,128)(2,1)}, u32[]{:S(2)}, u32[]{:S(2)}) collective-permute-start(bf16[1024,256]{1,0:T(8,128)(2,1)} %collective-permute-done.8.b1), channel_id=1, source_target_pairs={{0,3},{1,0},{2,1},{3,2},{4,7},{5,4},{6,5},{7,6},{8,11},{9,8},{10,9... | collective-permute-start | bytes 1572872 | tf_op jit(solution)/shard_map/ppermute | solution.py:432
  46.9 1.6 %collective-permute-start.5 = (bf16[1024,256]{1,0:T(8,128)(2,1)S(1)}, bf16[1024,256]{1,0:T(8,128)(2,1)}, u32[]{:S(2)}, u32[]{:S(2)}) collective-permute-start(bf16[1024,256]{1,0:T(8,128)(2,1)S(1)} %collective-permute-done.3.a0), channel_id=1, source_target_pairs={{0,4},{4,0},{8,12},{12,8},{16,20},{20,16},{24,28},{28,24},{32,36},... | collective-permute-start | bytes 1572872 | tf_op jit(solution)/shard_map/ppermute | solution.py:433
  48.5 0.0 collective-permute-done.4.a1
  48.5 0.9 collective-permute-start.10
  49.4 0.0 collective-permute-done.9.b0x
  49.4 0.0 copy-start.4
  49.4 0.1 collective-permute-start.6
  49.5 8.4 %collective-permute-done.11.c0 = bf16[1024,256]{1,0:T(8,128)(2,1)} collective-permute-done((bf16[1024,256]{1,0:T(8,128)(2,1)S(1)}, bf16[1024,256]{1,0:T(8,128)(2,1)}, u32[]{:S(2)}, u32[]{:S(2)}) %collective-permute-start.11) | collective-permute-done | bytes 524320 | tf_op jit(solution)/shard_map/ppermute | solution.py:431
  57.8 1.6 %collective-permute-start.13 = (bf16[1024,256]{1,0:T(8,128)(2,1)}, bf16[1024,256]{1,0:T(8,128)(2,1)}, u32[]{:S(2)}, u32[]{:S(2)}) collective-permute-start(bf16[1024,256]{1,0:T(8,128)(2,1)} %collective-permute-done.11.c0), channel_id=1, source_target_pairs={{0,4},{4,0},{8,12},{12,8},{16,20},{20,16},{24,28},{28,24},{32,36},... | collective-permute-start | bytes 1572872 | tf_op jit(solution)/shard_map/ppermute | solution.py:433
  59.4 0.0 collective-permute-done.12.c1
  59.4 0.0 collective-permute-start.14
  59.4 0.0 copy-done.4
  59.4 0.0 all-to-all-done.in_ref
  59.5 1.0 arrive_sort.1
  60.5 0.0 copy-start.1
  60.5 0.0 collective-permute-done.5.a0x
  60.5 0.1 collective-permute-start
  60.6 0.0 collective-permute-done.10.b1x
  60.6 4.5 %collective-permute-start.1 = (bf16[752,256]{1,0:T(8,128)(2,1)S(1)}, bf16[752,256]{1,0:T(8,128)(2,1)S(1)}, u32[]{:S(2)}, u32[]{:S(2)}) collective-permute-start(bf16[752,256]{1,0:T(8,128)(2,1)S(1)} %get-tuple-element.23), channel_id=1, source_target_pairs={{0,2},{1,3},{2,0},{3,1},{4,6},{5,7},{6,4},{7,5},{8,10},{9,11},{10,... | collective-permute-start | bytes 1155080 | tf_op jit(solution)/shard_map/ppermute | solution.py:412
  65.1 0.0 collective-permute-done.6.a1x
  65.1 0.0 collective-permute-start.2
  65.1 0.0 collective-permute-done.13.c0x
  65.1 0.0 collective-permute-done.14.c1x
  65.1 8.0 %collective-permute-done.x1 = bf16[752,256]{1,0:T(8,128)(2,1)S(1)} collective-permute-done((bf16[752,256]{1,0:T(8,128)(2,1)S(1)}, bf16[752,256]{1,0:T(8,128)(2,1)S(1)}, u32[]{:S(2)}, u32[]{:S(2)}) %collective-permute-start) | collective-permute-done | bytes 385056 | tf_op jit(solution)/shard_map/ppermute | solution.py:412
  73.1 9.3 %collective-permute-done.1.x2 = bf16[752,256]{1,0:T(8,128)(2,1)S(1)} collective-permute-done((bf16[752,256]{1,0:T(8,128)(2,1)S(1)}, bf16[752,256]{1,0:T(8,128)(2,1)S(1)}, u32[]{:S(2)}, u32[]{:S(2)}) %collective-permute-start.1) | collective-permute-done | bytes 385056 | tf_op jit(solution)/shard_map/ppermute | solution.py:412
  82.3 0.0 collective-permute-done.2.x3
  82.3 0.0 copy-done.2
  82.4 0.0 copy-done.3
  82.4 0.0 copy-done
  82.4 20.6 %block.1 = (bf16[800,256]{1,0:T(8,128)(2,1)S(1)}, bf16[800,256]{1,0:T(8,128)(2,1)S(1)}, bf16[800,256]{1,0:T(8,128)(2,1)S(1)}, bf16[800,256]{1,0:T(8,128)(2,1)S(1...) custom-call(s32[1]{0:T(128)} %bitcast.mp_ref.part_ref, ...), custom_call_target="tpu_custom_call" | custom-call | tf_op jit(solution)/shard_map/block/pallas_call | solution.py:321
  103.0 0.0 copy-done.1
  103.0 0.4 collective-permute-start.15
  103.4 3.1 %collective-permute-start.16 = (bf16[800,256]{1,0:T(8,128)(2,1)S(1)}, bf16[800,256]{1,0:T(8,128)(2,1)S(1)}, u32[]{:S(2)}, u32[]{:S(2)}) collective-permute-start(bf16[800,256]{1,0:T(8,128)(2,1)S(1)} %get-tuple-element.29), channel_id=1, source_target_pairs={{0,2},{1,3},{2,0},{3,1},{4,6},{5,7},{6,4},{7,5},{8,10},{9,11},{10,... | collective-permute-start | bytes 1228808 | tf_op jit(solution)/shard_map/ppermute | solution.py:412
  106.5 0.0 collective-permute-start.17
  106.5 1.5 collective-permute-start.18
  108.0 0.1 collective-permute-start.19
  108.1 15.9 %collective-permute-done.18 = f32[2,128]{1,0:T(2,128)S(1)} collective-permute-done((f32[2,128]{1,0:T(2,128)S(1)}, f32[2,128]{1,0:T(2,128)S(1)}, u32[]{:S(2)}, u32[]{:S(2)}) %collective-permute-start.18) | collective-permute-done | bytes 1056 | tf_op jit(solution)/shard_map/ppermute | solution.py:441
  124.0 0.2 collective-permute-start.20
  124.2 0.0 collective-permute-done.19
  124.2 2.2 %collective-permute-done.20 = f32[2,128]{1,0:T(2,128)S(1)} collective-permute-done((f32[2,128]{1,0:T(2,128)S(1)}, f32[2,128]{1,0:T(2,128)S(1)}, u32[]{:S(2)}, u32[]{:S(2)}) %collective-permute-start.20) | collective-permute-done | bytes 1056 | tf_op jit(solution)/shard_map/ppermute | solution.py:441
  126.4 0.6 broadcast_in_dim.2
  127.1 10.1 %all-to-all-start.1 = ((f32[64,2,128]{2,1,0:T(2,128)}), f32[64,2,128]{2,1,0:T(2,128)S(1)}, u32[]{:S(2)}, u32[]{:S(2)}) async-start(f32[64,2,128]{2,1,0:T(2,128)} %broadcast_in_dim.2), calls=%async_computation.1 | async-start | bytes 131072 | tf_op jit(solution)/shard_map/all_to_all | solution.py:444
  137.2 0.0 collective-permute-done.15.r1
  137.2 0.0 collective-permute-done.16.r2
  137.2 0.0 collective-permute-done.17.r3
  137.2 1.6 %finish.1 = (bf16[2048,256]{1,0:T(8,128)(2,1)}, f32[16,256]{1,0:T(8,128)}) custom-call(s32[1]{0:T(128)} %bitcast.mp_ref.part_ref, bf16[800,256]{1,0:T(8,128)(2,1)S(1)} %get-tuple-element.27.r0, bf16[800,256]{1,0:T(8,128)(2,1)S(1)} %collective-permute-done.15.r1, bf16[800,256]{1,0:T(8,128)(2,1)S(1)} %collective-permute-done.16.r2, ...), custom_call_target="tpu_custom_call" | custom-call | tf_op jit(solution)/shard_map/finish/pallas_call | solution.py:371
  138.9 8.4 %all-to-all-done.1.sums_ref = f32[64,2,128]{2,1,0:T(2,128)S(1)} async-done(((f32[64,2,128]{2,1,0:T(2,128)}), f32[64,2,128]{2,1,0:T(2,128)S(1)}, u32[]{:S(2)}, u32[]{:S(2)}) %all-to-all-start.1) | async-done | bytes 65568 | tf_op jit(solution)/shard_map/all_to_all | solution.py:444
  147.3 1.4 pool.1
  (1 shorter events, 0.0 us)
Async XLA Ops:
  5.2 15.9 %copy-start.5 = (bf16[1024,256]{1,0:T(8,128)(2,1)S(1)}, bf16[1024,256]{1,0:T(8,128)(2,1)}, u32[]{:S(2)}) copy-start(bf16[1024,256]{1,0:T(8,128)(2,1)} %get-tuple-element.26) | copy-start | bytes 1572868
  5.2 54.2 %all-to-all-start = ((bf16[64,72,128]{2,1,0:T(8,128)(2,1)}), bf16[64,72,128]{2,1,0:T(8,128)(2,1)S(1)}, u32[]{:S(2)}, u32[]{:S(2)}) async-start(bf16[64,72,128]{2,1,0:T(8,128)(2,1)} %get-tuple-element.20), calls=%async_computation | async-start | bytes 2359296 | tf_op jit(solution)/shard_map/all_to_all | solution.py:436
  18.5 63.8 %copy-start = (s32[128]{0:T(128)S(1)}, s32[128]{0:T(128)}, u32[]{:S(2)}) copy-start(s32[128]{0:T(128)} %image_ref.1) | copy-start | bytes 1540
  18.5 13.7 %collective-permute-start.7 = (bf16[1024,256]{1,0:T(8,128)(2,1)}, bf16[1024,256]{1,0:T(8,128)(2,1)S(1)}, u32[]{:S(2)}, u32[]{:S(2)}) collective-permute-start(bf16[1024,256]{1,0:T(8,128)(2,1)} %get-tuple-element.25), channel_id=1, source_target_pairs={{0,3},{1,0},{2,1},{3,2},{4,7},{5,4},{6,5},{7,6},{8,11},{9,8},{10,9... | collective-permute-start | bytes 1572872 | tf_op jit(solution)/shard_map/ppermute | solution.py:430
  21.1 14.2 %collective-permute-start.3 = (bf16[1024,256]{1,0:T(8,128)(2,1)}, bf16[1024,256]{1,0:T(8,128)(2,1)S(1)}, u32[]{:S(2)}, u32[]{:S(2)}) collective-permute-start(bf16[1024,256]{1,0:T(8,128)(2,1)} %get-tuple-element.25), channel_id=1, source_target_pairs={{0,1},{1,2},{2,3},{3,0},{4,5},{5,6},{6,7},{7,4},{8,9},{9,10},{10,1... | collective-permute-start | bytes 1572872 | tf_op jit(solution)/shard_map/ppermute | solution.py:429
  21.1 22.3 %collective-permute-start.8 = (bf16[1024,256]{1,0:T(8,128)(2,1)S(1)}, bf16[1024,256]{1,0:T(8,128)(2,1)}, u32[]{:S(2)}, u32[]{:S(2)}) collective-permute-start(bf16[1024,256]{1,0:T(8,128)(2,1)S(1)} %copy-done.5), channel_id=1, source_target_pairs={{0,3},{1,0},{2,1},{3,2},{4,7},{5,4},{6,5},{7,6},{8,11},{9,8},{10,9... | collective-permute-start | bytes 1572872 | tf_op jit(solution)/shard_map/ppermute | solution.py:430
  23.8 24.7 %collective-permute-start.4 = (bf16[1024,256]{1,0:T(8,128)(2,1)S(1)}, bf16[1024,256]{1,0:T(8,128)(2,1)}, u32[]{:S(2)}, u32[]{:S(2)}) collective-permute-start(bf16[1024,256]{1,0:T(8,128)(2,1)S(1)} %copy-done.5), channel_id=1, source_target_pairs={{0,1},{1,2},{2,3},{3,0},{4,5},{5,6},{6,7},{7,4},{8,9},{9,10},{10,1... | collective-permute-start | bytes 1572872 | tf_op jit(solution)/shard_map/ppermute | solution.py:429
  32.2 50.1 %copy-start.2 = (bf16[1024,256]{1,0:T(8,128)(2,1)}, bf16[1024,256]{1,0:T(8,128)(2,1)S(1)}, u32[]{:S(2)}) copy-start(bf16[1024,256]{1,0:T(8,128)(2,1)S(1)} %collective-permute-done.7.b0) | copy-start | bytes 1572868
  32.2 17.1 %collective-permute-start.9 = (bf16[1024,256]{1,0:T(8,128)(2,1)S(1)}, bf16[1024,256]{1,0:T(8,128)(2,1)S(1)}, u32[]{:S(2)}, u32[]{:S(2)}) collective-permute-start(bf16[1024,256]{1,0:T(8,128)(2,1)S(1)} %collective-permute-done.7.b0), channel_id=1, source_target_pairs={{0,4},{4,0},{8,12},{12,8},{16,20},{20,16},{24,28},{28,24},{32,36},... | collective-permute-start | bytes 1572872 | tf_op jit(solution)/shard_map/ppermute | solution.py:433
  35.3 47.1 %copy-start.3 = (bf16[1024,256]{1,0:T(8,128)(2,1)}, bf16[1024,256]{1,0:T(8,128)(2,1)S(1)}, u32[]{:S(2)}) copy-start(bf16[1024,256]{1,0:T(8,128)(2,1)S(1)} %collective-permute-done.3.a0) | copy-start | bytes 1572868
  35.3 22.6 %collective-permute-start.11 = (bf16[1024,256]{1,0:T(8,128)(2,1)S(1)}, bf16[1024,256]{1,0:T(8,128)(2,1)}, u32[]{:S(2)}, u32[]{:S(2)}) collective-permute-start(bf16[1024,256]{1,0:T(8,128)(2,1)S(1)} %collective-permute-done.3.a0), channel_id=1, source_target_pairs={{0,1},{1,2},{2,3},{3,0},{4,5},{5,6},{6,7},{7,4},{8,9},{9,10},{10,1... | collective-permute-start | bytes 1572872 | tf_op jit(solution)/shard_map/ppermute | solution.py:431
  43.4 16.1 %collective-permute-start.12 = (bf16[1024,256]{1,0:T(8,128)(2,1)}, bf16[1024,256]{1,0:T(8,128)(2,1)}, u32[]{:S(2)}, u32[]{:S(2)}) collective-permute-start(bf16[1024,256]{1,0:T(8,128)(2,1)} %collective-permute-done.8.b1), channel_id=1, source_target_pairs={{0,3},{1,0},{2,1},{3,2},{4,7},{5,4},{6,5},{7,6},{8,11},{9,8},{10,9... | collective-permute-start | bytes 1572872 | tf_op jit(solution)/shard_map/ppermute | solution.py:432
  46.9 13.6 %collective-permute-start.5 = (bf16[1024,256]{1,0:T(8,128)(2,1)S(1)}, bf16[1024,256]{1,0:T(8,128)(2,1)}, u32[]{:S(2)}, u32[]{:S(2)}) collective-permute-start(bf16[1024,256]{1,0:T(8,128)(2,1)S(1)} %collective-permute-done.3.a0), channel_id=1, source_target_pairs={{0,4},{4,0},{8,12},{12,8},{16,20},{20,16},{24,28},{28,24},{32,36},... | collective-permute-start | bytes 1572872 | tf_op jit(solution)/shard_map/ppermute | solution.py:433
  48.5 12.1 %collective-permute-start.10 = (bf16[1024,256]{1,0:T(8,128)(2,1)}, bf16[1024,256]{1,0:T(8,128)(2,1)}, u32[]{:S(2)}, u32[]{:S(2)}) collective-permute-start(bf16[1024,256]{1,0:T(8,128)(2,1)} %collective-permute-done.8.b1), channel_id=1, source_target_pairs={{0,4},{4,0},{8,12},{12,8},{16,20},{20,16},{24,28},{28,24},{32,36},... | collective-permute-start | bytes 1572872 | tf_op jit(solution)/shard_map/ppermute | solution.py:433
  49.4 10.1 %copy-start.4 = (bf16[1024,256]{1,0:T(8,128)(2,1)}, bf16[1024,256]{1,0:T(8,128)(2,1)S(1)}, u32[]{:S(2)}) copy-start(bf16[1024,256]{1,0:T(8,128)(2,1)S(1)} %collective-permute-done.9.b0x) | copy-start | bytes 1572868
  49.4 15.7 %collective-permute-start.6 = (bf16[1024,256]{1,0:T(8,128)(2,1)}, bf16[1024,256]{1,0:T(8,128)(2,1)}, u32[]{:S(2)}, u32[]{:S(2)}) collective-permute-start(bf16[1024,256]{1,0:T(8,128)(2,1)} %collective-permute-done.4.a1), channel_id=1, source_target_pairs={{0,4},{4,0},{8,12},{12,8},{16,20},{20,16},{24,28},{28,24},{32,36},... | collective-permute-start | bytes 1572872 | tf_op jit(solution)/shard_map/ppermute | solution.py:433
  57.8 7.2 %collective-permute-start.13 = (bf16[1024,256]{1,0:T(8,128)(2,1)}, bf16[1024,256]{1,0:T(8,128)(2,1)}, u32[]{:S(2)}, u32[]{:S(2)}) collective-permute-start(bf16[1024,256]{1,0:T(8,128)(2,1)} %collective-permute-done.11.c0), channel_id=1, source_target_pairs={{0,4},{4,0},{8,12},{12,8},{16,20},{20,16},{24,28},{28,24},{32,36},... | collective-permute-start | bytes 1572872 | tf_op jit(solution)/shard_map/ppermute | solution.py:433
  59.4 5.7 %collective-permute-start.14 = (bf16[1024,256]{1,0:T(8,128)(2,1)}, bf16[1024,256]{1,0:T(8,128)(2,1)}, u32[]{:S(2)}, u32[]{:S(2)}) collective-permute-start(bf16[1024,256]{1,0:T(8,128)(2,1)} %collective-permute-done.12.c1), channel_id=1, source_target_pairs={{0,4},{4,0},{8,12},{12,8},{16,20},{20,16},{24,28},{28,24},{32,36},... | collective-permute-start | bytes 1572872 | tf_op jit(solution)/shard_map/ppermute | solution.py:433
  60.5 42.5 %copy-start.1 = (f32[8,128]{1,0:T(8,128)}, f32[8,128]{1,0:T(8,128)S(1)}, u32[]{:S(2)}) copy-start(f32[8,128]{1,0:T(8,128)S(1)} %get-tuple-element.36.number_ref) | copy-start | bytes 12292
  60.5 12.5 %collective-permute-start = (bf16[752,256]{1,0:T(8,128)(2,1)S(1)}, bf16[752,256]{1,0:T(8,128)(2,1)S(1)}, u32[]{:S(2)}, u32[]{:S(2)}) collective-permute-start(bf16[752,256]{1,0:T(8,128)(2,1)S(1)} %get-tuple-element.22), channel_id=1, source_target_pairs={{0,1},{1,2},{2,3},{3,0},{4,5},{5,6},{6,7},{7,4},{8,9},{9,10},{10,1... | collective-permute-start | bytes 1155080 | tf_op jit(solution)/shard_map/ppermute | solution.py:412
  60.6 21.7 %collective-permute-start.1 = (bf16[752,256]{1,0:T(8,128)(2,1)S(1)}, bf16[752,256]{1,0:T(8,128)(2,1)S(1)}, u32[]{:S(2)}, u32[]{:S(2)}) collective-permute-start(bf16[752,256]{1,0:T(8,128)(2,1)S(1)} %get-tuple-element.23), channel_id=1, source_target_pairs={{0,2},{1,3},{2,0},{3,1},{4,6},{5,7},{6,4},{7,5},{8,10},{9,11},{10,... | collective-permute-start | bytes 1155080 | tf_op jit(solution)/shard_map/ppermute | solution.py:412
  65.1 17.3 %collective-permute-start.2 = (bf16[752,256]{1,0:T(8,128)(2,1)S(1)}, bf16[752,256]{1,0:T(8,128)(2,1)S(1)}, u32[]{:S(2)}, u32[]{:S(2)}) collective-permute-start(bf16[752,256]{1,0:T(8,128)(2,1)S(1)} %get-tuple-element.24), channel_id=1, source_target_pairs={{0,3},{1,0},{2,1},{3,2},{4,7},{5,4},{6,5},{7,6},{8,11},{9,8},{10,9... | collective-permute-start | bytes 1155080 | tf_op jit(solution)/shard_map/ppermute | solution.py:412
  103.0 34.2 %collective-permute-start.15 = (bf16[800,256]{1,0:T(8,128)(2,1)S(1)}, bf16[800,256]{1,0:T(8,128)(2,1)S(1)}, u32[]{:S(2)}, u32[]{:S(2)}) collective-permute-start(bf16[800,256]{1,0:T(8,128)(2,1)S(1)} %get-tuple-element.28), channel_id=1, source_target_pairs={{0,1},{1,2},{2,3},{3,0},{4,5},{5,6},{6,7},{7,4},{8,9},{9,10},{10,1... | collective-permute-start | bytes 1228808 | tf_op jit(solution)/shard_map/ppermute | solution.py:412
  103.4 33.8 %collective-permute-start.16 = (bf16[800,256]{1,0:T(8,128)(2,1)S(1)}, bf16[800,256]{1,0:T(8,128)(2,1)S(1)}, u32[]{:S(2)}, u32[]{:S(2)}) collective-permute-start(bf16[800,256]{1,0:T(8,128)(2,1)S(1)} %get-tuple-element.29), channel_id=1, source_target_pairs={{0,2},{1,3},{2,0},{3,1},{4,6},{5,7},{6,4},{7,5},{8,10},{9,11},{10,... | collective-permute-start | bytes 1228808 | tf_op jit(solution)/shard_map/ppermute | solution.py:412
  106.5 30.7 %collective-permute-start.17 = (bf16[800,256]{1,0:T(8,128)(2,1)S(1)}, bf16[800,256]{1,0:T(8,128)(2,1)S(1)}, u32[]{:S(2)}, u32[]{:S(2)}) collective-permute-start(bf16[800,256]{1,0:T(8,128)(2,1)S(1)} %get-tuple-element.30), channel_id=1, source_target_pairs={{0,3},{1,0},{2,1},{3,2},{4,7},{5,4},{6,5},{7,6},{8,11},{9,8},{10,9... | collective-permute-start | bytes 1228808 | tf_op jit(solution)/shard_map/ppermute | solution.py:412
  106.5 17.4 %collective-permute-start.18 = (f32[2,128]{1,0:T(2,128)S(1)}, f32[2,128]{1,0:T(2,128)S(1)}, u32[]{:S(2)}, u32[]{:S(2)}) collective-permute-start(f32[2,128]{1,0:T(2,128)S(1)} %get-tuple-element.33), channel_id=1, source_target_pairs={{0,1},{1,2},{2,3},{3,0},{4,5},{5,6},{6,7},{7,4},{8,9},{9,10},{10,1... | collective-permute-start | bytes 3080 | tf_op jit(solution)/shard_map/ppermute | solution.py:441
  108.0 16.2 %collective-permute-start.19 = (f32[2,128]{1,0:T(2,128)S(1)}, f32[2,128]{1,0:T(2,128)S(1)}, u32[]{:S(2)}, u32[]{:S(2)}) collective-permute-start(f32[2,128]{1,0:T(2,128)S(1)} %get-tuple-element.34), channel_id=1, source_target_pairs={{0,2},{1,3},{2,0},{3,1},{4,6},{5,7},{6,4},{7,5},{8,10},{9,11},{10,... | collective-permute-start | bytes 3080 | tf_op jit(solution)/shard_map/ppermute | solution.py:441
  124.0 2.4 %collective-permute-start.20 = (f32[2,128]{1,0:T(2,128)S(1)}, f32[2,128]{1,0:T(2,128)S(1)}, u32[]{:S(2)}, u32[]{:S(2)}) collective-permute-start(f32[2,128]{1,0:T(2,128)S(1)} %get-tuple-element.35), channel_id=1, source_target_pairs={{0,3},{1,0},{2,1},{3,2},{4,7},{5,4},{6,5},{7,6},{8,11},{9,8},{10,9... | collective-permute-start | bytes 3080 | tf_op jit(solution)/shard_map/ppermute | solution.py:441
  127.1 20.2 %all-to-all-start.1 = ((f32[64,2,128]{2,1,0:T(2,128)}), f32[64,2,128]{2,1,0:T(2,128)S(1)}, u32[]{:S(2)}, u32[]{:S(2)}) async-start(f32[64,2,128]{2,1,0:T(2,128)} %broadcast_in_dim.2), calls=%async_computation.1 | async-start | bytes 131072 | tf_op jit(solution)/shard_map/all_to_all | solution.py:444

commit v7 on v6

--- a/solution.py
+++ b/solution.py
@@ -426,8 +426,10 @@
     own = (w_query, w_key, w_value, w_out)
     image = packed_image.reshape(1, SLOTS)
     outgoing, s0, s1 = send_pack(dest_owner, dest_slot, part, core, image, patches, own, senders)
-    a0, a1 = (lax.ppermute(s, "mp", shift(1)) for s in (s0, s1))
-    b0, b1 = (lax.ppermute(s, "mp", shift(-1)) for s in (s0, s1))
+    a0 = lax.ppermute(s0, "mp", shift(1))
+    b1 = lax.ppermute(s1, "mp", shift(-1))
+    a1 = lax.ppermute(s1, "mp", shift(1))
+    b0 = lax.ppermute(s0, "mp", shift(-1))
     c0 = lax.ppermute(a0, "mp", shift(1))
     c1 = lax.ppermute(b1, "mp", shift(-1))
     a0x, a1x, b0x, b1x, c0x, c1x = (lax.ppermute(w, "dp", swap) for w in (a0, a1, b0, b1, c0, c1))

time: 149 us -> 149 us (level)
  no operation moved by 1% of the time
where the time goes in v7:
time: 149 us
  waiting for transfers between devices  69.5 us (47%)
  starting transfers between devices  48.5 us (33%)
  Pallas kernels  29.3 us (20%)
    pallas_call x1, Pallas kernels, block(): pl.pallas_call(block_kernel, grid_spec=pltpu.PrefetchScalarGridSpec(num_s...  20.6 us
    ppermute x3, waiting for transfers between devices, whole_block(): lax.ppermute(sums[d], 'mp', shift(d))  18.1 us
    ppermute x6, waiting for transfers between devices, passed_on(): got.append(lax.ppermute(pieces[d], 'mp', shift(d)))  17.3 us
    all_to_all x1, starting transfers between devices, whole_block(): lax.all_to_all(outgoing, 'dp', split_axis=0, concat_axis=0, tiled=True)  13.3 us
    all_to_all x1, starting transfers between devices, whole_block(): lax.all_to_all(spread, 'dp', split_axis=0, concat_axis=0, tiled=True)  10.1 us
    ppermute x1, waiting for transfers between devices, whole_block(): b0 = lax.ppermute(s0, 'mp', shift(-1))  8.46 us
    all_to_all x1, waiting for transfers between devices, whole_block(): lax.all_to_all(spread, 'dp', split_axis=0, concat_axis=0, tiled=True)  8.42 us
    ppermute x1, waiting for transfers between devices, whole_block(): c0 = lax.ppermute(a0, 'mp', shift(1))  8.36 us
  transfers between devices with their start and end apart: 23, of which 9 were waited for; matrix products, arithmetic and copies ran while one was open for 0% of the time, Pallas kernels for 2%

profile of v7, /device:TPU:1, one launch (start us, length us, event | category | flops | bytes accessed | tf_op | source)
XLA Modules:
  0.0 148.7 jit_solution(15133355466720558757)
XLA Ops:
  0.6 4.6 %send_pack.1 = (bf16[64,72,128]{2,1,0:T(8,128)(2,1)}, bf16[1024,256]{1,0:T(8,128)(2,1)}, bf16[1024,256]{1,0:T(8,128)(2,1)}) custom-call(s32[128]{0:T(128)} %owner_ref.1, s32[128]{0:T(128)} %slot_ref.1, s32[1]{0:T(128)} %bitcast.mp_ref.part_ref, s32[1]{0:T(128)} %bitcast.1.core_ref, s32[1,128]{1,0:T(1,128)} %bitcast.3, bf16[2048,1024]{1,0:T(8,128)(2,1)} %patch_ref.1, ...), custom_call_target="tpu_custom_call" | custom-call | tf_op jit(solution)/shard_map/send_pack/pallas_call | solution.py:88
  5.2 0.0 copy-start.5
  5.2 13.3 %all-to-all-start = ((bf16[64,72,128]{2,1,0:T(8,128)(2,1)}), bf16[64,72,128]{2,1,0:T(8,128)(2,1)S(1)}, u32[]{:S(2)}, u32[]{:S(2)}) async-start(bf16[64,72,128]{2,1,0:T(8,128)(2,1)} %get-tuple-element.20), calls=%async_computation | async-start | bytes 2359296 | tf_op jit(solution)/shard_map/all_to_all | solution.py:438
  18.5 0.0 copy-start
  18.5 2.6 %collective-permute-start.7 = (bf16[1024,256]{1,0:T(8,128)(2,1)}, bf16[1024,256]{1,0:T(8,128)(2,1)S(1)}, u32[]{:S(2)}, u32[]{:S(2)}) collective-permute-start(bf16[1024,256]{1,0:T(8,128)(2,1)} %get-tuple-element.25), channel_id=1, source_target_pairs={{0,3},{1,0},{2,1},{3,2},{4,7},{5,4},{6,5},{7,6},{8,11},{9,8},{10,9... | collective-permute-start | bytes 1572872 | tf_op jit(solution)/shard_map/ppermute | solution.py:432
  21.1 0.0 collective-permute-start.3
  21.1 0.0 copy-done.5
  21.1 2.7 %collective-permute-start.8 = (bf16[1024,256]{1,0:T(8,128)(2,1)S(1)}, bf16[1024,256]{1,0:T(8,128)(2,1)}, u32[]{:S(2)}, u32[]{:S(2)}) collective-permute-start(bf16[1024,256]{1,0:T(8,128)(2,1)S(1)} %copy-done.5), channel_id=1, source_target_pairs={{0,3},{1,0},{2,1},{3,2},{4,7},{5,4},{6,5},{7,6},{8,11},{9,8},{10,9... | collective-permute-start | bytes 1572872 | tf_op jit(solution)/shard_map/ppermute | solution.py:430
  23.8 0.0 collective-permute-start.4
  23.8 8.5 %collective-permute-done.7.b0 = bf16[1024,256]{1,0:T(8,128)(2,1)S(1)} collective-permute-done((bf16[1024,256]{1,0:T(8,128)(2,1)}, bf16[1024,256]{1,0:T(8,128)(2,1)S(1)}, u32[]{:S(2)}, u32[]{:S(2)}) %collective-permute-start.7) | collective-permute-done | bytes 524320 | tf_op jit(solution)/shard_map/ppermute | solution.py:432
  32.2 0.0 copy-start.2
  32.2 2.2 %collective-permute-start.9 = (bf16[1024,256]{1,0:T(8,128)(2,1)S(1)}, bf16[1024,256]{1,0:T(8,128)(2,1)S(1)}, u32[]{:S(2)}, u32[]{:S(2)}) collective-permute-start(bf16[1024,256]{1,0:T(8,128)(2,1)S(1)} %collective-permute-done.7.b0), channel_id=1, source_target_pairs={{0,4},{4,0},{8,12},{12,8},{16,20},{20,16},{24,28},{28,24},{32,36},... | collective-permute-start | bytes 1572872 | tf_op jit(solution)/shard_map/ppermute | solution.py:435
  34.5 0.8 collective-permute-done.3.a0
  35.3 0.0 copy-start.3
  35.3 0.0 collective-permute-start.11
  35.3 8.1 %collective-permute-done.8.b1 = bf16[1024,256]{1,0:T(8,128)(2,1)} collective-permute-done((bf16[1024,256]{1,0:T(8,128)(2,1)S(1)}, bf16[1024,256]{1,0:T(8,128)(2,1)}, u32[]{:S(2)}, u32[]{:S(2)}) %collective-permute-start.8) | collective-permute-done | bytes 524320 | tf_op jit(solution)/shard_map/ppermute | solution.py:430
  43.4 3.5 %collective-permute-start.12 = (bf16[1024,256]{1,0:T(8,128)(2,1)}, bf16[1024,256]{1,0:T(8,128)(2,1)}, u32[]{:S(2)}, u32[]{:S(2)}) collective-permute-start(bf16[1024,256]{1,0:T(8,128)(2,1)} %collective-permute-done.8.b1), channel_id=1, source_target_pairs={{0,3},{1,0},{2,1},{3,2},{4,7},{5,4},{6,5},{7,6},{8,11},{9,8},{10,9... | collective-permute-start | bytes 1572872 | tf_op jit(solution)/shard_map/ppermute | solution.py:434
  46.9 1.6 %collective-permute-start.5 = (bf16[1024,256]{1,0:T(8,128)(2,1)S(1)}, bf16[1024,256]{1,0:T(8,128)(2,1)}, u32[]{:S(2)}, u32[]{:S(2)}) collective-permute-start(bf16[1024,256]{1,0:T(8,128)(2,1)S(1)} %collective-permute-done.3.a0), channel_id=1, source_target_pairs={{0,4},{4,0},{8,12},{12,8},{16,20},{20,16},{24,28},{28,24},{32,36},... | collective-permute-start | bytes 1572872 | tf_op jit(solution)/shard_map/ppermute | solution.py:435
  48.5 0.0 collective-permute-done.4.a1
  48.5 0.9 collective-permute-start.10
  49.4 0.0 collective-permute-done.9.b0x
  49.4 0.0 copy-start.4
  49.4 0.1 collective-permute-start.6
  49.5 8.4 %collective-permute-done.11.c0 = bf16[1024,256]{1,0:T(8,128)(2,1)} collective-permute-done((bf16[1024,256]{1,0:T(8,128)(2,1)S(1)}, bf16[1024,256]{1,0:T(8,128)(2,1)}, u32[]{:S(2)}, u32[]{:S(2)}) %collective-permute-start.11) | collective-permute-done | bytes 524320 | tf_op jit(solution)/shard_map/ppermute | solution.py:433
  57.8 1.6 %collective-permute-start.13 = (bf16[1024,256]{1,0:T(8,128)(2,1)}, bf16[1024,256]{1,0:T(8,128)(2,1)}, u32[]{:S(2)}, u32[]{:S(2)}) collective-permute-start(bf16[1024,256]{1,0:T(8,128)(2,1)} %collective-permute-done.11.c0), channel_id=1, source_target_pairs={{0,4},{4,0},{8,12},{12,8},{16,20},{20,16},{24,28},{28,24},{32,36},... | collective-permute-start | bytes 1572872 | tf_op jit(solution)/shard_map/ppermute | solution.py:435
  59.4 0.0 collective-permute-done.12.c1
  59.4 0.0 collective-permute-start.14
  59.4 0.0 copy-done.4
  59.4 0.0 all-to-all-done.in_ref
  59.5 1.0 arrive_sort.1
  60.5 0.0 copy-start.1
  60.5 0.0 collective-permute-done.5.a0x
  60.5 0.1 collective-permute-start
  60.6 0.0 collective-permute-done.10.b1x
  60.6 4.5 %collective-permute-start.1 = (bf16[752,256]{1,0:T(8,128)(2,1)S(1)}, bf16[752,256]{1,0:T(8,128)(2,1)S(1)}, u32[]{:S(2)}, u32[]{:S(2)}) collective-permute-start(bf16[752,256]{1,0:T(8,128)(2,1)S(1)} %get-tuple-element.23), channel_id=1, source_target_pairs={{0,2},{1,3},{2,0},{3,1},{4,6},{5,7},{6,4},{7,5},{8,10},{9,11},{10,... | collective-permute-start | bytes 1155080 | tf_op jit(solution)/shard_map/ppermute | solution.py:412
  65.1 0.0 collective-permute-done.6.a1x
  65.1 0.0 collective-permute-start.2
  65.1 0.0 collective-permute-done.13.c0x
  65.1 0.0 collective-permute-done.14.c1x
  65.1 8.0 %collective-permute-done.x1 = bf16[752,256]{1,0:T(8,128)(2,1)S(1)} collective-permute-done((bf16[752,256]{1,0:T(8,128)(2,1)S(1)}, bf16[752,256]{1,0:T(8,128)(2,1)S(1)}, u32[]{:S(2)}, u32[]{:S(2)}) %collective-permute-start) | collective-permute-done | bytes 385056 | tf_op jit(solution)/shard_map/ppermute | solution.py:412
  73.1 9.3 %collective-permute-done.1.x2 = bf16[752,256]{1,0:T(8,128)(2,1)S(1)} collective-permute-done((bf16[752,256]{1,0:T(8,128)(2,1)S(1)}, bf16[752,256]{1,0:T(8,128)(2,1)S(1)}, u32[]{:S(2)}, u32[]{:S(2)}) %collective-permute-start.1) | collective-permute-done | bytes 385056 | tf_op jit(solution)/shard_map/ppermute | solution.py:412
  82.3 0.0 collective-permute-done.2.x3
  82.3 0.0 copy-done.2
  82.4 0.0 copy-done.3
  82.4 0.0 copy-done
  82.4 20.6 %block.1 = (bf16[800,256]{1,0:T(8,128)(2,1)S(1)}, bf16[800,256]{1,0:T(8,128)(2,1)S(1)}, bf16[800,256]{1,0:T(8,128)(2,1)S(1)}, bf16[800,256]{1,0:T(8,128)(2,1)S(1...) custom-call(s32[1]{0:T(128)} %bitcast.mp_ref.part_ref, ...), custom_call_target="tpu_custom_call" | custom-call | tf_op jit(solution)/shard_map/block/pallas_call | solution.py:321
  103.0 0.0 copy-done.1
  103.0 0.4 collective-permute-start.15
  103.4 3.1 %collective-permute-start.16 = (bf16[800,256]{1,0:T(8,128)(2,1)S(1)}, bf16[800,256]{1,0:T(8,128)(2,1)S(1)}, u32[]{:S(2)}, u32[]{:S(2)}) collective-permute-start(bf16[800,256]{1,0:T(8,128)(2,1)S(1)} %get-tuple-element.29), channel_id=1, source_target_pairs={{0,2},{1,3},{2,0},{3,1},{4,6},{5,7},{6,4},{7,5},{8,10},{9,11},{10,... | collective-permute-start | bytes 1228808 | tf_op jit(solution)/shard_map/ppermute | solution.py:412
  106.5 0.0 collective-permute-start.17
  106.5 1.5 collective-permute-start.18
  108.0 0.1 collective-permute-start.19
  108.1 15.9 %collective-permute-done.18 = f32[2,128]{1,0:T(2,128)S(1)} collective-permute-done((f32[2,128]{1,0:T(2,128)S(1)}, f32[2,128]{1,0:T(2,128)S(1)}, u32[]{:S(2)}, u32[]{:S(2)}) %collective-permute-start.18) | collective-permute-done | bytes 1056 | tf_op jit(solution)/shard_map/ppermute | solution.py:443
  124.0 0.2 collective-permute-start.20
  124.2 0.0 collective-permute-done.19
  124.2 2.2 %collective-permute-done.20 = f32[2,128]{1,0:T(2,128)S(1)} collective-permute-done((f32[2,128]{1,0:T(2,128)S(1)}, f32[2,128]{1,0:T(2,128)S(1)}, u32[]{:S(2)}, u32[]{:S(2)}) %collective-permute-start.20) | collective-permute-done | bytes 1056 | tf_op jit(solution)/shard_map/ppermute | solution.py:443
  126.4 0.6 broadcast_in_dim.2
  127.1 10.1 %all-to-all-start.1 = ((f32[64,2,128]{2,1,0:T(2,128)}), f32[64,2,128]{2,1,0:T(2,128)S(1)}, u32[]{:S(2)}, u32[]{:S(2)}) async-start(f32[64,2,128]{2,1,0:T(2,128)} %broadcast_in_dim.2), calls=%async_computation.1 | async-start | bytes 131072 | tf_op jit(solution)/shard_map/all_to_all | solution.py:446
  137.2 0.0 collective-permute-done.15.r1
  137.2 0.0 collective-permute-done.16.r2
  137.2 0.0 collective-permute-done.17.r3
  137.2 1.6 %finish.1 = (bf16[2048,256]{1,0:T(8,128)(2,1)}, f32[16,256]{1,0:T(8,128)}) custom-call(s32[1]{0:T(128)} %bitcast.mp_ref.part_ref, bf16[800,256]{1,0:T(8,128)(2,1)S(1)} %get-tuple-element.27.r0, bf16[800,256]{1,0:T(8,128)(2,1)S(1)} %collective-permute-done.15.r1, bf16[800,256]{1,0:T(8,128)(2,1)S(1)} %collective-permute-done.16.r2, ...), custom_call_target="tpu_custom_call" | custom-call | tf_op jit(solution)/shard_map/finish/pallas_call | solution.py:371
  138.9 8.4 %all-to-all-done.1.sums_ref = f32[64,2,128]{2,1,0:T(2,128)S(1)} async-done(((f32[64,2,128]{2,1,0:T(2,128)}), f32[64,2,128]{2,1,0:T(2,128)S(1)}, u32[]{:S(2)}, u32[]{:S(2)}) %all-to-all-start.1) | async-done | bytes 65568 | tf_op jit(solution)/shard_map/all_to_all | solution.py:446
  147.3 1.4 pool.1
  (1 shorter events, 0.0 us)
Async XLA Ops:
  5.2 15.9 %copy-start.5 = (bf16[1024,256]{1,0:T(8,128)(2,1)S(1)}, bf16[1024,256]{1,0:T(8,128)(2,1)}, u32[]{:S(2)}) copy-start(bf16[1024,256]{1,0:T(8,128)(2,1)} %get-tuple-element.26) | copy-start | bytes 1572868
  5.2 54.2 %all-to-all-start = ((bf16[64,72,128]{2,1,0:T(8,128)(2,1)}), bf16[64,72,128]{2,1,0:T(8,128)(2,1)S(1)}, u32[]{:S(2)}, u32[]{:S(2)}) async-start(bf16[64,72,128]{2,1,0:T(8,128)(2,1)} %get-tuple-element.20), calls=%async_computation | async-start | bytes 2359296 | tf_op jit(solution)/shard_map/all_to_all | solution.py:438
  18.5 63.8 %copy-start = (s32[128]{0:T(128)S(1)}, s32[128]{0:T(128)}, u32[]{:S(2)}) copy-start(s32[128]{0:T(128)} %image_ref.1) | copy-start | bytes 1540
  18.5 13.7 %collective-permute-start.7 = (bf16[1024,256]{1,0:T(8,128)(2,1)}, bf16[1024,256]{1,0:T(8,128)(2,1)S(1)}, u32[]{:S(2)}, u32[]{:S(2)}) collective-permute-start(bf16[1024,256]{1,0:T(8,128)(2,1)} %get-tuple-element.25), channel_id=1, source_target_pairs={{0,3},{1,0},{2,1},{3,2},{4,7},{5,4},{6,5},{7,6},{8,11},{9,8},{10,9... | collective-permute-start | bytes 1572872 | tf_op jit(solution)/shard_map/ppermute | solution.py:432
  21.1 14.2 %collective-permute-start.3 = (bf16[1024,256]{1,0:T(8,128)(2,1)}, bf16[1024,256]{1,0:T(8,128)(2,1)S(1)}, u32[]{:S(2)}, u32[]{:S(2)}) collective-permute-start(bf16[1024,256]{1,0:T(8,128)(2,1)} %get-tuple-element.25), channel_id=1, source_target_pairs={{0,1},{1,2},{2,3},{3,0},{4,5},{5,6},{6,7},{7,4},{8,9},{9,10},{10,1... | collective-permute-start | bytes 1572872 | tf_op jit(solution)/shard_map/ppermute | solution.py:429
  21.1 22.3 %collective-permute-start.8 = (bf16[1024,256]{1,0:T(8,128)(2,1)S(1)}, bf16[1024,256]{1,0:T(8,128)(2,1)}, u32[]{:S(2)}, u32[]{:S(2)}) collective-permute-start(bf16[1024,256]{1,0:T(8,128)(2,1)S(1)} %copy-done.5), channel_id=1, source_target_pairs={{0,3},{1,0},{2,1},{3,2},{4,7},{5,4},{6,5},{7,6},{8,11},{9,8},{10,9... | collective-permute-start | bytes 1572872 | tf_op jit(solution)/shard_map/ppermute | solution.py:430
  23.8 24.7 %collective-permute-start.4 = (bf16[1024,256]{1,0:T(8,128)(2,1)S(1)}, bf16[1024,256]{1,0:T(8,128)(2,1)}, u32[]{:S(2)}, u32[]{:S(2)}) collective-permute-start(bf16[1024,256]{1,0:T(8,128)(2,1)S(1)} %copy-done.5), channel_id=1, source_target_pairs={{0,1},{1,2},{2,3},{3,0},{4,5},{5,6},{6,7},{7,4},{8,9},{9,10},{10,1... | collective-permute-start | bytes 1572872 | tf_op jit(solution)/shard_map/ppermute | solution.py:431
  32.2 50.1 %copy-start.2 = (bf16[1024,256]{1,0:T(8,128)(2,1)}, bf16[1024,256]{1,0:T(8,128)(2,1)S(1)}, u32[]{:S(2)}) copy-start(bf16[1024,256]{1,0:T(8,128)(2,1)S(1)} %collective-permute-done.7.b0) | copy-start | bytes 1572868
  32.2 17.1 %collective-permute-start.9 = (bf16[1024,256]{1,0:T(8,128)(2,1)S(1)}, bf16[1024,256]{1,0:T(8,128)(2,1)S(1)}, u32[]{:S(2)}, u32[]{:S(2)}) collective-permute-start(bf16[1024,256]{1,0:T(8,128)(2,1)S(1)} %collective-permute-done.7.b0), channel_id=1, source_target_pairs={{0,4},{4,0},{8,12},{12,8},{16,20},{20,16},{24,28},{28,24},{32,36},... | collective-permute-start | bytes 1572872 | tf_op jit(solution)/shard_map/ppermute | solution.py:435
  35.3 47.1 %copy-start.3 = (bf16[1024,256]{1,0:T(8,128)(2,1)}, bf16[1024,256]{1,0:T(8,128)(2,1)S(1)}, u32[]{:S(2)}) copy-start(bf16[1024,256]{1,0:T(8,128)(2,1)S(1)} %collective-permute-done.3.a0) | copy-start | bytes 1572868
  35.3 22.6 %collective-permute-start.11 = (bf16[1024,256]{1,0:T(8,128)(2,1)S(1)}, bf16[1024,256]{1,0:T(8,128)(2,1)}, u32[]{:S(2)}, u32[]{:S(2)}) collective-permute-start(bf16[1024,256]{1,0:T(8,128)(2,1)S(1)} %collective-permute-done.3.a0), channel_id=1, source_target_pairs={{0,1},{1,2},{2,3},{3,0},{4,5},{5,6},{6,7},{7,4},{8,9},{9,10},{10,1... | collective-permute-start | bytes 1572872 | tf_op jit(solution)/shard_map/ppermute | solution.py:433
  43.4 16.1 %collective-permute-start.12 = (bf16[1024,256]{1,0:T(8,128)(2,1)}, bf16[1024,256]{1,0:T(8,128)(2,1)}, u32[]{:S(2)}, u32[]{:S(2)}) collective-permute-start(bf16[1024,256]{1,0:T(8,128)(2,1)} %collective-permute-done.8.b1), channel_id=1, source_target_pairs={{0,3},{1,0},{2,1},{3,2},{4,7},{5,4},{6,5},{7,6},{8,11},{9,8},{10,9... | collective-permute-start | bytes 1572872 | tf_op jit(solution)/shard_map/ppermute | solution.py:434
  46.9 13.6 %collective-permute-start.5 = (bf16[1024,256]{1,0:T(8,128)(2,1)S(1)}, bf16[1024,256]{1,0:T(8,128)(2,1)}, u32[]{:S(2)}, u32[]{:S(2)}) collective-permute-start(bf16[1024,256]{1,0:T(8,128)(2,1)S(1)} %collective-permute-done.3.a0), channel_id=1, source_target_pairs={{0,4},{4,0},{8,12},{12,8},{16,20},{20,16},{24,28},{28,24},{32,36},... | collective-permute-start | bytes 1572872 | tf_op jit(solution)/shard_map/ppermute | solution.py:435
  48.5 12.1 %collective-permute-start.10 = (bf16[1024,256]{1,0:T(8,128)(2,1)}, bf16[1024,256]{1,0:T(8,128)(2,1)}, u32[]{:S(2)}, u32[]{:S(2)}) collective-permute-start(bf16[1024,256]{1,0:T(8,128)(2,1)} %collective-permute-done.8.b1), channel_id=1, source_target_pairs={{0,4},{4,0},{8,12},{12,8},{16,20},{20,16},{24,28},{28,24},{32,36},... | collective-permute-start | bytes 1572872 | tf_op jit(solution)/shard_map/ppermute | solution.py:435
  49.4 10.1 %copy-start.4 = (bf16[1024,256]{1,0:T(8,128)(2,1)}, bf16[1024,256]{1,0:T(8,128)(2,1)S(1)}, u32[]{:S(2)}) copy-start(bf16[1024,256]{1,0:T(8,128)(2,1)S(1)} %collective-permute-done.9.b0x) | copy-start | bytes 1572868
  49.4 15.7 %collective-permute-start.6 = (bf16[1024,256]{1,0:T(8,128)(2,1)}, bf16[1024,256]{1,0:T(8,128)(2,1)}, u32[]{:S(2)}, u32[]{:S(2)}) collective-permute-start(bf16[1024,256]{1,0:T(8,128)(2,1)} %collective-permute-done.4.a1), channel_id=1, source_target_pairs={{0,4},{4,0},{8,12},{12,8},{16,20},{20,16},{24,28},{28,24},{32,36},... | collective-permute-start | bytes 1572872 | tf_op jit(solution)/shard_map/ppermute | solution.py:435
  57.8 7.2 %collective-permute-start.13 = (bf16[1024,256]{1,0:T(8,128)(2,1)}, bf16[1024,256]{1,0:T(8,128)(2,1)}, u32[]{:S(2)}, u32[]{:S(2)}) collective-permute-start(bf16[1024,256]{1,0:T(8,128)(2,1)} %collective-permute-done.11.c0), channel_id=1, source_target_pairs={{0,4},{4,0},{8,12},{12,8},{16,20},{20,16},{24,28},{28,24},{32,36},... | collective-permute-start | bytes 1572872 | tf_op jit(solution)/shard_map/ppermute | solution.py:435
  59.4 5.7 %collective-permute-start.14 = (bf16[1024,256]{1,0:T(8,128)(2,1)}, bf16[1024,256]{1,0:T(8,128)(2,1)}, u32[]{:S(2)}, u32[]{:S(2)}) collective-permute-start(bf16[1024,256]{1,0:T(8,128)(2,1)} %collective-permute-done.12.c1), channel_id=1, source_target_pairs={{0,4},{4,0},{8,12},{12,8},{16,20},{20,16},{24,28},{28,24},{32,36},... | collective-permute-start | bytes 1572872 | tf_op jit(solution)/shard_map/ppermute | solution.py:435
  60.5 42.5 %copy-start.1 = (f32[8,128]{1,0:T(8,128)}, f32[8,128]{1,0:T(8,128)S(1)}, u32[]{:S(2)}) copy-start(f32[8,128]{1,0:T(8,128)S(1)} %get-tuple-element.36.number_ref) | copy-start | bytes 12292
  60.5 12.5 %collective-permute-start = (bf16[752,256]{1,0:T(8,128)(2,1)S(1)}, bf16[752,256]{1,0:T(8,128)(2,1)S(1)}, u32[]{:S(2)}, u32[]{:S(2)}) collective-permute-start(bf16[752,256]{1,0:T(8,128)(2,1)S(1)} %get-tuple-element.22), channel_id=1, source_target_pairs={{0,1},{1,2},{2,3},{3,0},{4,5},{5,6},{6,7},{7,4},{8,9},{9,10},{10,1... | collective-permute-start | bytes 1155080 | tf_op jit(solution)/shard_map/ppermute | solution.py:412
  60.6 21.7 %collective-permute-start.1 = (bf16[752,256]{1,0:T(8,128)(2,1)S(1)}, bf16[752,256]{1,0:T(8,128)(2,1)S(1)}, u32[]{:S(2)}, u32[]{:S(2)}) collective-permute-start(bf16[752,256]{1,0:T(8,128)(2,1)S(1)} %get-tuple-element.23), channel_id=1, source_target_pairs={{0,2},{1,3},{2,0},{3,1},{4,6},{5,7},{6,4},{7,5},{8,10},{9,11},{10,... | collective-permute-start | bytes 1155080 | tf_op jit(solution)/shard_map/ppermute | solution.py:412
  65.1 17.3 %collective-permute-start.2 = (bf16[752,256]{1,0:T(8,128)(2,1)S(1)}, bf16[752,256]{1,0:T(8,128)(2,1)S(1)}, u32[]{:S(2)}, u32[]{:S(2)}) collective-permute-start(bf16[752,256]{1,0:T(8,128)(2,1)S(1)} %get-tuple-element.24), channel_id=1, source_target_pairs={{0,3},{1,0},{2,1},{3,2},{4,7},{5,4},{6,5},{7,6},{8,11},{9,8},{10,9... | collective-permute-start | bytes 1155080 | tf_op jit(solution)/shard_map/ppermute | solution.py:412
  103.0 34.2 %collective-permute-start.15 = (bf16[800,256]{1,0:T(8,128)(2,1)S(1)}, bf16[800,256]{1,0:T(8,128)(2,1)S(1)}, u32[]{:S(2)}, u32[]{:S(2)}) collective-permute-start(bf16[800,256]{1,0:T(8,128)(2,1)S(1)} %get-tuple-element.28), channel_id=1, source_target_pairs={{0,1},{1,2},{2,3},{3,0},{4,5},{5,6},{6,7},{7,4},{8,9},{9,10},{10,1... | collective-permute-start | bytes 1228808 | tf_op jit(solution)/shard_map/ppermute | solution.py:412
  103.4 33.8 %collective-permute-start.16 = (bf16[800,256]{1,0:T(8,128)(2,1)S(1)}, bf16[800,256]{1,0:T(8,128)(2,1)S(1)}, u32[]{:S(2)}, u32[]{:S(2)}) collective-permute-start(bf16[800,256]{1,0:T(8,128)(2,1)S(1)} %get-tuple-element.29), channel_id=1, source_target_pairs={{0,2},{1,3},{2,0},{3,1},{4,6},{5,7},{6,4},{7,5},{8,10},{9,11},{10,... | collective-permute-start | bytes 1228808 | tf_op jit(solution)/shard_map/ppermute | solution.py:412
  106.5 30.7 %collective-permute-start.17 = (bf16[800,256]{1,0:T(8,128)(2,1)S(1)}, bf16[800,256]{1,0:T(8,128)(2,1)S(1)}, u32[]{:S(2)}, u32[]{:S(2)}) collective-permute-start(bf16[800,256]{1,0:T(8,128)(2,1)S(1)} %get-tuple-element.30), channel_id=1, source_target_pairs={{0,3},{1,0},{2,1},{3,2},{4,7},{5,4},{6,5},{7,6},{8,11},{9,8},{10,9... | collective-permute-start | bytes 1228808 | tf_op jit(solution)/shard_map/ppermute | solution.py:412
  106.5 17.4 %collective-permute-start.18 = (f32[2,128]{1,0:T(2,128)S(1)}, f32[2,128]{1,0:T(2,128)S(1)}, u32[]{:S(2)}, u32[]{:S(2)}) collective-permute-start(f32[2,128]{1,0:T(2,128)S(1)} %get-tuple-element.33), channel_id=1, source_target_pairs={{0,1},{1,2},{2,3},{3,0},{4,5},{5,6},{6,7},{7,4},{8,9},{9,10},{10,1... | collective-permute-start | bytes 3080 | tf_op jit(solution)/shard_map/ppermute | solution.py:443
  108.0 16.2 %collective-permute-start.19 = (f32[2,128]{1,0:T(2,128)S(1)}, f32[2,128]{1,0:T(2,128)S(1)}, u32[]{:S(2)}, u32[]{:S(2)}) collective-permute-start(f32[2,128]{1,0:T(2,128)S(1)} %get-tuple-element.34), channel_id=1, source_target_pairs={{0,2},{1,3},{2,0},{3,1},{4,6},{5,7},{6,4},{7,5},{8,10},{9,11},{10,... | collective-permute-start | bytes 3080 | tf_op jit(solution)/shard_map/ppermute | solution.py:443
  124.0 2.4 %collective-permute-start.20 = (f32[2,128]{1,0:T(2,128)S(1)}, f32[2,128]{1,0:T(2,128)S(1)}, u32[]{:S(2)}, u32[]{:S(2)}) collective-permute-start(f32[2,128]{1,0:T(2,128)S(1)} %get-tuple-element.35), channel_id=1, source_target_pairs={{0,3},{1,0},{2,1},{3,2},{4,7},{5,4},{6,5},{7,6},{8,11},{9,8},{10,9... | collective-permute-start | bytes 3080 | tf_op jit(solution)/shard_map/ppermute | solution.py:443
  127.1 20.2 %all-to-all-start.1 = ((f32[64,2,128]{2,1,0:T(2,128)}), f32[64,2,128]{2,1,0:T(2,128)S(1)}, u32[]{:S(2)}, u32[]{:S(2)}) async-start(f32[64,2,128]{2,1,0:T(2,128)} %broadcast_in_dim.2), calls=%async_computation.1 | async-start | bytes 131072 | tf_op jit(solution)/shard_map/all_to_all | solution.py:446

commit v8 on v7

--- a/solution.py
+++ b/solution.py
@@ -15,7 +15,7 @@
 WIN = PART_SLOTS + 15
 ROWS_W = WIN * TILE
 IMG = 16
-EXTRA = 3 * IMG
+EXTRA = TILE
 HD = 64
 MAX_LOCAL = 4
 PAY = 72
@@ -25,9 +25,16 @@
 SMALL = pltpu.CompilerParams(vmem_limit_bytes=16 * 1024 * 1024)
 
 
-def send_kernel(owner_ref, slot_ref, mp_ref, core_ref, image_ref, patch_ref, wq, wk, wv, wo, out_ref, s0, s1, count_ref, place_ref, sems):
+def send_kernel(owner_ref, slot_ref, mp_ref, core_ref, image_ref, patch_ref, wq, wk, wv, wo, out_ref, s0, s1, count_ref, place_ref, rank_ref, rows_ref, sems, row_sems):
     owners = out_ref.shape[0]
     core = core_ref[0]
+    chunk = SLOTS * TILE // PARTS
+    own_columns = pl.ds(pl.multiple_of(mp_ref[0] * PW, PW), PW)
+    fetches = []
+    for n in range(PARTS):
+        some = pl.ds(n * chunk, chunk)
+        fetches.append(pltpu.make_async_copy(patch_ref.at[some, own_columns], rows_ref.at[some, :], row_sems.at[n]))
+        fetches[-1].start()
     even = [pltpu.make_async_copy(wq, s0, sems.at[0]), pltpu.make_async_copy(wk, s1, sems.at[1])]
     odd = [pltpu.make_async_copy(wv, s0, sems.at[0])]
     for n in range(PARTS):
@@ -50,18 +57,15 @@
 
     lax.fori_loop(0, owners, clear, 0, unroll=8)
 
-    def move(t, carry):
+    def rank(t, carry):
         o = owner_ref[t]
         r = count_ref[o]
         count_ref[o] = r + 1
         place_ref[2 * o + r] = slot_ref[t]
-        rows = patch_ref[pl.ds(pl.multiple_of(t * TILE, TILE), TILE), :]
-        base = pl.multiple_of(r * 2 * TILE, TILE)
-        out_ref[o, pl.ds(base, TILE), :] = rows[:, :128]
-        out_ref[o, pl.ds(base + TILE, TILE), :] = rows[:, 128:]
-        return carry
-
-    lax.fori_loop(0, SLOTS, move, 0, unroll=8)
+        rank_ref[t] = r
+        return carry
+
+    lax.fori_loop(0, SLOTS, rank, 0, unroll=8)
     row = lax.broadcasted_iota(jnp.int32, (PAY - 64, 128), 0)
     images = jnp.max(image_ref[...], axis=1, keepdims=True) + 1
     images = jnp.broadcast_to(images, row.shape)
@@ -72,6 +76,18 @@
         return carry
 
     lax.fori_loop(0, owners, label, 0, unroll=8)
+
+    def move(t, carry):
+        o = owner_ref[t]
+        rows = rows_ref[pl.ds(pl.multiple_of(t * TILE, TILE), TILE), :]
+        base = pl.multiple_of(rank_ref[t] * 2 * TILE, TILE)
+        out_ref[o, pl.ds(base, TILE), :] = rows[:, :128]
+        out_ref[o, pl.ds(base + TILE, TILE), :] = rows[:, 128:]
+        return carry
+
+    for n in range(PARTS):
+        fetches[n].wait()
+        lax.fori_loop(n * SLOTS // PARTS, (n + 1) * SLOTS // PARTS, move, 0, unroll=8)
 
     @pl.when(core == 0)
     def _():
@@ -92,15 +108,17 @@
             grid=(1,),
             in_specs=[
                 pl.BlockSpec((1, SLOTS), lambda i, a, b, m, c: (0, 0)),
-                pl.BlockSpec((SLOTS * TILE, PW), lambda i, a, b, m, c: (0, m[0])),
             ]
-            + [pl.BlockSpec(memory_space=pl.ANY)] * 4,
+            + [pl.BlockSpec(memory_space=pl.ANY)] * 5,
             out_specs=[pl.BlockSpec((senders, PAY, 128), lambda i, a, b, m, c: (0, 0, 0))]
             + [pl.BlockSpec((D, PW), lambda i, a, b, m, c: (0, 0))] * 2,
             scratch_shapes=[
                 pltpu.SMEM((senders,), jnp.int32),
                 pltpu.SMEM((2 * senders,), jnp.int32),
+                pltpu.SMEM((SLOTS,), jnp.int32),
+                pltpu.VMEM((SLOTS * TILE, PW), jnp.bfloat16),
                 pltpu.SemaphoreType.DMA((1 + PARTS,)),
+                pltpu.SemaphoreType.DMA((PARTS,)),
             ],
         ),
         out_shape=[jax.ShapeDtypeStruct((senders, PAY, 128), jnp.bfloat16)]
@@ -203,7 +221,7 @@
         return label, count, first, mine
 
     before = jnp.where(part > 0, image_ref[jnp.maximum(window - 1, 0)], -1)
-    _, count, first, _ = lax.fori_loop(0, WIN + 1, scan, (before, jnp.int32(0), jnp.int32(0), jnp.int32(0)), unroll=4)
+    _, count, _, _ = lax.fori_loop(0, WIN + 1, scan, (before, jnp.int32(0), jnp.int32(0), jnp.int32(0)), unroll=4)
 
     chunk = 128
 
@@ -282,13 +300,9 @@
     row_ids = lax.broadcasted_iota(jnp.int32, (ROWS_W, PW), 0)
     live = (row_ids >= start_row) & (row_ids < end_row)
     tile_ids = lax.broadcasted_iota(jnp.int32, (WIN, 8, PW), 0)
-    pooled_ids = lax.broadcasted_iota(jnp.int32, (IMG, PW), 0)
-    lengths = jnp.ones((IMG, PW), jnp.float32)
-    tiles = []
-    for i in range(MAX_LOCAL):
-        tiles.append((tile_ids >= begin_ref[i]) & (tile_ids < end_ref[i]))
-        rows_i = ((end_ref[i] - begin_ref[i]) * TILE).astype(jnp.float32)
-        lengths = jnp.where((pooled_ids == first + i) & (rows_i > 0), rows_i, lengths)
+    term_ids = lax.broadcasted_iota(jnp.int32, (EXTRA, PW), 0)
+    tiles = [(tile_ids >= begin_ref[i]) & (tile_ids < end_ref[i]) for i in range(MAX_LOCAL)]
+    lengths = [jnp.maximum((end_ref[i] - begin_ref[i]) * TILE, 1).astype(jnp.float32) for i in range(MAX_LOCAL)]
     for d, (out, sum_ref) in enumerate(((out0, sum0), (out1, sum1), (out2, sum2), (out3, sum3))):
         n = (part + d) % PARTS
         block_rows = pl.ds(pl.multiple_of(n * PW, PW), PW)
@@ -298,19 +312,17 @@
         out[:ROWS_W, :] = result.astype(jnp.bfloat16)
         pairs = result.reshape(WIN, 2, 8, PW)
         pairs = pairs[:, 0] + pairs[:, 1]
-        sums = jnp.zeros((IMG, PW), jnp.float32)
+        terms = jnp.zeros((EXTRA, PW), jnp.float32)
+        line = jnp.zeros((1, PW), jnp.float32)
         for i in range(MAX_LOCAL):
             held = jnp.sum(jnp.where(tiles[i], pairs, 0.0), axis=0)
-            sums = jnp.where(pooled_ids == first + i, jnp.sum(held, axis=0, keepdims=True), sums)
-        pooled = sums / lengths
-        one = pooled.astype(jnp.bfloat16)
-        rest = pooled - one.astype(jnp.float32)
-        two = rest.astype(jnp.bfloat16)
-        three = (rest - two.astype(jnp.float32)).astype(jnp.bfloat16)
-        out[ROWS_W : ROWS_W + IMG, :] = one
-        out[ROWS_W + IMG : ROWS_W + 2 * IMG, :] = two
-        out[ROWS_W + 2 * IMG : ROWS_W + 3 * IMG, :] = three
-        line = jnp.sum(pooled, axis=0, keepdims=True)
+            rest = jnp.sum(held, axis=0, keepdims=True) / lengths[i]
+            line = line + rest
+            for k in range(3):
+                term = rest.astype(jnp.bfloat16).astype(jnp.float32)
+                terms = jnp.where(term_ids == k * MAX_LOCAL + i, term, terms)
+                rest = rest - term
+        out[ROWS_W:, :] = terms.astype(jnp.bfloat16)
         sum_ref[0:1, :] = line[:, : PW // 2]
         sum_ref[1:2, :] = line[:, PW // 2 :]
 
@@ -344,12 +356,13 @@
     )(part, core, image, *xs, *weights)
 
 
-def finish_kernel(part_ref, r0, r1, r2, r3, out_ref, pooled_ref, out_vmem, sems):
+def finish_kernel(part_ref, image_ref, r0, r1, r2, r3, out_ref, pooled_ref, out_vmem, sems):
     size = PART_SLOTS * TILE
     halo = ROWS_W - size
     received = (r0, r1, r2, r3)
     writes = []
     pooled = jnp.zeros((IMG, PW), jnp.float32)
+    image_ids = lax.broadcasted_iota(jnp.int32, (IMG, PW), 0)
     for d, r in enumerate(received):
         p = (part_ref[0] + PARTS - d) % PARTS
         base = pl.multiple_of(p * size, size)
@@ -360,21 +373,24 @@
         rows = pl.ds(base, size)
         writes.append(pltpu.make_async_copy(out_vmem.at[rows, :], out_ref.at[rows, :], sems.at[d]))
         writes[-1].start()
-        for n in range(3):
-            pooled = pooled + r[ROWS_W + n * IMG : ROWS_W + (n + 1) * IMG, :].astype(jnp.float32)
+        first = jnp.where(p > 0, image_ref[jnp.maximum(p * PART_SLOTS - 1, 0)] + 1, 0)
+        terms = r[ROWS_W:, :].astype(jnp.float32)
+        for i in range(MAX_LOCAL):
+            value = terms[i : i + 1] + terms[MAX_LOCAL + i : MAX_LOCAL + i + 1] + terms[2 * MAX_LOCAL + i : 2 * MAX_LOCAL + i + 1]
+            pooled = pooled + jnp.where(image_ids == first + i, value, 0.0)
     pooled_ref[...] = pooled
     for write in writes:
         write.wait()
 
 
-def finish(part, received):
+def finish(part, image, received):
     return pl.pallas_call(
         finish_kernel,
         grid_spec=pltpu.PrefetchScalarGridSpec(
-            num_scalar_prefetch=1,
+            num_scalar_prefetch=2,
             grid=(1,),
             in_specs=[pl.BlockSpec(memory_space=pltpu.VMEM)] * PARTS,
-            out_specs=[pl.BlockSpec(memory_space=pl.ANY), pl.BlockSpec((IMG, PW), lambda i, a: (0, 0))],
+            out_specs=[pl.BlockSpec(memory_space=pl.ANY), pl.BlockSpec((IMG, PW), lambda i, a, b: (0, 0))],
             scratch_shapes=[
                 pltpu.VMEM((SLOTS * TILE, PW), jnp.bfloat16),
                 pltpu.SemaphoreType.DMA((PARTS,)),
@@ -386,7 +402,7 @@
         ],
         compiler_params=VMEM,
         name="finish",
-    )(part, *received)
+    )(part, image, *received)
 
 
 def pool_kernel(sums_ref, number_ref, pooled_ref, image_ref, out_ref):
@@ -444,7 +460,7 @@
     received = [results[0]] + passed_on(results, shift)
     spread = jnp.broadcast_to(total[None], (senders, 2, PW // 2))
     gathered = lax.all_to_all(spread, "dp", split_axis=0, concat_axis=0, tiled=True)
-    packed_out, pooled = finish(part, [near(r) for r in received])
+    packed_out, pooled = finish(part, packed_image, [near(r) for r in received])
     pooled_out = pool(near(gathered), number, pooled, image)
     return (packed_out, pooled_out)
 

time: 149 us -> 148 us (level)
  no operation moved by 1% of the time
where the time goes in v8:
time: 148 us
  waiting for transfers between devices  68.1 us (46%)
  starting transfers between devices  48.7 us (33%)
  Pallas kernels  29.8 us (20%)
    pallas_call x1, Pallas kernels, block(): pl.pallas_call(block_kernel, grid_spec=pltpu.PrefetchScalarGridSpec(num_s...  20.6 us
    ppermute x3, waiting for transfers between devices, whole_block(): lax.ppermute(sums[d], 'mp', shift(d))  17.3 us
    ppermute x6, waiting for transfers between devices, passed_on(): got.append(lax.ppermute(pieces[d], 'mp', shift(d)))  17.3 us
    all_to_all x1, starting transfers between devices, whole_block(): lax.all_to_all(outgoing, 'dp', split_axis=0, concat_axis=0, tiled=True)  13.5 us
    all_to_all x1, starting transfers between devices, whole_block(): lax.all_to_all(spread, 'dp', split_axis=0, concat_axis=0, tiled=True)  10.2 us
    ppermute x1, waiting for transfers between devices, whole_block(): b0 = lax.ppermute(s0, 'mp', shift(-1))  8.46 us
    ppermute x1, waiting for transfers between devices, whole_block(): c0 = lax.ppermute(a0, 'mp', shift(1))  8.36 us
    ppermute x6, starting transfers between devices, passed_on(): got.append(lax.ppermute(pieces[d], 'mp', shift(d)))  8.1 us
  transfers between devices with their start and end apart: 23, of which 9 were waited for; matrix products, arithmetic and copies ran while one was open for 0% of the time, Pallas kernels for 2%

profile of v8, /device:TPU:1, one launch (start us, length us, event | category | flops | bytes accessed | tf_op | source)
XLA Modules:
  0.0 148.1 jit_solution(4081932500433936117)
XLA Ops:
  0.6 4.6 %send_pack.1 = (bf16[64,72,128]{2,1,0:T(8,128)(2,1)}, bf16[1024,256]{1,0:T(8,128)(2,1)}, bf16[1024,256]{1,0:T(8,128)(2,1)}) custom-call(s32[128]{0:T(128)} %owner_ref.1, s32[128]{0:T(128)} %slot_ref.1, s32[1]{0:T(128)} %bitcast.mp_ref.part_ref, s32[1]{0:T(128)} %bitcast.1.core_ref, s32[1,128]{1,0:T(1,128)} %bitcast.3, bf16[2048,1024]{1,0:T(8,128)(2,1)} %patch_ref.1, ...), custom_call_target="tpu_custom_call" | custom-call | tf_op jit(solution)/shard_map/send_pack/pallas_call | solution.py:104
  5.2 0.0 copy-start.5
  5.2 13.5 %all-to-all-start = ((bf16[64,72,128]{2,1,0:T(8,128)(2,1)}), bf16[64,72,128]{2,1,0:T(8,128)(2,1)S(1)}, u32[]{:S(2)}, u32[]{:S(2)}) async-start(bf16[64,72,128]{2,1,0:T(8,128)(2,1)} %get-tuple-element.20), calls=%async_computation | async-start | bytes 2359296 | tf_op jit(solution)/shard_map/all_to_all | solution.py:454
  18.7 0.0 copy-start
  18.7 2.5 %collective-permute-start.7 = (bf16[1024,256]{1,0:T(8,128)(2,1)}, bf16[1024,256]{1,0:T(8,128)(2,1)S(1)}, u32[]{:S(2)}, u32[]{:S(2)}) collective-permute-start(bf16[1024,256]{1,0:T(8,128)(2,1)} %get-tuple-element.25), channel_id=1, source_target_pairs={{0,3},{1,0},{2,1},{3,2},{4,7},{5,4},{6,5},{7,6},{8,11},{9,8},{10,9... | collective-permute-start | bytes 1572872 | tf_op jit(solution)/shard_map/ppermute | solution.py:448
  21.2 0.0 collective-permute-start.3
  21.2 0.0 copy-done.5
  21.2 2.7 %collective-permute-start.8 = (bf16[1024,256]{1,0:T(8,128)(2,1)S(1)}, bf16[1024,256]{1,0:T(8,128)(2,1)}, u32[]{:S(2)}, u32[]{:S(2)}) collective-permute-start(bf16[1024,256]{1,0:T(8,128)(2,1)S(1)} %copy-done.5), channel_id=1, source_target_pairs={{0,3},{1,0},{2,1},{3,2},{4,7},{5,4},{6,5},{7,6},{8,11},{9,8},{10,9... | collective-permute-start | bytes 1572872 | tf_op jit(solution)/shard_map/ppermute | solution.py:446
  23.9 0.0 collective-permute-start.4
  23.9 8.5 %collective-permute-done.7.b0 = bf16[1024,256]{1,0:T(8,128)(2,1)S(1)} collective-permute-done((bf16[1024,256]{1,0:T(8,128)(2,1)}, bf16[1024,256]{1,0:T(8,128)(2,1)S(1)}, u32[]{:S(2)}, u32[]{:S(2)}) %collective-permute-start.7) | collective-permute-done | bytes 524320 | tf_op jit(solution)/shard_map/ppermute | solution.py:448
  32.4 0.0 copy-start.2
  32.4 2.2 %collective-permute-start.9 = (bf16[1024,256]{1,0:T(8,128)(2,1)S(1)}, bf16[1024,256]{1,0:T(8,128)(2,1)S(1)}, u32[]{:S(2)}, u32[]{:S(2)}) collective-permute-start(bf16[1024,256]{1,0:T(8,128)(2,1)S(1)} %collective-permute-done.7.b0), channel_id=1, source_target_pairs={{0,4},{4,0},{8,12},{12,8},{16,20},{20,16},{24,28},{28,24},{32,36},... | collective-permute-start | bytes 1572872 | tf_op jit(solution)/shard_map/ppermute | solution.py:451
  34.6 0.8 collective-permute-done.3.a0
  35.4 0.0 copy-start.3
  35.4 0.0 collective-permute-start.11
  35.4 8.1 %collective-permute-done.8.b1 = bf16[1024,256]{1,0:T(8,128)(2,1)} collective-permute-done((bf16[1024,256]{1,0:T(8,128)(2,1)S(1)}, bf16[1024,256]{1,0:T(8,128)(2,1)}, u32[]{:S(2)}, u32[]{:S(2)}) %collective-permute-start.8) | collective-permute-done | bytes 524320 | tf_op jit(solution)/shard_map/ppermute | solution.py:446
  43.5 3.5 %collective-permute-start.12 = (bf16[1024,256]{1,0:T(8,128)(2,1)}, bf16[1024,256]{1,0:T(8,128)(2,1)}, u32[]{:S(2)}, u32[]{:S(2)}) collective-permute-start(bf16[1024,256]{1,0:T(8,128)(2,1)} %collective-permute-done.8.b1), channel_id=1, source_target_pairs={{0,3},{1,0},{2,1},{3,2},{4,7},{5,4},{6,5},{7,6},{8,11},{9,8},{10,9... | collective-permute-start | bytes 1572872 | tf_op jit(solution)/shard_map/ppermute | solution.py:450
  47.0 1.6 %collective-permute-start.5 = (bf16[1024,256]{1,0:T(8,128)(2,1)S(1)}, bf16[1024,256]{1,0:T(8,128)(2,1)}, u32[]{:S(2)}, u32[]{:S(2)}) collective-permute-start(bf16[1024,256]{1,0:T(8,128)(2,1)S(1)} %collective-permute-done.3.a0), channel_id=1, source_target_pairs={{0,4},{4,0},{8,12},{12,8},{16,20},{20,16},{24,28},{28,24},{32,36},... | collective-permute-start | bytes 1572872 | tf_op jit(solution)/shard_map/ppermute | solution.py:451
  48.6 0.0 collective-permute-done.4.a1
  48.6 0.9 collective-permute-start.10
  49.5 0.0 collective-permute-done.9.b0x
  49.5 0.0 copy-start.4
  49.5 0.1 collective-permute-start.6
  49.6 8.4 %collective-permute-done.11.c0 = bf16[1024,256]{1,0:T(8,128)(2,1)} collective-permute-done((bf16[1024,256]{1,0:T(8,128)(2,1)S(1)}, bf16[1024,256]{1,0:T(8,128)(2,1)}, u32[]{:S(2)}, u32[]{:S(2)}) %collective-permute-start.11) | collective-permute-done | bytes 524320 | tf_op jit(solution)/shard_map/ppermute | solution.py:449
  58.0 1.6 %collective-permute-start.13 = (bf16[1024,256]{1,0:T(8,128)(2,1)}, bf16[1024,256]{1,0:T(8,128)(2,1)}, u32[]{:S(2)}, u32[]{:S(2)}) collective-permute-start(bf16[1024,256]{1,0:T(8,128)(2,1)} %collective-permute-done.11.c0), channel_id=1, source_target_pairs={{0,4},{4,0},{8,12},{12,8},{16,20},{20,16},{24,28},{28,24},{32,36},... | collective-permute-start | bytes 1572872 | tf_op jit(solution)/shard_map/ppermute | solution.py:451
  59.6 0.0 collective-permute-done.12.c1
  59.6 0.0 collective-permute-start.14
  59.6 0.0 copy-done.4
  59.6 0.0 all-to-all-done.in_ref
  59.6 1.0 arrive_sort.1
  60.6 0.0 copy-start.1
  60.6 0.0 collective-permute-done.5.a0x
  60.6 0.1 collective-permute-start
  60.7 0.0 collective-permute-done.10.b1x
  60.7 4.5 %collective-permute-start.1 = (bf16[752,256]{1,0:T(8,128)(2,1)S(1)}, bf16[752,256]{1,0:T(8,128)(2,1)S(1)}, u32[]{:S(2)}, u32[]{:S(2)}) collective-permute-start(bf16[752,256]{1,0:T(8,128)(2,1)S(1)} %get-tuple-element.23), channel_id=1, source_target_pairs={{0,2},{1,3},{2,0},{3,1},{4,6},{5,7},{6,4},{7,5},{8,10},{9,11},{10,... | collective-permute-start | bytes 1155080 | tf_op jit(solution)/shard_map/ppermute | solution.py:428
  65.2 0.0 collective-permute-done.6.a1x
  65.2 0.0 collective-permute-start.2
  65.2 0.0 collective-permute-done.13.c0x
  65.2 0.0 collective-permute-done.14.c1x
  65.2 8.0 %collective-permute-done.x1 = bf16[752,256]{1,0:T(8,128)(2,1)S(1)} collective-permute-done((bf16[752,256]{1,0:T(8,128)(2,1)S(1)}, bf16[752,256]{1,0:T(8,128)(2,1)S(1)}, u32[]{:S(2)}, u32[]{:S(2)}) %collective-permute-start) | collective-permute-done | bytes 385056 | tf_op jit(solution)/shard_map/ppermute | solution.py:428
  73.2 9.3 %collective-permute-done.1.x2 = bf16[752,256]{1,0:T(8,128)(2,1)S(1)} collective-permute-done((bf16[752,256]{1,0:T(8,128)(2,1)S(1)}, bf16[752,256]{1,0:T(8,128)(2,1)S(1)}, u32[]{:S(2)}, u32[]{:S(2)}) %collective-permute-start.1) | collective-permute-done | bytes 385056 | tf_op jit(solution)/shard_map/ppermute | solution.py:428
  82.5 0.0 collective-permute-done.2.x3
  82.5 0.0 copy-done.2
  82.5 0.0 copy-done.3
  82.5 0.0 copy-done
  82.5 20.6 %block.1 = (bf16[768,256]{1,0:T(8,128)(2,1)S(1)}, bf16[768,256]{1,0:T(8,128)(2,1)S(1)}, bf16[768,256]{1,0:T(8,128)(2,1)S(1)}, bf16[768,256]{1,0:T(8,128)(2,1)S(1...) custom-call(s32[1]{0:T(128)} %bitcast.mp_ref.part_ref, ...), custom_call_target="tpu_custom_call" | custom-call | tf_op jit(solution)/shard_map/block/pallas_call | solution.py:333
  103.1 0.0 copy-done.1
  103.1 0.4 collective-permute-start.15
  103.5 3.1 %collective-permute-start.16 = (bf16[768,256]{1,0:T(8,128)(2,1)S(1)}, bf16[768,256]{1,0:T(8,128)(2,1)S(1)}, u32[]{:S(2)}, u32[]{:S(2)}) collective-permute-start(bf16[768,256]{1,0:T(8,128)(2,1)S(1)} %get-tuple-element.29), channel_id=1, source_target_pairs={{0,2},{1,3},{2,0},{3,1},{4,6},{5,7},{6,4},{7,5},{8,10},{9,11},{10,... | collective-permute-start | bytes 1179656 | tf_op jit(solution)/shard_map/ppermute | solution.py:428
  106.6 0.0 collective-permute-start.17
  106.6 1.5 collective-permute-start.18
  108.1 0.1 collective-permute-start.19
  108.2 15.2 %collective-permute-done.18 = f32[2,128]{1,0:T(2,128)S(1)} collective-permute-done((f32[2,128]{1,0:T(2,128)S(1)}, f32[2,128]{1,0:T(2,128)S(1)}, u32[]{:S(2)}, u32[]{:S(2)}) %collective-permute-start.18) | collective-permute-done | bytes 1056 | tf_op jit(solution)/shard_map/ppermute | solution.py:459
  123.4 0.2 collective-permute-start.20
  123.6 0.0 collective-permute-done.19
  123.6 2.2 %collective-permute-done.20 = f32[2,128]{1,0:T(2,128)S(1)} collective-permute-done((f32[2,128]{1,0:T(2,128)S(1)}, f32[2,128]{1,0:T(2,128)S(1)}, u32[]{:S(2)}, u32[]{:S(2)}) %collective-permute-start.20) | collective-permute-done | bytes 1056 | tf_op jit(solution)/shard_map/ppermute | solution.py:459
  125.8 0.6 broadcast_in_dim.2
  126.4 10.2 %all-to-all-start.1 = ((f32[64,2,128]{2,1,0:T(2,128)}), f32[64,2,128]{2,1,0:T(2,128)S(1)}, u32[]{:S(2)}, u32[]{:S(2)}) async-start(f32[64,2,128]{2,1,0:T(2,128)} %broadcast_in_dim.2), calls=%async_computation.1 | async-start | bytes 131072 | tf_op jit(solution)/shard_map/all_to_all | solution.py:462
  136.6 0.0 collective-permute-done.15.r1
  136.6 0.0 collective-permute-done.16.r2
  136.6 0.0 collective-permute-done.17.r3
  136.6 2.3 %finish.1 = (bf16[2048,256]{1,0:T(8,128)(2,1)}, f32[16,256]{1,0:T(8,128)}) custom-call(s32[1]{0:T(128)} %bitcast.mp_ref.part_ref, s32[128]{0:T(128)} %image_ref.3, bf16[768,256]{1,0:T(8,128)(2,1)S(1)} %get-tuple-element.27.r0, bf16[768,256]{1,0:T(8,128)(2,1)S(1)} %collective-permute-done.15.r1, bf16[768,256]{1,0:T(8,128)(2,1)S(1)} %collective-permute-done.16.r2, ...), custom_call_target="tpu_custom_call" | custom-call | tf_op jit(solution)/shard_map/finish/pallas_call | solution.py:387
  138.9 7.8 %all-to-all-done.1.sums_ref = f32[64,2,128]{2,1,0:T(2,128)S(1)} async-done(((f32[64,2,128]{2,1,0:T(2,128)}), f32[64,2,128]{2,1,0:T(2,128)S(1)}, u32[]{:S(2)}, u32[]{:S(2)}) %all-to-all-start.1) | async-done | bytes 65568 | tf_op jit(solution)/shard_map/all_to_all | solution.py:462
  146.7 1.4 pool.1
  (1 shorter events, 0.0 us)
Async XLA Ops:
  5.2 16.0 %copy-start.5 = (bf16[1024,256]{1,0:T(8,128)(2,1)S(1)}, bf16[1024,256]{1,0:T(8,128)(2,1)}, u32[]{:S(2)}) copy-start(bf16[1024,256]{1,0:T(8,128)(2,1)} %get-tuple-element.26) | copy-start | bytes 1572868
  5.2 54.4 %all-to-all-start = ((bf16[64,72,128]{2,1,0:T(8,128)(2,1)}), bf16[64,72,128]{2,1,0:T(8,128)(2,1)S(1)}, u32[]{:S(2)}, u32[]{:S(2)}) async-start(bf16[64,72,128]{2,1,0:T(8,128)(2,1)} %get-tuple-element.20), calls=%async_computation | async-start | bytes 2359296 | tf_op jit(solution)/shard_map/all_to_all | solution.py:454
  18.7 63.8 %copy-start = (s32[128]{0:T(128)S(1)}, s32[128]{0:T(128)}, u32[]{:S(2)}) copy-start(s32[128]{0:T(128)} %image_ref.3) | copy-start | bytes 1540
  18.7 13.7 %collective-permute-start.7 = (bf16[1024,256]{1,0:T(8,128)(2,1)}, bf16[1024,256]{1,0:T(8,128)(2,1)S(1)}, u32[]{:S(2)}, u32[]{:S(2)}) collective-permute-start(bf16[1024,256]{1,0:T(8,128)(2,1)} %get-tuple-element.25), channel_id=1, source_target_pairs={{0,3},{1,0},{2,1},{3,2},{4,7},{5,4},{6,5},{7,6},{8,11},{9,8},{10,9... | collective-permute-start | bytes 1572872 | tf_op jit(solution)/shard_map/ppermute | solution.py:448
  21.2 14.2 %collective-permute-start.3 = (bf16[1024,256]{1,0:T(8,128)(2,1)}, bf16[1024,256]{1,0:T(8,128)(2,1)S(1)}, u32[]{:S(2)}, u32[]{:S(2)}) collective-permute-start(bf16[1024,256]{1,0:T(8,128)(2,1)} %get-tuple-element.25), channel_id=1, source_target_pairs={{0,1},{1,2},{2,3},{3,0},{4,5},{5,6},{6,7},{7,4},{8,9},{9,10},{10,1... | collective-permute-start | bytes 1572872 | tf_op jit(solution)/shard_map/ppermute | solution.py:445
  21.2 22.3 %collective-permute-start.8 = (bf16[1024,256]{1,0:T(8,128)(2,1)S(1)}, bf16[1024,256]{1,0:T(8,128)(2,1)}, u32[]{:S(2)}, u32[]{:S(2)}) collective-permute-start(bf16[1024,256]{1,0:T(8,128)(2,1)S(1)} %copy-done.5), channel_id=1, source_target_pairs={{0,3},{1,0},{2,1},{3,2},{4,7},{5,4},{6,5},{7,6},{8,11},{9,8},{10,9... | collective-permute-start | bytes 1572872 | tf_op jit(solution)/shard_map/ppermute | solution.py:446
  23.9 24.7 %collective-permute-start.4 = (bf16[1024,256]{1,0:T(8,128)(2,1)S(1)}, bf16[1024,256]{1,0:T(8,128)(2,1)}, u32[]{:S(2)}, u32[]{:S(2)}) collective-permute-start(bf16[1024,256]{1,0:T(8,128)(2,1)S(1)} %copy-done.5), channel_id=1, source_target_pairs={{0,1},{1,2},{2,3},{3,0},{4,5},{5,6},{6,7},{7,4},{8,9},{9,10},{10,1... | collective-permute-start | bytes 1572872 | tf_op jit(solution)/shard_map/ppermute | solution.py:447
  32.4 50.1 %copy-start.2 = (bf16[1024,256]{1,0:T(8,128)(2,1)}, bf16[1024,256]{1,0:T(8,128)(2,1)S(1)}, u32[]{:S(2)}) copy-start(bf16[1024,256]{1,0:T(8,128)(2,1)S(1)} %collective-permute-done.7.b0) | copy-start | bytes 1572868
  32.4 17.1 %collective-permute-start.9 = (bf16[1024,256]{1,0:T(8,128)(2,1)S(1)}, bf16[1024,256]{1,0:T(8,128)(2,1)S(1)}, u32[]{:S(2)}, u32[]{:S(2)}) collective-permute-start(bf16[1024,256]{1,0:T(8,128)(2,1)S(1)} %collective-permute-done.7.b0), channel_id=1, source_target_pairs={{0,4},{4,0},{8,12},{12,8},{16,20},{20,16},{24,28},{28,24},{32,36},... | collective-permute-start | bytes 1572872 | tf_op jit(solution)/shard_map/ppermute | solution.py:451
  35.4 47.1 %copy-start.3 = (bf16[1024,256]{1,0:T(8,128)(2,1)}, bf16[1024,256]{1,0:T(8,128)(2,1)S(1)}, u32[]{:S(2)}) copy-start(bf16[1024,256]{1,0:T(8,128)(2,1)S(1)} %collective-permute-done.3.a0) | copy-start | bytes 1572868
  35.4 22.6 %collective-permute-start.11 = (bf16[1024,256]{1,0:T(8,128)(2,1)S(1)}, bf16[1024,256]{1,0:T(8,128)(2,1)}, u32[]{:S(2)}, u32[]{:S(2)}) collective-permute-start(bf16[1024,256]{1,0:T(8,128)(2,1)S(1)} %collective-permute-done.3.a0), channel_id=1, source_target_pairs={{0,1},{1,2},{2,3},{3,0},{4,5},{5,6},{6,7},{7,4},{8,9},{9,10},{10,1... | collective-permute-start | bytes 1572872 | tf_op jit(solution)/shard_map/ppermute | solution.py:449
  43.5 16.1 %collective-permute-start.12 = (bf16[1024,256]{1,0:T(8,128)(2,1)}, bf16[1024,256]{1,0:T(8,128)(2,1)}, u32[]{:S(2)}, u32[]{:S(2)}) collective-permute-start(bf16[1024,256]{1,0:T(8,128)(2,1)} %collective-permute-done.8.b1), channel_id=1, source_target_pairs={{0,3},{1,0},{2,1},{3,2},{4,7},{5,4},{6,5},{7,6},{8,11},{9,8},{10,9... | collective-permute-start | bytes 1572872 | tf_op jit(solution)/shard_map/ppermute | solution.py:450
  47.0 13.6 %collective-permute-start.5 = (bf16[1024,256]{1,0:T(8,128)(2,1)S(1)}, bf16[1024,256]{1,0:T(8,128)(2,1)}, u32[]{:S(2)}, u32[]{:S(2)}) collective-permute-start(bf16[1024,256]{1,0:T(8,128)(2,1)S(1)} %collective-permute-done.3.a0), channel_id=1, source_target_pairs={{0,4},{4,0},{8,12},{12,8},{16,20},{20,16},{24,28},{28,24},{32,36},... | collective-permute-start | bytes 1572872 | tf_op jit(solution)/shard_map/ppermute | solution.py:451
  48.6 12.1 %collective-permute-start.10 = (bf16[1024,256]{1,0:T(8,128)(2,1)}, bf16[1024,256]{1,0:T(8,128)(2,1)}, u32[]{:S(2)}, u32[]{:S(2)}) collective-permute-start(bf16[1024,256]{1,0:T(8,128)(2,1)} %collective-permute-done.8.b1), channel_id=1, source_target_pairs={{0,4},{4,0},{8,12},{12,8},{16,20},{20,16},{24,28},{28,24},{32,36},... | collective-permute-start | bytes 1572872 | tf_op jit(solution)/shard_map/ppermute | solution.py:451
  49.5 10.1 %copy-start.4 = (bf16[1024,256]{1,0:T(8,128)(2,1)}, bf16[1024,256]{1,0:T(8,128)(2,1)S(1)}, u32[]{:S(2)}) copy-start(bf16[1024,256]{1,0:T(8,128)(2,1)S(1)} %collective-permute-done.9.b0x) | copy-start | bytes 1572868
  49.5 15.7 %collective-permute-start.6 = (bf16[1024,256]{1,0:T(8,128)(2,1)}, bf16[1024,256]{1,0:T(8,128)(2,1)}, u32[]{:S(2)}, u32[]{:S(2)}) collective-permute-start(bf16[1024,256]{1,0:T(8,128)(2,1)} %collective-permute-done.4.a1), channel_id=1, source_target_pairs={{0,4},{4,0},{8,12},{12,8},{16,20},{20,16},{24,28},{28,24},{32,36},... | collective-permute-start | bytes 1572872 | tf_op jit(solution)/shard_map/ppermute | solution.py:451
  58.0 7.2 %collective-permute-start.13 = (bf16[1024,256]{1,0:T(8,128)(2,1)}, bf16[1024,256]{1,0:T(8,128)(2,1)}, u32[]{:S(2)}, u32[]{:S(2)}) collective-permute-start(bf16[1024,256]{1,0:T(8,128)(2,1)} %collective-permute-done.11.c0), channel_id=1, source_target_pairs={{0,4},{4,0},{8,12},{12,8},{16,20},{20,16},{24,28},{28,24},{32,36},... | collective-permute-start | bytes 1572872 | tf_op jit(solution)/shard_map/ppermute | solution.py:451
  59.6 5.7 %collective-permute-start.14 = (bf16[1024,256]{1,0:T(8,128)(2,1)}, bf16[1024,256]{1,0:T(8,128)(2,1)}, u32[]{:S(2)}, u32[]{:S(2)}) collective-permute-start(bf16[1024,256]{1,0:T(8,128)(2,1)} %collective-permute-done.12.c1), channel_id=1, source_target_pairs={{0,4},{4,0},{8,12},{12,8},{16,20},{20,16},{24,28},{28,24},{32,36},... | collective-permute-start | bytes 1572872 | tf_op jit(solution)/shard_map/ppermute | solution.py:451
  60.6 42.4 %copy-start.1 = (f32[8,128]{1,0:T(8,128)}, f32[8,128]{1,0:T(8,128)S(1)}, u32[]{:S(2)}) copy-start(f32[8,128]{1,0:T(8,128)S(1)} %get-tuple-element.36.number_ref) | copy-start | bytes 12292
  60.6 12.5 %collective-permute-start = (bf16[752,256]{1,0:T(8,128)(2,1)S(1)}, bf16[752,256]{1,0:T(8,128)(2,1)S(1)}, u32[]{:S(2)}, u32[]{:S(2)}) collective-permute-start(bf16[752,256]{1,0:T(8,128)(2,1)S(1)} %get-tuple-element.22), channel_id=1, source_target_pairs={{0,1},{1,2},{2,3},{3,0},{4,5},{5,6},{6,7},{7,4},{8,9},{9,10},{10,1... | collective-permute-start | bytes 1155080 | tf_op jit(solution)/shard_map/ppermute | solution.py:428
  60.7 21.7 %collective-permute-start.1 = (bf16[752,256]{1,0:T(8,128)(2,1)S(1)}, bf16[752,256]{1,0:T(8,128)(2,1)S(1)}, u32[]{:S(2)}, u32[]{:S(2)}) collective-permute-start(bf16[752,256]{1,0:T(8,128)(2,1)S(1)} %get-tuple-element.23), channel_id=1, source_target_pairs={{0,2},{1,3},{2,0},{3,1},{4,6},{5,7},{6,4},{7,5},{8,10},{9,11},{10,... | collective-permute-start | bytes 1155080 | tf_op jit(solution)/shard_map/ppermute | solution.py:428
  65.2 17.3 %collective-permute-start.2 = (bf16[752,256]{1,0:T(8,128)(2,1)S(1)}, bf16[752,256]{1,0:T(8,128)(2,1)S(1)}, u32[]{:S(2)}, u32[]{:S(2)}) collective-permute-start(bf16[752,256]{1,0:T(8,128)(2,1)S(1)} %get-tuple-element.24), channel_id=1, source_target_pairs={{0,3},{1,0},{2,1},{3,2},{4,7},{5,4},{6,5},{7,6},{8,11},{9,8},{10,9... | collective-permute-start | bytes 1155080 | tf_op jit(solution)/shard_map/ppermute | solution.py:428
  103.1 33.5 %collective-permute-start.15 = (bf16[768,256]{1,0:T(8,128)(2,1)S(1)}, bf16[768,256]{1,0:T(8,128)(2,1)S(1)}, u32[]{:S(2)}, u32[]{:S(2)}) collective-permute-start(bf16[768,256]{1,0:T(8,128)(2,1)S(1)} %get-tuple-element.28), channel_id=1, source_target_pairs={{0,1},{1,2},{2,3},{3,0},{4,5},{5,6},{6,7},{7,4},{8,9},{9,10},{10,1... | collective-permute-start | bytes 1179656 | tf_op jit(solution)/shard_map/ppermute | solution.py:428
  103.5 33.1 %collective-permute-start.16 = (bf16[768,256]{1,0:T(8,128)(2,1)S(1)}, bf16[768,256]{1,0:T(8,128)(2,1)S(1)}, u32[]{:S(2)}, u32[]{:S(2)}) collective-permute-start(bf16[768,256]{1,0:T(8,128)(2,1)S(1)} %get-tuple-element.29), channel_id=1, source_target_pairs={{0,2},{1,3},{2,0},{3,1},{4,6},{5,7},{6,4},{7,5},{8,10},{9,11},{10,... | collective-permute-start | bytes 1179656 | tf_op jit(solution)/shard_map/ppermute | solution.py:428
  106.6 30.0 %collective-permute-start.17 = (bf16[768,256]{1,0:T(8,128)(2,1)S(1)}, bf16[768,256]{1,0:T(8,128)(2,1)S(1)}, u32[]{:S(2)}, u32[]{:S(2)}) collective-permute-start(bf16[768,256]{1,0:T(8,128)(2,1)S(1)} %get-tuple-element.30), channel_id=1, source_target_pairs={{0,3},{1,0},{2,1},{3,2},{4,7},{5,4},{6,5},{7,6},{8,11},{9,8},{10,9... | collective-permute-start | bytes 1179656 | tf_op jit(solution)/shard_map/ppermute | solution.py:428
  106.6 16.7 %collective-permute-start.18 = (f32[2,128]{1,0:T(2,128)S(1)}, f32[2,128]{1,0:T(2,128)S(1)}, u32[]{:S(2)}, u32[]{:S(2)}) collective-permute-start(f32[2,128]{1,0:T(2,128)S(1)} %get-tuple-element.33), channel_id=1, source_target_pairs={{0,1},{1,2},{2,3},{3,0},{4,5},{5,6},{6,7},{7,4},{8,9},{9,10},{10,1... | collective-permute-start | bytes 3080 | tf_op jit(solution)/shard_map/ppermute | solution.py:459
  108.1 15.5 %collective-permute-start.19 = (f32[2,128]{1,0:T(2,128)S(1)}, f32[2,128]{1,0:T(2,128)S(1)}, u32[]{:S(2)}, u32[]{:S(2)}) collective-permute-start(f32[2,128]{1,0:T(2,128)S(1)} %get-tuple-element.34), channel_id=1, source_target_pairs={{0,2},{1,3},{2,0},{3,1},{4,6},{5,7},{6,4},{7,5},{8,10},{9,11},{10,... | collective-permute-start | bytes 3080 | tf_op jit(solution)/shard_map/ppermute | solution.py:459
  123.4 2.4 %collective-permute-start.20 = (f32[2,128]{1,0:T(2,128)S(1)}, f32[2,128]{1,0:T(2,128)S(1)}, u32[]{:S(2)}, u32[]{:S(2)}) collective-permute-start(f32[2,128]{1,0:T(2,128)S(1)} %get-tuple-element.35), channel_id=1, source_target_pairs={{0,3},{1,0},{2,1},{3,2},{4,7},{5,4},{6,5},{7,6},{8,11},{9,8},{10,9... | collective-permute-start | bytes 3080 | tf_op jit(solution)/shard_map/ppermute | solution.py:459
  126.4 20.3 %all-to-all-start.1 = ((f32[64,2,128]{2,1,0:T(2,128)}), f32[64,2,128]{2,1,0:T(2,128)S(1)}, u32[]{:S(2)}, u32[]{:S(2)}) async-start(f32[64,2,128]{2,1,0:T(2,128)} %broadcast_in_dim.2), calls=%async_computation.1 | async-start | bytes 131072 | tf_op jit(solution)/shard_map/all_to_all | solution.py:462
